TPU v7x, 32 devices: a whole 2x2x4 slice. The times are simulated.
32 devices in a mesh: row: 4 (over y, x), col: 8 (over z, core).
Axes of the slice: x: 2, y: 2, z: 4, core: 2. Of those that a mesh axis runs over, the one named last changes fastest.
Arguments:
- b_diag: float32 [512, 512], P('row'), as said below
- a_diag: float32 [512, 512], P('row'), as said below
- b_panel: float32 [1024, 512], P(('row', 'col')), may hold values from -2 to 2
- a_panel: float32 [1024, 512], P(('row', 'col')), may hold values from -2 to 2
- a_trail: float32 [1024, 1024], P('row', 'col'), as said below
Outputs:
- a_diag_new: float32 [512, 512], P('row')
- l_panel: float32 [1024, 512], P(('row', 'col'))
- a_panel_new: float32 [1024, 512], P(('row', 'col'))
- a_trail_new: float32 [1024, 1024], P('row', 'col')
Inputs may be any that keep to these rules, and one draw needn't show every extreme that they name: b_diag is symmetric positive definite, its smallest eigenvalue 0.5 or more. a_diag is symmetric. a_trail is symmetric.
All inputs are finite; a program needn't handle non-finite values.
Results may differ from a plain program's by a relative error of at most 0.0001.
Values sent between devices are 32-bit elements; how exact they have to be, the bound alone decides.
No kernel may reach another device: no remote copies, remote signals or barrier semaphores. Data moves between devices by JAX's collectives and lax.ppermute only.
A program may use at most 64 MiB of HBM per device.

v0:
```python
import functools

import jax
import jax.numpy as jnp
from jax import lax
from jax.experimental import pallas as pl
from jax.experimental.pallas import tpu as pltpu
from jax.sharding import Mesh
from jax.sharding import PartitionSpec as P


HIGHEST = lax.Precision.HIGHEST
SMALL = 32
BLOCK = 128
TOKEN = jax.ShapeDtypeStruct((8, 128), jnp.float32)
VMEM = pl.BlockSpec(memory_space=pltpu.VMEM)
SMEM = pl.BlockSpec(memory_space=pltpu.SMEM)


def memory(*elements):
    return pltpu.CompilerParams(vmem_limit_bytes=min(2**23 + 12 * sum(elements), 60 * 2**20))


def nt(left, right):
    return lax.dot_general(
        left, right, (((1,), (1,)), ((), ())), precision=HIGHEST, preferred_element_type=jnp.float32
    )


def nn(left, right):
    return lax.dot_general(
        left, right, (((1,), (0,)), ((), ())), precision=HIGHEST, preferred_element_type=jnp.float32
    )


def invert_small(block, offset):
    lanes = block.shape[1]
    groups = SMALL // 8
    cols = []
    for m in range(SMALL):
        column = block[:, offset + m : offset + m + 1]
        cols.append(
            [
                jnp.broadcast_to(column[8 * h : 8 * h + 8], (8, lanes)) if h >= m // 8 else None
                for h in range(groups)
            ]
        )
    sublane = lax.broadcasted_iota(jnp.int32, (8, lanes), 0)
    lane = lax.broadcasted_iota(jnp.int32, (8, lanes), 1)
    rows = [jnp.where(lane == sublane + (offset + 8 * h), 1.0, 0.0).astype(jnp.float32) for h in range(groups)]
    pivots = [None] * groups

    def spread_row(value, s):
        return jnp.broadcast_to(value[s : s + 1, :], (8, lanes))

    for j in range(SMALL):
        g = j // 8
        c = cols[j]
        pivot = spread_row(c[g], j % 8)
        scale = 1.0 / pivot
        pivots[g] = pivot if j % 8 == 0 else jnp.where(sublane == j % 8, pivot, pivots[g])
        row = spread_row(rows[g], j % 8)
        low = [None if c[h] is None else c[h] * scale for h in range(groups)]
        for m in range(j + 1, SMALL):
            t = spread_row(c[m // 8], m % 8)
            for h in range(m // 8, groups):
                if m == j + 1:
                    cols[m][h] = cols[m][h] - (c[h] * t) * scale
                else:
                    cols[m][h] = cols[m][h] - low[h] * t
        for h in range(g, groups):
            factor = jnp.where(sublane > j % 8, low[h], 0.0) if h == g else low[h]
            rows[h] = rows[h] - factor * row
    return jnp.concatenate([rows[h] * lax.rsqrt(pivots[h]) for h in range(groups)], axis=0)


def invert_block(block):
    size = block.shape[0]
    done = []
    total = None
    for b in range(size // SMALL):
        offset = b * SMALL
        below = offset + SMALL
        small = invert_small(block[offset:below, :], offset)
        last = below == size
        if not last:
            low = nt(block[below:, :], small)
            full = jnp.concatenate([jnp.zeros((below, SMALL), jnp.float32), low], axis=0)
            block = jnp.concatenate([block[:below], block[below:, :] - nt(low, full)], axis=0)
        strip = small if total is None else small - nn(small, total)
        done.append(strip)
        if not last:
            update = nn(full, strip)
            total = update if total is None else total + update
    return jnp.concatenate(done, axis=0)


def factor_steps(work, sums, out_ref, base, first, last, count):
    start = first * BLOCK
    for k in range(first, last):
        lo, hi = k * BLOCK, (k + 1) * BLOCK
        here = slice(lo - base, hi - base)
        rows = slice(lo - start, hi - start)
        inverse = invert_block(work[here, here])
        out_ref[rows, lo:hi] = inverse
        if k + 1 < count:
            below = slice(hi - base, count * BLOCK - base)
            low = nt(work[below, here], inverse)
            for i in range(k + 1, count):
                part = slice(i * BLOCK - base, (i + 1) * BLOCK - base)
                wide = slice(hi - base, (i + 1) * BLOCK - base)
                mine = low[i * BLOCK - hi : (i + 1) * BLOCK - hi]
                work[part, wide] = work[part, wide] - nt(mine, low[: (i + 1) * BLOCK - hi])
        if k > 0:
            out_ref[rows, :lo] = -nn(inverse, sums[here, :lo])
        if k + 1 < count:
            update = nn(low, out_ref[rows, :hi])
            if k > 0:
                sums[below, :lo] = sums[below, :lo] + update[:, :lo]
            sums[below, lo:hi] = update[:, lo:hi]
        if hi < out_ref.shape[1]:
            out_ref[rows, hi:] = jnp.zeros((BLOCK, out_ref.shape[1] - hi), jnp.float32)


def first_kernel(shifts, last, row_ref, *refs):
    pieces, (top_out, work_out, sums_out, token_out, work, sums) = refs[:shifts], refs[shifts:]
    height, size = pieces[0].shape
    me = row_ref[0]
    for s in range(shifts):
        source = lax.rem(me - s + shifts, shifts)
        work[pl.ds(pl.multiple_of(source * height, 8), height), :] = pieces[s][...]
    factor_steps(work, sums, top_out, 0, 0, last, size // BLOCK)
    work_out[...] = work[last * BLOCK :, last * BLOCK :]
    sums_out[...] = sums[last * BLOCK :, : last * BLOCK]
    token_out[...] = jnp.zeros_like(token_out)


def second_kernel(first, token_in, work_in, sums_in, bottom_out, work, sums):
    size = bottom_out.shape[1]
    work[...] = work_in[...]
    sums[:, : first * BLOCK] = sums_in[...]
    factor_steps(work, sums, bottom_out, first * BLOCK, first, size // BLOCK, size // BLOCK)


def first_half(row, pieces):
    size = pieces[0].shape[1]
    last = size // BLOCK // 2
    cut = last * BLOCK
    rest = size - cut
    return pl.pallas_call(
        functools.partial(first_kernel, len(pieces), last),
        out_shape=(
            jax.ShapeDtypeStruct((cut, cut), jnp.float32),
            jax.ShapeDtypeStruct((rest, rest), jnp.float32),
            jax.ShapeDtypeStruct((rest, cut), jnp.float32),
            TOKEN,
        ),
        in_specs=[SMEM] + [VMEM] * len(pieces),
        out_specs=(VMEM,) * 4,
        scratch_shapes=[pltpu.VMEM((size, size), jnp.float32)] * 2,
        cost_estimate=pl.CostEstimate(flops=50 * size**3, bytes_accessed=8 * size * size, transcendentals=0),
        compiler_params=memory(4 * size * size),
        name="first_half",
    )(row, *pieces)


def second_half(token, work, sums):
    rest, cut = sums.shape
    size = rest + cut
    return pl.pallas_call(
        functools.partial(second_kernel, cut // BLOCK),
        out_shape=jax.ShapeDtypeStruct((rest, size), jnp.float32),
        in_specs=[VMEM] * 3,
        out_specs=VMEM,
        scratch_shapes=[pltpu.VMEM((rest, rest), jnp.float32), pltpu.VMEM((rest, size), jnp.float32)],
        cost_estimate=pl.CostEstimate(flops=50 * size**3, bytes_accessed=8 * size * size, transcendentals=0),
        compiler_params=memory(4 * size * size),
        name="second_half",
    )(token, work, sums)


def pack_kernel(place_ref, diag_ref, b_ref, a_ref, plane_out, panel_out):
    core = place_ref[1]
    rows = b_ref.shape[0]
    half = plane_out.shape[0] - 2 * rows
    plane_out[:half] = diag_ref[pl.ds(pl.multiple_of(core * half, 8), half), :]
    plane_out[half : half + rows] = b_ref[...]
    plane_out[half + rows :] = a_ref[...]
    panel_out[:rows] = b_ref[...]
    panel_out[rows:] = a_ref[...]


def pack(places, a_diag, b_panel, a_panel, cores):
    rows, size = b_panel.shape
    half = a_diag.shape[0] // cores
    return pl.pallas_call(
        pack_kernel,
        out_shape=(
            jax.ShapeDtypeStruct((half + 2 * rows, size), jnp.float32),
            jax.ShapeDtypeStruct((2 * rows, size), jnp.float32),
        ),
        in_specs=[SMEM] + [VMEM] * 3,
        out_specs=(VMEM,) * 2,
        compiler_params=memory(4 * a_diag.size + 4 * b_panel.size),
        name="pack",
    )(places, a_diag, b_panel, a_panel)


def route_kernel(count, chips, place_ref, *refs):
    planes, panels, refs = refs[:count], refs[count : count + chips], refs[count + chips + 1 :]
    diag_out, rows_out, sends, token_out, held = refs[0], refs[1], refs[2:-2], refs[-2], refs[-1]
    token_out[...] = jnp.zeros_like(token_out)
    row, chip, slot = place_ref[0], place_ref[2], place_ref[3]
    half = diag_out.shape[1]
    for s in range(count):
        source = lax.rem(row - s + count, count)
        diag_out[source] = planes[s][:half]
        held[source] = planes[s][half:]
    for s in range(chips):
        rows_out[lax.rem(chip - s + chips, chips)] = panels[s][...]
    for s in range(chips):
        sends[s][...] = held[lax.rem(slot + s, chips)]


def route(token, places, planes, panels):
    count, chips = len(planes), len(panels)
    both, size = panels[0].shape
    half = planes[0].shape[0] - both
    shape = jax.ShapeDtypeStruct
    outs = [shape((count, half, size), jnp.float32), shape((chips, both, size), jnp.float32)]
    outs += [shape((both, size), jnp.float32)] * chips + [TOKEN]
    found = pl.pallas_call(
        functools.partial(route_kernel, count, chips),
        out_shape=tuple(outs),
        in_specs=[SMEM] + [VMEM] * (count + chips + 1),
        out_specs=(VMEM,) * len(outs),
        scratch_shapes=[pltpu.VMEM((count, both, size), jnp.float32)],
        compiler_params=memory(2 * count * planes[0].size + 3 * chips * both * size),
        name="route",
    )(places, *planes, *panels, token)
    return found[0], found[1], list(found[2:-1]), found[-1]


def split(value):
    high = value.astype(jnp.bfloat16)
    return high, (value - high.astype(jnp.float32)).astype(jnp.bfloat16)


def product(left, right, dims):
    def dot(x, y):
        return lax.dot_general(x, y, (dims, ((), ())), preferred_element_type=jnp.float32)

    return dot(left[0], right[0]) + (dot(left[0], right[1]) + dot(left[1], right[0]))


NT = ((1,), (1,))
NN = ((1,), (0,))


def update_kernel(place_ref, *refs):
    top_ref, bottom_ref, diag_ref, diag_other, rows_ref, rows_other, trail_ref = refs[:7]
    chips = rows_ref.shape[0]
    pieces = refs[7 : 7 + chips]
    diag_out, low_out, panel_out, trail_out, inverse_work, diag_work, rows_work, cols_work = refs[7 + chips :]
    row, core, chip, place = place_ref[0], place_ref[1], place_ref[2], place_ref[4]
    count, half, size = diag_ref.shape
    cores = 2
    rows = rows_ref.shape[1] // 2
    height = cores * half
    cut = top_ref.shape[0]
    for r in range(count):
        diag_work[pl.ds(pl.multiple_of(r * height + core * half, 8), half), :] = diag_ref[r]
        diag_work[pl.ds(pl.multiple_of(r * height + (1 - core) * half, 8), half), :] = diag_other[r]
    for z in range(chips):
        mine = pl.ds(pl.multiple_of((z * cores + core) * rows, 8), rows)
        theirs = pl.ds(pl.multiple_of((z * cores + 1 - core) * rows, 8), rows)
        spot = pl.ds(pl.multiple_of(lax.rem(chip - z + chips, chips) * rows, 8), rows)
        for which in range(2):
            part = slice(which * rows, (which + 1) * rows)
            rows_work[which, mine, :] = rows_ref[z, part]
            rows_work[which, theirs, :] = rows_other[z, part]
            cols_work[which, spot, :] = pieces[z][part]
    inverse_work[:cut, :cut] = top_ref[...]
    inverse_work[:cut, cut:] = jnp.zeros((cut, size - cut), jnp.float32)
    inverse_work[cut:, :] = bottom_ref[...]

    inverse = split(inverse_work[...])
    left = split(product(inverse, split(diag_work[...]), NN))
    reduced = product(left, inverse, NT)
    diag_work[...] = reduced
    diag_out[...] = diag_work[pl.ds(pl.multiple_of(row * height, 8), height), :]
    reduced = split(reduced)

    def panel(work):
        low = product(split(work[0]), inverse, NT)
        correction = 0.5 * product(split(low), reduced, NN)
        mixed = product(split(work[1]), inverse, NT) - correction
        return low, mixed, correction

    low_rows, mixed_rows, correction = panel(rows_work)
    rows_work[0] = low_rows
    rows_work[1] = mixed_rows - correction
    mine = pl.ds(pl.multiple_of(place * rows, 8), rows)
    low_out[...] = rows_work[0, mine, :]
    panel_out[...] = rows_work[1, mine, :]
    low_cols, mixed_cols, _ = panel(cols_work)
    trail_out[...] = trail_ref[...] - (
        product(split(mixed_rows), split(low_cols), NT) + product(split(low_rows), split(mixed_cols), NT)
    )


def update(places, top, bottom, diag, diag_other, own, other, a_trail, pieces, shapes):
    size = bottom.shape[1]
    height, width = a_trail.shape
    return pl.pallas_call(
        update_kernel,
        out_shape=tuple(jax.ShapeDtypeStruct(shape, jnp.float32) for shape in shapes),
        in_specs=[SMEM] + [VMEM] * (7 + len(pieces)),
        out_specs=(VMEM,) * 4,
        scratch_shapes=[
            pltpu.VMEM((size, size), jnp.float32),
            pltpu.VMEM((size, size), jnp.float32),
            pltpu.VMEM((2, height, size), jnp.float32),
            pltpu.VMEM((2, width, size), jnp.float32),
        ],
        cost_estimate=pl.CostEstimate(flops=10 * size**3, bytes_accessed=8 * size * size, transcendentals=0),
        compiler_params=memory(3 * size * size + 4 * height * size + 4 * width * size + 2 * height * width),
        name="update",
    )(places, top, bottom, diag, diag_other, own, other, a_trail, *pieces)


def body(b_diag, a_diag, b_panel, a_panel, a_trail):
    count, chips, cores = (lax.axis_size(name) for name in ("row", "chip", "core"))
    row, chip, core = (lax.axis_index(name) for name in ("row", "chip", "core"))
    rows, _ = b_panel.shape
    height, width = a_trail.shape
    assert chips == count and height == chips * cores * rows and width * cores == height
    span = chips // cores
    slot = lax.rem(chip, span) * cores + core

    def shift(array, axis, s):
        n = lax.axis_size(axis)
        return lax.ppermute(array, axis, [(i, (i + s) % n) for i in range(n)])

    def swap(array):
        return lax.ppermute(array, "core", [(0, 1), (1, 0)])

    places = jnp.stack([row, core, chip, slot, chip * cores + core]).astype(jnp.int32)
    b_pieces = [b_diag] + [shift(b_diag, "row", s) for s in range(1, count)]
    plane, panel = pack(places, a_diag, b_panel, a_panel, cores)
    panels = [panel] + [shift(panel, "chip", s) for s in range(1, chips)]
    planes = [plane] + [shift(plane, "row", s) for s in range(1, count)]
    top, work, sums, token = first_half(places, b_pieces)
    diag, own, sends, token = route(token, places, planes, panels)
    pieces = []
    for s in range(chips):
        pairs = []
        for r in range(count):
            for z in range(chips):
                for c in range(cores):
                    target = ((z % span) * cores + c + s) % chips
                    pairs.append(((r * chips + z) * cores + c, (r * chips + target) * cores + z // span))
        pieces.append(lax.ppermute(sends[s], ("row", "chip", "core"), pairs))
    diag_other, other = swap(diag), swap(own)
    bottom = second_half(token, work, sums)
    shapes = (a_diag.shape, b_panel.shape, a_panel.shape, a_trail.shape)
    return update(places, top, bottom, diag, diag_other, own, other, a_trail, pieces, shapes)


def solution(mesh):
    count, cols = mesh.devices.shape
    cores = 2
    fine = Mesh(mesh.devices.reshape(count, cols // cores, cores), ("row", "chip", "core"))
    in_specs = (
        P("row", None),
        P("row", None),
        P(("row", "chip", "core"), None),
        P(("row", "chip", "core"), None),
        P("row", ("chip", "core")),
    )
    out_specs = (
        P("row", None),
        P(("row", "chip", "core"), None),
        P(("row", "chip", "core"), None),
        P("row", ("chip", "core")),
    )
    return jax.shard_map(body, mesh=fine, in_specs=in_specs, out_specs=out_specs, check_vma=False)
```

profile of v0, /device:TPU:0, one launch (start us, length us, event | category | flops | bytes accessed | tf_op | source)
XLA Modules:
  0.0 61.5 jit_solution(13977906470984242350)
XLA Ops:
  0.6 3.1 %collective-permute-start.1 = (f32[128,512]{1,0:T(8,128)}, f32[128,512]{1,0:T(8,128)S(1)}, u32[]{:S(2)}, u32[]{:S(2)}) collective-permute-start(f32[128,512]{1,0:T(8,128)} %refs_0_.1), channel_id=1, source_target_pairs={{0,16},{8,24},{16,0},{24,8},{1,17},{9,25},{17,1},{25,9},{2,18},{10... | collective-permute-start | bytes 786440 | tf_op jit(solution)/shard_map/ppermute | solution.py:343
  3.7 1.5 %collective-permute-start = (f32[128,512]{1,0:T(8,128)}, f32[128,512]{1,0:T(8,128)S(1)}, u32[]{:S(2)}, u32[]{:S(2)}) collective-permute-start(f32[128,512]{1,0:T(8,128)} %refs_0_.1), channel_id=1, source_target_pairs={{0,8},{8,16},{16,24},{24,0},{1,9},{9,17},{17,25},{25,1},{2,10},{10... | collective-permute-start | bytes 786440 | tf_op jit(solution)/shard_map/ppermute | solution.py:343
  5.2 1.4 %collective-permute-start.2 = (f32[128,512]{1,0:T(8,128)}, f32[128,512]{1,0:T(8,128)S(1)}, u32[]{:S(2)}, u32[]{:S(2)}) collective-permute-start(f32[128,512]{1,0:T(8,128)} %refs_0_.1), channel_id=1, source_target_pairs={{0,24},{8,0},{16,8},{24,16},{1,25},{9,1},{17,9},{25,17},{2,26},{10... | collective-permute-start | bytes 786440 | tf_op jit(solution)/shard_map/ppermute | solution.py:343
  6.6 0.1 stack.23.row_ref.place_ref
  6.7 0.0 copy-start
  6.7 0.9 %copy-done = f32[128,512]{1,0:T(8,128)S(1)} copy-done((f32[128,512]{1,0:T(8,128)S(1)}, f32[128,512]{1,0:T(8,128)}, u32[]{:S(2)}) %copy-start) | copy-done | bytes 262168
  7.7 0.0 copy-start.1
  7.7 0.8 %copy-done.1 = f32[32,512]{1,0:T(8,128)S(1)} copy-done((f32[32,512]{1,0:T(8,128)S(1)}, f32[32,512]{1,0:T(8,128)}, u32[]{:S(2)}) %copy-start.1) | copy-done | bytes 65560
  8.5 0.0 copy-start.2
  8.5 0.8 %copy-done.2 = f32[32,512]{1,0:T(8,128)S(1)} copy-done((f32[32,512]{1,0:T(8,128)S(1)}, f32[32,512]{1,0:T(8,128)}, u32[]{:S(2)}) %copy-start.2) | copy-done | bytes 65560
  9.3 0.0 copy-start.3
  9.3 0.6 pack.1
  9.9 3.7 %collective-permute-start.8 = (f32[64,512]{1,0:T(8,128)S(1)}, f32[64,512]{1,0:T(8,128)S(1)}, u32[]{:S(2)}, u32[]{:S(2)}) collective-permute-start(f32[64,512]{1,0:T(8,128)S(1)} %get-tuple-element.19.refs_4_), channel_id=1, source_target_pairs={{0,6},{2,0},{4,2},{6,4},{1,7},{3,1},{5,3},{7,5},{8,14},{10,8},{12,... | collective-permute-start | bytes 393224 | tf_op jit(solution)/shard_map/ppermute | solution.py:343
  13.6 0.0 collective-permute-start.7
  13.6 3.9 %collective-permute-done.8.refs_7_ = f32[64,512]{1,0:T(8,128)S(1)} collective-permute-done((f32[64,512]{1,0:T(8,128)S(1)}, f32[64,512]{1,0:T(8,128)S(1)}, u32[]{:S(2)}, u32[]{:S(2)}) %collective-permute-start.8) | collective-permute-done | bytes 131104 | tf_op jit(solution)/shard_map/ppermute | solution.py:343
  17.5 4.1 %collective-permute-start.6 = (f32[64,512]{1,0:T(8,128)S(1)}, f32[64,512]{1,0:T(8,128)S(1)}, u32[]{:S(2)}, u32[]{:S(2)}) collective-permute-start(f32[64,512]{1,0:T(8,128)S(1)} %get-tuple-element.19.refs_4_), channel_id=1, source_target_pairs={{0,2},{2,4},{4,6},{6,0},{1,3},{3,5},{5,7},{7,1},{8,10},{10,12},{12... | collective-permute-start | bytes 393224 | tf_op jit(solution)/shard_map/ppermute | solution.py:343
  21.6 0.0 collective-permute-done.1.refs_2_
  21.6 0.5 collective-permute-start.5
  22.1 0.0 collective-permute-done.refs_1_
  22.1 1.5 %collective-permute-start.4 = (f32[128,512]{1,0:T(8,128)S(1)}, f32[128,512]{1,0:T(8,128)S(1)}, u32[]{:S(2)}, u32[]{:S(2)}) collective-permute-start(f32[128,512]{1,0:T(8,128)S(1)} %get-tuple-element.18.refs_0_), channel_id=1, source_target_pairs={{0,16},{8,24},{16,0},{24,8},{1,17},{9,25},{17,1},{25,9},{2,18},{10... | collective-permute-start | bytes 786440 | tf_op jit(solution)/shard_map/ppermute | solution.py:343
  23.6 0.0 collective-permute-done.2.refs_3_
  23.6 0.5 collective-permute-start.3
  24.1 0.0 copy-done.3
  24.1 10.5 %first_half.1 = (f32[256,256]{1,0:T(8,128)S(1)}, f32[256,256]{1,0:T(8,128)S(1)}, f32[256,256]{1,0:T(8,128)S(1)}, f32[8,128]{1,0:T(8,128)S(1)}) custom-call(s32[5]{0:T(128)S(1)} %stack.23.row_ref.place_ref, f32[128,512]{1,0:T(8,128)S(1)} %copy-done.3, f32[128,512]{1,0:T(8,128)S(1)} %collective-permute-done.refs_1_, ...), custom_call_target="tpu_custom_call" | custom-call | flops 6710886400 | bytes 2097152 | tf_op jit(solution)/shard_map/first_half/pallas_call | solution.py:150
  34.6 0.0 collective-permute-done.7.refs_6_
  34.6 0.0 collective-permute-done.6.refs_5_
  34.6 0.0 collective-permute-done.5.refs_3_
  34.6 0.0 collective-permute-done.4.refs_2_
  34.7 0.0 collective-permute-done.3.refs_1_
  34.7 0.7 %route.1 = (f32[4,64,512]{2,1,0:T(8,128)S(1)}, f32[4,64,512]{2,1,0:T(8,128)S(1)}, f32[64,512]{1,0:T(8,128)S(1)}, f32[64,512]{1,0:T(8,128)S(1)}, f32[64,512]{1,0:...) custom-call(s32[5]{0:T(128)S(1)} %stack.23.row_ref.place_ref, f32[128,512]{1,0:T(8,128)S(1)} %get-tuple-element.18.refs_0_, ...), custom_call_target="tpu_custom_call" | custom-call | tf_op jit(solution)/shard_map/route/pallas_call | solution.py:232
  35.4 0.7 %collective-permute-start.11 = (f32[64,512]{1,0:T(8,128)S(1)}, f32[64,512]{1,0:T(8,128)S(1)}, u32[]{:S(2)}, u32[]{:S(2)}) collective-permute-start(f32[64,512]{1,0:T(8,128)S(1)} %get-tuple-element.26), channel_id=1, source_target_pairs={{0,0},{1,2},{2,4},{3,6},{4,1},{5,3},{6,5},{7,7},{8,8},{9,10},{10,1... | collective-permute-start | bytes 393224 | tf_op jit(solution)/shard_map/ppermute | solution.py:363
  36.0 4.5 %collective-permute-start.12 = (f32[64,512]{1,0:T(8,128)S(1)}, f32[64,512]{1,0:T(8,128)S(1)}, u32[]{:S(2)}, u32[]{:S(2)}) collective-permute-start(f32[64,512]{1,0:T(8,128)S(1)} %get-tuple-element.27), channel_id=1, source_target_pairs={{0,2},{1,4},{2,6},{3,0},{4,3},{5,5},{6,7},{7,1},{8,10},{9,12},{10,... | collective-permute-start | bytes 393224 | tf_op jit(solution)/shard_map/ppermute | solution.py:363
  40.6 0.7 %collective-permute-start.13 = (f32[64,512]{1,0:T(8,128)S(1)}, f32[64,512]{1,0:T(8,128)S(1)}, u32[]{:S(2)}, u32[]{:S(2)}) collective-permute-start(f32[64,512]{1,0:T(8,128)S(1)} %get-tuple-element.28), channel_id=1, source_target_pairs={{0,4},{1,6},{2,0},{3,2},{4,5},{5,7},{6,1},{7,3},{8,12},{9,14},{10,... | collective-permute-start | bytes 393224 | tf_op jit(solution)/shard_map/ppermute | solution.py:363
  41.3 4.4 %collective-permute-start.14 = (f32[64,512]{1,0:T(8,128)S(1)}, f32[64,512]{1,0:T(8,128)S(1)}, u32[]{:S(2)}, u32[]{:S(2)}) collective-permute-start(f32[64,512]{1,0:T(8,128)S(1)} %get-tuple-element.29), channel_id=1, source_target_pairs={{0,6},{1,0},{2,2},{3,4},{4,7},{5,1},{6,3},{7,5},{8,14},{9,8},{10,1... | collective-permute-start | bytes 393224 | tf_op jit(solution)/shard_map/ppermute | solution.py:363
  45.7 0.1 collective-permute-start.9
  45.8 0.0 collective-permute-done.11.refs_7_
  45.8 0.5 collective-permute-start.10
  46.3 0.0 copy-start.4
  46.3 8.8 %second_half.1.refs_1_ = f32[256,512]{1,0:T(8,128)S(1)} custom-call(f32[8,128]{1,0:T(8,128)S(1)} %get-tuple-element.21.token_in, f32[256,256]{1,0:T(8,128)S(1)} %get-tuple-element.22.work_in, f32[256,256]{1,0:T(8,128)S(1)} %get-tuple-element.23.sums_in), custom_call_target="tpu_custom_call" | custom-call | flops 6710886400 | bytes 2097152 | tf_op jit(solution)/shard_map/second_half/pallas_call | solution.py:170
  55.1 0.0 collective-permute-done.12.refs_8_
  55.1 0.0 collective-permute-done.13.refs_9_
  55.1 0.0 collective-permute-done.14.refs_10_
  55.2 0.0 collective-permute-done.9.refs_3_
  55.2 0.0 collective-permute-done.10.refs_5_
  55.2 0.0 copy-done.4
  55.2 6.3 %update.1 = (f32[128,512]{1,0:T(8,128)}, f32[32,512]{1,0:T(8,128)}, f32[32,512]{1,0:T(8,128)}, f32[256,128]{1,0:T(8,128)}) custom-call(s32[5]{0:T(128)S(1)} %stack.23.row_ref.place_ref, f32[256,256]{1,0:T(8,128)S(1)} %get-tuple-element.17.refs_0_, f32[256,512]{1,0:T(8,128)S(1)} %second_half.1.refs_1_, f32[4,64,512]{2,1,0:T(8,128)S(1)} %get-tuple-element.24.refs_2_, ...), custom_call_target="tpu_custom_call" | custom-call | flops 1342177280 | bytes 2097152 | tf_op jit(solution)/shard_map/update/pallas_call | solution.py:315
Async XLA Ops:
  0.6 20.9 %collective-permute-start.1 = (f32[128,512]{1,0:T(8,128)}, f32[128,512]{1,0:T(8,128)S(1)}, u32[]{:S(2)}, u32[]{:S(2)}) collective-permute-start(f32[128,512]{1,0:T(8,128)} %refs_0_.1), channel_id=1, source_target_pairs={{0,16},{8,24},{16,0},{24,8},{1,17},{9,25},{17,1},{25,9},{2,18},{10... | collective-permute-start | bytes 786440 | tf_op jit(solution)/shard_map/ppermute | solution.py:343
  3.7 18.4 %collective-permute-start = (f32[128,512]{1,0:T(8,128)}, f32[128,512]{1,0:T(8,128)S(1)}, u32[]{:S(2)}, u32[]{:S(2)}) collective-permute-start(f32[128,512]{1,0:T(8,128)} %refs_0_.1), channel_id=1, source_target_pairs={{0,8},{8,16},{16,24},{24,0},{1,9},{9,17},{17,25},{25,1},{2,10},{10... | collective-permute-start | bytes 786440 | tf_op jit(solution)/shard_map/ppermute | solution.py:343
  5.2 18.5 %collective-permute-start.2 = (f32[128,512]{1,0:T(8,128)}, f32[128,512]{1,0:T(8,128)S(1)}, u32[]{:S(2)}, u32[]{:S(2)}) collective-permute-start(f32[128,512]{1,0:T(8,128)} %refs_0_.1), channel_id=1, source_target_pairs={{0,24},{8,0},{16,8},{24,16},{1,25},{9,1},{17,9},{25,17},{2,26},{10... | collective-permute-start | bytes 786440 | tf_op jit(solution)/shard_map/ppermute | solution.py:343
  6.7 1.0 %copy-start = (f32[128,512]{1,0:T(8,128)S(1)}, f32[128,512]{1,0:T(8,128)}, u32[]{:S(2)}) copy-start(f32[128,512]{1,0:T(8,128)} %diag_ref.1) | copy-start | bytes 786436
  7.7 0.8 %copy-start.1 = (f32[32,512]{1,0:T(8,128)S(1)}, f32[32,512]{1,0:T(8,128)}, u32[]{:S(2)}) copy-start(f32[32,512]{1,0:T(8,128)} %b_ref.1) | copy-start | bytes 196612
  8.5 0.8 %copy-start.2 = (f32[32,512]{1,0:T(8,128)S(1)}, f32[32,512]{1,0:T(8,128)}, u32[]{:S(2)}) copy-start(f32[32,512]{1,0:T(8,128)} %a_ref.1) | copy-start | bytes 196612
  9.3 14.8 %copy-start.3 = (f32[128,512]{1,0:T(8,128)S(1)}, f32[128,512]{1,0:T(8,128)}, u32[]{:S(2)}) copy-start(f32[128,512]{1,0:T(8,128)} %refs_0_.1) | copy-start | bytes 786436
  9.9 7.5 %collective-permute-start.8 = (f32[64,512]{1,0:T(8,128)S(1)}, f32[64,512]{1,0:T(8,128)S(1)}, u32[]{:S(2)}, u32[]{:S(2)}) collective-permute-start(f32[64,512]{1,0:T(8,128)S(1)} %get-tuple-element.19.refs_4_), channel_id=1, source_target_pairs={{0,6},{2,0},{4,2},{6,4},{1,7},{3,1},{5,3},{7,5},{8,14},{10,8},{12,... | collective-permute-start | bytes 393224 | tf_op jit(solution)/shard_map/ppermute | solution.py:343
  13.6 21.1 %collective-permute-start.7 = (f32[64,512]{1,0:T(8,128)S(1)}, f32[64,512]{1,0:T(8,128)S(1)}, u32[]{:S(2)}, u32[]{:S(2)}) collective-permute-start(f32[64,512]{1,0:T(8,128)S(1)} %get-tuple-element.19.refs_4_), channel_id=1, source_target_pairs={{0,4},{2,6},{4,0},{6,2},{1,5},{3,7},{5,1},{7,3},{8,12},{10,14},{12... | collective-permute-start | bytes 393224 | tf_op jit(solution)/shard_map/ppermute | solution.py:343
  17.5 17.2 %collective-permute-start.6 = (f32[64,512]{1,0:T(8,128)S(1)}, f32[64,512]{1,0:T(8,128)S(1)}, u32[]{:S(2)}, u32[]{:S(2)}) collective-permute-start(f32[64,512]{1,0:T(8,128)S(1)} %get-tuple-element.19.refs_4_), channel_id=1, source_target_pairs={{0,2},{2,4},{4,6},{6,0},{1,3},{3,5},{5,7},{7,1},{8,10},{10,12},{12... | collective-permute-start | bytes 393224 | tf_op jit(solution)/shard_map/ppermute | solution.py:343
  21.6 13.1 %collective-permute-start.5 = (f32[128,512]{1,0:T(8,128)S(1)}, f32[128,512]{1,0:T(8,128)S(1)}, u32[]{:S(2)}, u32[]{:S(2)}) collective-permute-start(f32[128,512]{1,0:T(8,128)S(1)} %get-tuple-element.18.refs_0_), channel_id=1, source_target_pairs={{0,24},{8,0},{16,8},{24,16},{1,25},{9,1},{17,9},{25,17},{2,26},{10... | collective-permute-start | bytes 786440 | tf_op jit(solution)/shard_map/ppermute | solution.py:343
  22.1 12.5 %collective-permute-start.4 = (f32[128,512]{1,0:T(8,128)S(1)}, f32[128,512]{1,0:T(8,128)S(1)}, u32[]{:S(2)}, u32[]{:S(2)}) collective-permute-start(f32[128,512]{1,0:T(8,128)S(1)} %get-tuple-element.18.refs_0_), channel_id=1, source_target_pairs={{0,16},{8,24},{16,0},{24,8},{1,17},{9,25},{17,1},{25,9},{2,18},{10... | collective-permute-start | bytes 786440 | tf_op jit(solution)/shard_map/ppermute | solution.py:343
  23.6 11.0 %collective-permute-start.3 = (f32[128,512]{1,0:T(8,128)S(1)}, f32[128,512]{1,0:T(8,128)S(1)}, u32[]{:S(2)}, u32[]{:S(2)}) collective-permute-start(f32[128,512]{1,0:T(8,128)S(1)} %get-tuple-element.18.refs_0_), channel_id=1, source_target_pairs={{0,8},{8,16},{16,24},{24,0},{1,9},{9,17},{17,25},{25,1},{2,10},{10... | collective-permute-start | bytes 786440 | tf_op jit(solution)/shard_map/ppermute | solution.py:343
  35.4 10.4 %collective-permute-start.11 = (f32[64,512]{1,0:T(8,128)S(1)}, f32[64,512]{1,0:T(8,128)S(1)}, u32[]{:S(2)}, u32[]{:S(2)}) collective-permute-start(f32[64,512]{1,0:T(8,128)S(1)} %get-tuple-element.26), channel_id=1, source_target_pairs={{0,0},{1,2},{2,4},{3,6},{4,1},{5,3},{6,5},{7,7},{8,8},{9,10},{10,1... | collective-permute-start | bytes 393224 | tf_op jit(solution)/shard_map/ppermute | solution.py:363
  36.0 19.1 %collective-permute-start.12 = (f32[64,512]{1,0:T(8,128)S(1)}, f32[64,512]{1,0:T(8,128)S(1)}, u32[]{:S(2)}, u32[]{:S(2)}) collective-permute-start(f32[64,512]{1,0:T(8,128)S(1)} %get-tuple-element.27), channel_id=1, source_target_pairs={{0,2},{1,4},{2,6},{3,0},{4,3},{5,5},{6,7},{7,1},{8,10},{9,12},{10,... | collective-permute-start | bytes 393224 | tf_op jit(solution)/shard_map/ppermute | solution.py:363
  40.6 14.6 %collective-permute-start.13 = (f32[64,512]{1,0:T(8,128)S(1)}, f32[64,512]{1,0:T(8,128)S(1)}, u32[]{:S(2)}, u32[]{:S(2)}) collective-permute-start(f32[64,512]{1,0:T(8,128)S(1)} %get-tuple-element.28), channel_id=1, source_target_pairs={{0,4},{1,6},{2,0},{3,2},{4,5},{5,7},{6,1},{7,3},{8,12},{9,14},{10,... | collective-permute-start | bytes 393224 | tf_op jit(solution)/shard_map/ppermute | solution.py:363
  41.3 13.9 %collective-permute-start.14 = (f32[64,512]{1,0:T(8,128)S(1)}, f32[64,512]{1,0:T(8,128)S(1)}, u32[]{:S(2)}, u32[]{:S(2)}) collective-permute-start(f32[64,512]{1,0:T(8,128)S(1)} %get-tuple-element.29), channel_id=1, source_target_pairs={{0,6},{1,0},{2,2},{3,4},{4,7},{5,1},{6,3},{7,5},{8,14},{9,8},{10,1... | collective-permute-start | bytes 393224 | tf_op jit(solution)/shard_map/ppermute | solution.py:363
  45.7 9.4 %collective-permute-start.9 = (f32[4,64,512]{2,1,0:T(8,128)S(1)}, f32[4,64,512]{2,1,0:T(8,128)S(1)}, u32[]{:S(2)}, u32[]{:S(2)}) collective-permute-start(f32[4,64,512]{2,1,0:T(8,128)S(1)} %get-tuple-element.24.refs_2_), channel_id=1, source_target_pairs={{0,1},{1,0},{2,3},{3,2},{4,5},{5,4},{6,7},{7,6},{8,9},{9,8},{10,11... | collective-permute-start | bytes 1572872 | tf_op jit(solution)/shard_map/ppermute | solution.py:346
  45.8 9.4 %collective-permute-start.10 = (f32[4,64,512]{2,1,0:T(8,128)S(1)}, f32[4,64,512]{2,1,0:T(8,128)S(1)}, u32[]{:S(2)}, u32[]{:S(2)}) collective-permute-start(f32[4,64,512]{2,1,0:T(8,128)S(1)} %get-tuple-element.25.refs_4_), channel_id=1, source_target_pairs={{0,1},{1,0},{2,3},{3,2},{4,5},{5,4},{6,7},{7,6},{8,9},{9,8},{10,11... | collective-permute-start | bytes 1572872 | tf_op jit(solution)/shard_map/ppermute | solution.py:346
  46.3 8.9 %copy-start.4 = (f32[256,128]{1,0:T(8,128)S(1)}, f32[256,128]{1,0:T(8,128)}, u32[]{:S(2)}) copy-start(f32[256,128]{1,0:T(8,128)} %refs_6_.1) | copy-start | bytes 393220
where the time goes:
time: 61.8 us; the launch traced here: 61.5 us
  starting transfers between devices  27.2 us (44%)
  Pallas kernels  26.9 us (44%)
  waiting for transfers between devices  3.92 us (6%)
  local copies, waits for them, and re-layouts  2.72 us (4%)
  between operations  0.8 us (1%)
    ppermute x9, starting transfers between devices, shift(): return lax.ppermute(array, axis, [(i, (i + s) % n) for i in range(n)])  16.3 us
    pallas_call x1, Pallas kernels, first_half(): pl.pallas_call(functools.partial(first_kernel, len(pieces), last), out_sh...  10.5 us
    ppermute x4, starting transfers between devices, body(): pieces.append(lax.ppermute(sends[s], ('row', 'chip', 'core'), pairs))  10.3 us
    pallas_call x1, Pallas kernels, second_half(): pl.pallas_call(functools.partial(second_kernel, cut // BLOCK), out_shape=...  8.82 us
    pallas_call x1, Pallas kernels, update(): pl.pallas_call(update_kernel, out_shape=tuple((jax.ShapeDtypeStruct(shape...  6.33 us
    ppermute x9, waiting for transfers between devices, shift(): return lax.ppermute(array, axis, [(i, (i + s) % n) for i in range(n)])  3.91 us
    unnamed x10, local copies, waits for them, and re-layouts  2.64 us
  transfers between devices with their start and end apart: 15, of which 1 were waited for; matrix products, arithmetic and copies ran while one was open for 0% of the time, Pallas kernels for 32%

commit v1 on v0

v1 whole, which is shorter than its diff:
```python
import functools

import jax
import jax.numpy as jnp
from jax import lax
from jax.experimental import pallas as pl
from jax.experimental.pallas import tpu as pltpu
from jax.sharding import Mesh
from jax.sharding import PartitionSpec as P


HIGHEST = lax.Precision.HIGHEST
SMALL = 32
BLOCK = 128
TOKEN = jax.ShapeDtypeStruct((8, 128), jnp.float32)
VMEM = pl.BlockSpec(memory_space=pltpu.VMEM)
SMEM = pl.BlockSpec(memory_space=pltpu.SMEM)


def memory(*elements):
    return pltpu.CompilerParams(vmem_limit_bytes=min(2**23 + 12 * sum(elements), 60 * 2**20))


def nt(left, right):
    return lax.dot_general(
        left, right, (((1,), (1,)), ((), ())), precision=HIGHEST, preferred_element_type=jnp.float32
    )


def nn(left, right):
    return lax.dot_general(
        left, right, (((1,), (0,)), ((), ())), precision=HIGHEST, preferred_element_type=jnp.float32
    )


def invert_small(block, offset):
    lanes = block.shape[1]
    groups = SMALL // 8
    cols = []
    for m in range(SMALL):
        column = block[:, offset + m : offset + m + 1]
        cols.append(
            [
                jnp.broadcast_to(column[8 * h : 8 * h + 8], (8, lanes)) if h >= m // 8 else None
                for h in range(groups)
            ]
        )
    sublane = lax.broadcasted_iota(jnp.int32, (8, lanes), 0)
    lane = lax.broadcasted_iota(jnp.int32, (8, lanes), 1)
    rows = [jnp.where(lane == sublane + (offset + 8 * h), 1.0, 0.0).astype(jnp.float32) for h in range(groups)]
    pivots = [None] * groups

    def spread_row(value, s):
        return jnp.broadcast_to(value[s : s + 1, :], (8, lanes))

    for j in range(SMALL):
        g = j // 8
        c = cols[j]
        pivot = spread_row(c[g], j % 8)
        scale = 1.0 / pivot
        pivots[g] = pivot if j % 8 == 0 else jnp.where(sublane == j % 8, pivot, pivots[g])
        row = spread_row(rows[g], j % 8)
        low = [None if c[h] is None else c[h] * scale for h in range(groups)]
        for m in range(j + 1, SMALL):
            t = spread_row(c[m // 8], m % 8)
            for h in range(m // 8, groups):
                if m == j + 1:
                    cols[m][h] = cols[m][h] - (c[h] * t) * scale
                else:
                    cols[m][h] = cols[m][h] - low[h] * t
        for h in range(g, groups):
            factor = jnp.where(sublane > j % 8, low[h], 0.0) if h == g else low[h]
            rows[h] = rows[h] - factor * row
    return jnp.concatenate([rows[h] * lax.rsqrt(pivots[h]) for h in range(groups)], axis=0)


def invert_block(block):
    size = block.shape[0]
    done = []
    total = None
    for b in range(size // SMALL):
        offset = b * SMALL
        below = offset + SMALL
        small = invert_small(block[offset:below, :], offset)
        last = below == size
        if not last:
            low = nt(block[below:, :], small)
            full = jnp.concatenate([jnp.zeros((below, SMALL), jnp.float32), low], axis=0)
            block = jnp.concatenate([block[:below], block[below:, :] - nt(low, full)], axis=0)
        strip = small if total is None else small - nn(small, total)
        done.append(strip)
        if not last:
            update = nn(full, strip)
            total = update if total is None else total + update
    return jnp.concatenate(done, axis=0)


def factor_steps(work, sums, out_ref, base, first, last, count):
    start = first * BLOCK
    for k in range(first, last):
        lo, hi = k * BLOCK, (k + 1) * BLOCK
        here = slice(lo - base, hi - base)
        rows = slice(lo - start, hi - start)
        inverse = invert_block(work[here, here])
        out_ref[rows, lo:hi] = inverse
        if k + 1 < count:
            below = slice(hi - base, count * BLOCK - base)
            low = nt(work[below, here], inverse)
            for i in range(k + 1, count):
                part = slice(i * BLOCK - base, (i + 1) * BLOCK - base)
                wide = slice(hi - base, (i + 1) * BLOCK - base)
                mine = low[i * BLOCK - hi : (i + 1) * BLOCK - hi]
                work[part, wide] = work[part, wide] - nt(mine, low[: (i + 1) * BLOCK - hi])
        if k > 0:
            out_ref[rows, :lo] = -nn(inverse, sums[here, :lo])
        if k + 1 < count:
            update = nn(low, out_ref[rows, :hi])
            if k > 0:
                sums[below, :lo] = sums[below, :lo] + update[:, :lo]
            sums[below, lo:hi] = update[:, lo:hi]
        if hi < out_ref.shape[1]:
            out_ref[rows, hi:] = jnp.zeros((BLOCK, out_ref.shape[1] - hi), jnp.float32)


def gather_square(work, core, me, count, own, ops, swapped, last, last_swapped, holder):
    height = own.shape[0]

    def place(source, piece):
        work[pl.ds(pl.multiple_of(source * height, 8), height), :] = piece[...]

    place(me, own)
    for j in range(len(ops)):
        place(me ^ (2 * j + 1 + core), ops[j])
        place(me ^ (2 * j + 2 - core), swapped[j])

    @pl.when(core == holder)
    def _():
        place(me ^ (count - 1), last)

    @pl.when(core != holder)
    def _():
        place(me ^ (count - 1), last_swapped)


def step_kernel(count, first, last, place_ref, *refs):
    if first == 0:
        own, final, final_swapped = refs[:3]
        extra = count // 2 - 1
        ops, swapped = refs[3 : 3 + extra], refs[3 + extra : 3 + 2 * extra]
        refs = refs[3 + 2 * extra :]
    else:
        _, work_in, sums_in = refs[:3]
        refs = refs[3:]
    inverse_out, work, sums = refs[0], refs[-2], refs[-1]
    total, size = inverse_out.shape[1] // BLOCK, work.shape[0]
    if first == 0:
        gather_square(work, place_ref[1], place_ref[0], count, own, ops, swapped, final, final_swapped, 0)
        total = size // BLOCK
    else:
        work[...] = work_in[...]
        sums[:, : first * BLOCK] = sums_in[...]
        total = first + size // BLOCK
    factor_steps(work, sums, inverse_out, first * BLOCK, first, last, total)
    if last < total:
        work_out, sums_out, token_out = refs[1:4]
        cut = (last - first) * BLOCK
        work_out[...] = work[cut:, cut:]
        sums_out[...] = sums[cut:, : last * BLOCK]
        token_out[...] = jnp.zeros_like(token_out)


def factor_part(places, operands, count, first, last, total):
    shape = jax.ShapeDtypeStruct
    size = (total - first) * BLOCK
    rest = (total - last) * BLOCK
    made = last * BLOCK
    outs = [shape(((last - first) * BLOCK, made), jnp.float32)]
    if rest:
        outs += [shape((rest, rest), jnp.float32), shape((rest, made), jnp.float32), TOKEN]
    return pl.pallas_call(
        functools.partial(step_kernel, count, first, last),
        out_shape=tuple(outs),
        in_specs=[SMEM] + [VMEM] * len(operands),
        out_specs=(VMEM,) * len(outs),
        scratch_shapes=[pltpu.VMEM((size, size), jnp.float32), pltpu.VMEM((size, total * BLOCK), jnp.float32)],
        cost_estimate=pl.CostEstimate(flops=10**10, bytes_accessed=8 * size * size, transcendentals=0),
        compiler_params=memory(4 * size * size),
    )(places, *operands)


def pack_kernel(place_ref, b_diag, a_diag, b_panel, a_panel, last_out, panel_out, sems):
    rows = b_panel.shape[0]
    upper = pltpu.make_async_copy(b_panel, panel_out.at[pl.ds(0, rows)], sems.at[0])
    lower = pltpu.make_async_copy(a_panel, panel_out.at[pl.ds(rows, rows)], sems.at[1])
    upper.start()
    lower.start()

    @pl.when(place_ref[1] == 0)
    def _():
        copy = pltpu.make_async_copy(b_diag, last_out, sems.at[2])
        copy.start()
        copy.wait()

    @pl.when(place_ref[1] != 0)
    def _():
        copy = pltpu.make_async_copy(a_diag, last_out, sems.at[3])
        copy.start()
        copy.wait()

    upper.wait()
    lower.wait()


def pack(places, b_diag, a_diag, b_panel, a_panel):
    rows, size = b_panel.shape
    return pl.pallas_call(
        pack_kernel,
        out_shape=(
            jax.ShapeDtypeStruct(b_diag.shape, jnp.float32),
            jax.ShapeDtypeStruct((2 * rows, size), jnp.float32),
        ),
        in_specs=[SMEM] + [pl.BlockSpec(memory_space=pltpu.HBM)] * 4,
        out_specs=(VMEM,) * 2,
        scratch_shapes=[pltpu.SemaphoreType.DMA((4,))],
        compiler_params=memory(4 * a_diag.size + 4 * b_panel.size),
        name="pack",
    )(places, b_diag, a_diag, b_panel, a_panel)


def join_kernel(place_ref, own, other, out):
    both = own.shape[0]
    core = place_ref[1]
    out[pl.ds(pl.multiple_of(core * both, 8), both), :] = own[...]
    out[pl.ds(pl.multiple_of((1 - core) * both, 8), both), :] = other[...]


def join(places, own, other):
    both, size = own.shape
    return pl.pallas_call(
        join_kernel,
        out_shape=jax.ShapeDtypeStruct((2 * both, size), jnp.float32),
        in_specs=[SMEM] + [VMEM] * 2,
        out_specs=VMEM,
        compiler_params=memory(4 * own.size),
        name="join",
    )(places, own, other)


def route_kernel(count, chips, place_ref, _, own, last, last_swapped, *refs):
    extra = count // 2 - 1
    ops, swapped = refs[:extra], refs[extra : 2 * extra]
    sends, token_out, held = refs[2 * extra : -2], refs[-2], refs[-1]
    row, core, slot = place_ref[0], place_ref[1], place_ref[3]
    token_out[...] = jnp.zeros_like(token_out)
    held[row] = own[...]
    for j in range(extra):
        held[row ^ (2 * j + 1 + core)] = ops[j][...]
        held[row ^ (2 * j + 2 - core)] = swapped[j][...]

    @pl.when(core == 0)
    def _():
        held[row ^ (count - 1)] = last[...]

    @pl.when(core != 0)
    def _():
        held[row ^ (count - 1)] = last_swapped[...]

    for t in range(len(sends)):
        sends[t][...] = held[lax.rem(slot + 2 * t, chips)]


def route(places, token, own, last, last_swapped, ops, swapped, count, chips):
    shape = jax.ShapeDtypeStruct
    outs = [shape(own.shape, jnp.float32)] * (chips // 2) + [TOKEN]
    found = pl.pallas_call(
        functools.partial(route_kernel, count, chips),
        out_shape=tuple(outs),
        in_specs=[SMEM] + [VMEM] * (4 + len(ops) + len(swapped)),
        out_specs=(VMEM,) * len(outs),
        scratch_shapes=[pltpu.VMEM((count,) + own.shape, jnp.float32)],
        compiler_params=memory(2 * (count + chips) * own.size),
        name="route",
    )(places, token, own, last, last_swapped, *ops, *swapped)
    return list(found[:-1]), found[-1]


def split(value):
    high = value.astype(jnp.bfloat16)
    return high, (value - high.astype(jnp.float32)).astype(jnp.bfloat16)


def product(left, right, dims):
    def dot(x, y):
        return lax.dot_general(x, y, (dims, ((), ())), preferred_element_type=jnp.float32)

    return dot(left[0], right[0]) + (dot(left[0], right[1]) + dot(left[1], right[0]))


NT = ((1,), (1,))
NN = ((1,), (0,))


def update_kernel(count, chips, parts, place_ref, *refs):
    inverses, refs = refs[:parts], refs[parts:]
    (diag, square, square_swapped, panel, final, final_swapped, trail_ref), refs = refs[:7], refs[7:]
    extra, more, pairs = count // 2 - 1, chips // 2 - 1, chips // 2
    groups = []
    for n in (extra, extra, more, more, pairs):
        groups.append(refs[:n])
        refs = refs[n:]
    diag_ops, diag_swapped, row_ops, row_swapped, pieces = groups
    diag_out, low_out, panel_out, trail_out, inverse_work, diag_work, rows_work, cols_work = refs
    row, core, chip, place = place_ref[0], place_ref[1], place_ref[2], place_ref[4]
    height, size = diag.shape
    rows = panel.shape[0] // 4
    gather_square(diag_work, core, row, count, diag, diag_ops, diag_swapped, square, square_swapped, 1)

    def store(work, spot, piece):
        for c in range(2):
            for which in range(2):
                part = slice((2 * c + which) * rows, (2 * c + which + 1) * rows)
                work[which, pl.ds(pl.multiple_of((2 * spot + c) * rows, 8), rows), :] = piece[part]

    store(rows_work, chip, panel)
    for j in range(more):
        store(rows_work, chip ^ (2 * j + 1 + core), row_ops[j])
        store(rows_work, chip ^ (2 * j + 2 - core), row_swapped[j])

    @pl.when(core == 1)
    def _():
        store(rows_work, chip ^ (chips - 1), final)

    @pl.when(core != 1)
    def _():
        store(rows_work, chip ^ (chips - 1), final_swapped)

    for t in range(pairs):
        store(cols_work, lax.rem(chip - 2 * t + chips, chips) // 2, pieces[t])
    at = 0
    for part in inverses:
        tall, wide = part.shape
        inverse_work[at : at + tall, :wide] = part[...]
        if wide < size:
            inverse_work[at : at + tall, wide:] = jnp.zeros((tall, size - wide), jnp.float32)
        at += tall

    inverse = split(inverse_work[...])
    left = split(product(inverse, split(diag_work[...]), NN))
    reduced = product(left, inverse, NT)
    diag_work[...] = reduced
    diag_out[...] = diag_work[pl.ds(pl.multiple_of(row * height, 8), height), :]
    reduced = split(reduced)

    def panel(work):
        low = product(split(work[0]), inverse, NT)
        correction = 0.5 * product(split(low), reduced, NN)
        mixed = product(split(work[1]), inverse, NT) - correction
        return low, mixed, correction

    low_rows, mixed_rows, correction = panel(rows_work)
    rows_work[0] = low_rows
    rows_work[1] = mixed_rows - correction
    mine = pl.ds(pl.multiple_of(place * rows, 8), rows)
    low_out[...] = rows_work[0, mine, :]
    panel_out[...] = rows_work[1, mine, :]
    low_cols, mixed_cols, _ = panel(cols_work)
    trail_out[...] = trail_ref[...] - (
        product(split(mixed_rows), split(low_cols), NT) + product(split(low_rows), split(mixed_cols), NT)
    )


def update(places, inverses, singles, groups, count, chips, shapes):
    size = inverses[-1].shape[1]
    height, width = shapes[-1]
    operands = list(inverses) + list(singles) + [piece for group in groups for piece in group]
    return pl.pallas_call(
        functools.partial(update_kernel, count, chips, len(inverses)),
        out_shape=tuple(jax.ShapeDtypeStruct(shape, jnp.float32) for shape in shapes),
        in_specs=[SMEM] + [VMEM] * len(operands),
        out_specs=(VMEM,) * 4,
        scratch_shapes=[
            pltpu.VMEM((size, size), jnp.float32),
            pltpu.VMEM((size, size), jnp.float32),
            pltpu.VMEM((2, height, size), jnp.float32),
            pltpu.VMEM((2, width, size), jnp.float32),
        ],
        cost_estimate=pl.CostEstimate(flops=10**10, bytes_accessed=8 * size * size, transcendentals=0),
        compiler_params=memory(3 * size * size + 4 * height * size + 4 * width * size + 2 * height * width),
        name="update",
    )(places, *operands)


def body(b_diag, a_diag, b_panel, a_panel, a_trail):
    count, chips, cores = (lax.axis_size(name) for name in ("row", "chip", "core"))
    row, chip, core = (lax.axis_index(name) for name in ("row", "chip", "core"))
    rows, size = b_panel.shape
    height, width = a_trail.shape
    assert cores == 2 and chips == count and height == chips * cores * rows and width * cores == height
    assert count & (count - 1) == 0
    span = chips // cores

    def exchange(array, target):
        pairs = []
        for r in range(count):
            for z in range(chips):
                for c in range(cores):
                    to = target(r, z, c)
                    pairs.append(((r * chips + z) * cores + c, (to[0] * chips + to[1]) * cores + to[2]))
        return lax.ppermute(array, ("row", "chip", "core"), pairs)

    def to_rows(array, j):
        return exchange(array, lambda r, z, c: (r ^ (2 * j + 1 + c), z, c))

    def to_chips(array, j):
        return exchange(array, lambda r, z, c: (r, z ^ (2 * j + 1 + c), c))

    def swap(array):
        return exchange(array, lambda r, z, c: (r, z, 1 - c))

    slot = lax.rem(chip, span) * 2 + core
    places = jnp.stack([row, core, chip, slot, chip * 2 + core]).astype(jnp.int32)
    extra, more = range(count // 2 - 1), range(chips // 2 - 1)
    b_ops = [to_rows(b_diag, j) for j in extra]
    mixed, own = pack(places, b_diag, a_diag, b_panel, a_panel)
    other = swap(own)
    square = exchange(mixed, lambda r, z, c: (r ^ (count - 1), z, c))
    panel = join(places, own, other)
    p_ops = [to_rows(panel, j) for j in extra]
    final = exchange(panel, lambda r, z, c: (r, z ^ (chips - 1), c) if c else (r ^ (count - 1), z, c))
    z_ops = [to_chips(panel, j) for j in more]
    a_ops = [to_rows(a_diag, j) for j in extra]
    b_swapped = [swap(x) for x in b_ops]
    square_swapped = swap(square)
    total = size // BLOCK
    cuts = (0, total // 4, total // 2, total)
    top, work, sums, token = factor_part(
        places, [b_diag, square, square_swapped, *b_ops, *b_swapped], count, cuts[0], cuts[1], total
    )
    p_swapped = [swap(x) for x in p_ops]
    final_swapped = swap(final)
    middle, work, sums, token = factor_part(places, [token, work, sums], count, cuts[1], cuts[2], total)
    sends, token = route(places, token, panel, final, final_swapped, p_ops, p_swapped, count, chips)
    pieces = [
        exchange(
            sends[t], lambda r, z, c: (r, ((z % span) * 2 + c + 2 * t) % chips, z // span)
        )
        for t in range(span)
    ]
    z_swapped = [swap(x) for x in z_ops]
    a_swapped = [swap(x) for x in a_ops]
    (bottom,) = factor_part(places, [token, work, sums], count, cuts[2], cuts[3], total)
    shapes = (a_diag.shape, b_panel.shape, a_panel.shape, a_trail.shape)
    singles = (a_diag, square, square_swapped, panel, final, final_swapped, a_trail)
    groups = (a_ops, a_swapped, z_ops, z_swapped, pieces)
    return update(places, (top, middle, bottom), singles, groups, count, chips, shapes)


def solution(mesh):
    count, cols = mesh.devices.shape
    cores = 2
    fine = Mesh(mesh.devices.reshape(count, cols // cores, cores), ("row", "chip", "core"))
    in_specs = (
        P("row", None),
        P("row", None),
        P(("row", "chip", "core"), None),
        P(("row", "chip", "core"), None),
        P("row", ("chip", "core")),
    )
    out_specs = (
        P("row", None),
        P(("row", "chip", "core"), None),
        P(("row", "chip", "core"), None),
        P("row", ("chip", "core")),
    )
    return jax.shard_map(body, mesh=fine, in_specs=in_specs, out_specs=out_specs, check_vma=False)
```

time: 61.8 us -> 62.7 us (1.015)
  the two profiles are of different devices: /device:TPU:0 before, /device:TPU:1 now
where the time goes in v1:
time: 62.7 us; the launch traced here: 62.4 us
  Pallas kernels  29 us (46%)
  starting transfers between devices  20.5 us (33%)
  waiting for transfers between devices  8.47 us (14%)
  local copies, waits for them, and re-layouts  3.67 us (6%)
  between operations  0.75 us (1%)
    pallas_call x3, Pallas kernels, factor_part(): pl.pallas_call(functools.partial(step_kernel, count, first, last), out_sh...  20.6 us
    ppermute x15, starting transfers between devices, exchange(): return lax.ppermute(array, ('row', 'chip', 'core'), pairs)  20.5 us
    ppermute x15, waiting for transfers between devices, exchange(): return lax.ppermute(array, ('row', 'chip', 'core'), pairs)  8.47 us
    pallas_call x1, Pallas kernels, update(): pl.pallas_call(functools.partial(update_kernel, count, chips, len(inverse...  6.39 us
    unnamed x14, local copies, waits for them, and re-layouts  3.59 us
  transfers between devices with their start and end apart: 15, of which 6 were waited for; matrix products, arithmetic and copies ran while one was open for 0% of the time, Pallas kernels for 35%

profile of v1, /device:TPU:1, one launch (start us, length us, event | category | flops | bytes accessed | tf_op | source)
XLA Modules:
  0.0 62.4 jit_solution(10806322639056800741)
XLA Ops:
  0.6 0.1 stack.23.place_ref
  0.7 0.0 copy-start
  0.7 0.9 %copy-done = f32[128,512]{1,0:T(8,128)S(1)} copy-done((f32[128,512]{1,0:T(8,128)S(1)}, f32[128,512]{1,0:T(8,128)}, u32[]{:S(2)}) %copy-start) | copy-done | bytes 262168
  1.7 0.0 copy-start.2
  1.7 0.9 %copy-done.2 = f32[128,512]{1,0:T(8,128)S(1)} copy-done((f32[128,512]{1,0:T(8,128)S(1)}, f32[128,512]{1,0:T(8,128)}, u32[]{:S(2)}) %copy-start.2) | copy-done | bytes 262168
  2.6 0.0 copy-start.4
  2.6 0.8 %copy-done.4 = f32[32,512]{1,0:T(8,128)S(1)} copy-done((f32[32,512]{1,0:T(8,128)S(1)}, f32[32,512]{1,0:T(8,128)}, u32[]{:S(2)}) %copy-start.4) | copy-done | bytes 65560
  3.5 0.0 copy-start.5
  3.5 0.8 %copy-done.5 = f32[32,512]{1,0:T(8,128)S(1)} copy-done((f32[32,512]{1,0:T(8,128)S(1)}, f32[32,512]{1,0:T(8,128)}, u32[]{:S(2)}) %copy-start.5) | copy-done | bytes 65560
  4.3 0.8 %pack.1 = (f32[128,512]{1,0:T(8,128)S(1)}, f32[64,512]{1,0:T(8,128)S(1)}) custom-call(s32[5]{0:T(128)S(1)} %stack.23.place_ref, f32[128,512]{1,0:T(8,128)S(1)} %copy-done, f32[128,512]{1,0:T(8,128)S(1)} %copy-done.2, f32[32,512]{1,0:T(8,128)S(1)} %copy-done.4, f32[32,512]{1,0:T(8,128)S(1)} %copy-done.5), custom_call_target="tpu_custom_call" | custom-call | tf_op jit(solution)/shard_map/pack/pallas_call | solution.py:216
  5.1 3.0 %collective-permute-start = (f32[128,512]{1,0:T(8,128)S(1)}, f32[128,512]{1,0:T(8,128)S(1)}, u32[]{:S(2)}, u32[]{:S(2)}) collective-permute-start(f32[128,512]{1,0:T(8,128)S(1)} %get-tuple-element.17), channel_id=1, source_target_pairs={{0,24},{1,25},{2,26},{3,27},{4,28},{5,29},{6,30},{7,31},{8,16},{9,... | collective-permute-start | bytes 786440 | tf_op jit(solution)/shard_map/ppermute | solution.py:409
  8.1 0.2 collective-permute-start.2
  8.4 1.2 %collective-permute-start.9 = (f32[128,512]{1,0:T(8,128)S(1)}, f32[128,512]{1,0:T(8,128)S(1)}, u32[]{:S(2)}, u32[]{:S(2)}) collective-permute-start(f32[128,512]{1,0:T(8,128)S(1)} %copy-done.2), channel_id=1, source_target_pairs={{0,8},{1,17},{2,10},{3,19},{4,12},{5,21},{6,14},{7,23},{8,0},{9,25... | collective-permute-start | bytes 786440 | tf_op jit(solution)/shard_map/ppermute | solution.py:409
  9.6 0.0 copy-start.1
  9.6 1.5 %collective-permute-start.4 = (f32[64,512]{1,0:T(8,128)S(1)}, f32[64,512]{1,0:T(8,128)S(1)}, u32[]{:S(2)}, u32[]{:S(2)}) collective-permute-start(f32[64,512]{1,0:T(8,128)S(1)} %get-tuple-element.24.own), channel_id=1, source_target_pairs={{0,1},{1,0},{2,3},{3,2},{4,5},{5,4},{6,7},{7,6},{8,9},{9,8},{10,11... | collective-permute-start | bytes 393224 | tf_op jit(solution)/shard_map/ppermute | solution.py:409
  11.1 1.0 %collective-permute-done.4.other = f32[64,512]{1,0:T(8,128)S(1)} collective-permute-done((f32[64,512]{1,0:T(8,128)S(1)}, f32[64,512]{1,0:T(8,128)S(1)}, u32[]{:S(2)}, u32[]{:S(2)}) %collective-permute-start.4) | collective-permute-done | bytes 131104 | tf_op jit(solution)/shard_map/ppermute | solution.py:409
  12.1 0.6 join.1.own.refs_6_
  12.7 3.4 %collective-permute-start.5 = (f32[128,512]{1,0:T(8,128)S(1)}, f32[128,512]{1,0:T(8,128)S(1)}, u32[]{:S(2)}, u32[]{:S(2)}) collective-permute-start(f32[128,512]{1,0:T(8,128)S(1)} %join.1.own.refs_6_), channel_id=1, source_target_pairs={{0,24},{1,7},{2,26},{3,5},{4,28},{5,3},{6,30},{7,1},{8,16},{9,15},... | collective-permute-start | bytes 786440 | tf_op jit(solution)/shard_map/ppermute | solution.py:409
  16.1 0.2 collective-permute-start.7
  16.3 0.0 collective-permute-done.refs_1_.refs_4_
  16.3 0.1 collective-permute-start.11
  16.4 1.4 %collective-permute-done.2.refs_3_ = f32[128,512]{1,0:T(8,128)S(1)} collective-permute-done((f32[128,512]{1,0:T(8,128)S(1)}, f32[128,512]{1,0:T(8,128)S(1)}, u32[]{:S(2)}, u32[]{:S(2)}) %collective-permute-start.2) | collective-permute-done | bytes 262176 | tf_op jit(solution)/shard_map/ppermute | solution.py:409
  17.8 0.7 %collective-permute-start.1 = (f32[128,512]{1,0:T(8,128)S(1)}, f32[128,512]{1,0:T(8,128)S(1)}, u32[]{:S(2)}, u32[]{:S(2)}) collective-permute-start(f32[128,512]{1,0:T(8,128)S(1)} %collective-permute-done.refs_1_.refs_4_), channel_id=1, source_target_pairs={{0,1},{1,0},{2,3},{3,2},{4,5},{5,4},{6,7},{7,6},{8,9},{9,8},{10,11... | collective-permute-start | bytes 786440 | tf_op jit(solution)/shard_map/ppermute | solution.py:409
  18.5 2.1 %collective-permute-done.9.refs_10_ = f32[128,512]{1,0:T(8,128)S(1)} collective-permute-done((f32[128,512]{1,0:T(8,128)S(1)}, f32[128,512]{1,0:T(8,128)S(1)}, u32[]{:S(2)}, u32[]{:S(2)}) %collective-permute-start.9) | collective-permute-done | bytes 262176 | tf_op jit(solution)/shard_map/ppermute | solution.py:409
  20.6 0.7 %collective-permute-start.3 = (f32[128,512]{1,0:T(8,128)S(1)}, f32[128,512]{1,0:T(8,128)S(1)}, u32[]{:S(2)}, u32[]{:S(2)}) collective-permute-start(f32[128,512]{1,0:T(8,128)S(1)} %collective-permute-done.2.refs_3_), channel_id=1, source_target_pairs={{0,1},{1,0},{2,3},{3,2},{4,5},{5,4},{6,7},{7,6},{8,9},{9,8},{10,11... | collective-permute-start | bytes 786440 | tf_op jit(solution)/shard_map/ppermute | solution.py:409
  21.3 0.0 collective-permute-done.5.last.refs_7_
  21.3 2.7 %collective-permute-start.10 = (f32[128,512]{1,0:T(8,128)S(1)}, f32[128,512]{1,0:T(8,128)S(1)}, u32[]{:S(2)}, u32[]{:S(2)}) collective-permute-start(f32[128,512]{1,0:T(8,128)S(1)} %collective-permute-done.9.refs_10_), channel_id=1, source_target_pairs={{0,1},{1,0},{2,3},{3,2},{4,5},{5,4},{6,7},{7,6},{8,9},{9,8},{10,11... | collective-permute-start | bytes 786440 | tf_op jit(solution)/shard_map/ppermute | solution.py:409
  24.0 2.3 %collective-permute-done.7.refs_0_ = f32[128,512]{1,0:T(8,128)S(1)} collective-permute-done((f32[128,512]{1,0:T(8,128)S(1)}, f32[128,512]{1,0:T(8,128)S(1)}, u32[]{:S(2)}, u32[]{:S(2)}) %collective-permute-start.7) | collective-permute-done | bytes 262176 | tf_op jit(solution)/shard_map/ppermute | solution.py:409
  26.2 0.7 %collective-permute-start.6 = (f32[128,512]{1,0:T(8,128)S(1)}, f32[128,512]{1,0:T(8,128)S(1)}, u32[]{:S(2)}, u32[]{:S(2)}) collective-permute-start(f32[128,512]{1,0:T(8,128)S(1)} %collective-permute-done.5.last.refs_7_), channel_id=1, source_target_pairs={{0,1},{1,0},{2,3},{3,2},{4,5},{5,4},{6,7},{7,6},{8,9},{9,8},{10,11... | collective-permute-start | bytes 786440 | tf_op jit(solution)/shard_map/ppermute | solution.py:409
  27.0 0.4 collective-permute-done.11.refs_12_
  27.4 0.0 collective-permute-start.8
  27.4 0.0 collective-permute-done.1.refs_2_.refs_5_
  27.4 0.5 collective-permute-start.12
  27.9 0.0 collective-permute-done.3.refs_4_
  27.9 0.0 copy-done.1
  27.9 5.7 %shard_map.84 = (f32[128,128]{1,0:T(8,128)S(1)}, f32[384,384]{1,0:T(8,128)S(1)}, f32[384,128]{1,0:T(8,128)S(1)}, f32[8,128]{1,0:T(8,128)S(1)}) custom-call(s32[5]{0:T(128)S(1)} %stack.23.place_ref, f32[128,512]{1,0:T(8,128)S(1)} %copy-done.1, f32[128,512]{1,0:T(8,128)S(1)} %collective-permute-done.refs_1_.refs_4_, ...), custom_call_target="tpu_custom_call" | custom-call | flops 10000000000 | bytes 2097152 | tf_op jit(solution)/shard_map/pallas_call | solution.py:180
  33.6 5.6 %shard_map.85 = (f32[128,256]{1,0:T(8,128)S(1)}, f32[256,256]{1,0:T(8,128)S(1)}, f32[256,256]{1,0:T(8,128)S(1)}, f32[8,128]{1,0:T(8,128)S(1)}) custom-call(s32[5]{0:T(128)S(1)} %stack.23.place_ref, f32[8,128]{1,0:T(8,128)S(1)} %get-tuple-element.19.refs_0_, f32[384,384]{1,0:T(8,128)S(1)} %get-tuple-element.20.refs_1_, f32[384,128]{1,0:T(8,128)S(1)} %get-tuple-element.21.refs_2_), custom_call_target="tpu_custom_call" | custom-call | flops 10000000000 | bytes 1179648 | tf_op jit(solution)/shard_map/pallas_call | solution.py:180
  39.2 0.0 collective-permute-done.6.last_swapped.refs_8_
  39.2 0.0 collective-permute-done.8.refs_1_
  39.2 0.7 %route.1 = (f32[128,512]{1,0:T(8,128)S(1)}, f32[128,512]{1,0:T(8,128)S(1)}, f32[8,128]{1,0:T(8,128)S(1)}) custom-call(s32[5]{0:T(128)S(1)} %stack.23.place_ref, f32[8,128]{1,0:T(8,128)S(1)} %get-tuple-element.23._, f32[128,512]{1,0:T(8,128)S(1)} %join.1.own.refs_6_, f32[128,512]{1,0:T(8,128)S(1)} %collective-permute-done.5.last.refs_7_, ...), custom_call_target="tpu_custom_call" | custom-call | tf_op jit(solution)/shard_map/route/pallas_call | solution.py:275
  39.9 2.7 %collective-permute-start.13 = (f32[128,512]{1,0:T(8,128)S(1)}, f32[128,512]{1,0:T(8,128)S(1)}, u32[]{:S(2)}, u32[]{:S(2)}) collective-permute-start(f32[128,512]{1,0:T(8,128)S(1)} %get-tuple-element.28), channel_id=1, source_target_pairs={{0,0},{1,2},{2,4},{3,6},{4,1},{5,3},{6,5},{7,7},{8,8},{9,10},{10,1... | collective-permute-start | bytes 786440 | tf_op jit(solution)/shard_map/ppermute | solution.py:409
  42.6 2.8 %collective-permute-start.14 = (f32[128,512]{1,0:T(8,128)S(1)}, f32[128,512]{1,0:T(8,128)S(1)}, u32[]{:S(2)}, u32[]{:S(2)}) collective-permute-start(f32[128,512]{1,0:T(8,128)S(1)} %get-tuple-element.29), channel_id=1, source_target_pairs={{0,4},{1,6},{2,0},{3,2},{4,5},{5,7},{6,1},{7,3},{8,12},{9,14},{10,... | collective-permute-start | bytes 786440 | tf_op jit(solution)/shard_map/ppermute | solution.py:409
  45.4 0.0 copy-start.3
  45.4 0.0 copy-start.6
  45.4 9.4 %shard_map.86.refs_2_ = f32[256,512]{1,0:T(8,128)S(1)} custom-call(s32[5]{0:T(128)S(1)} %stack.23.place_ref, f32[8,128]{1,0:T(8,128)S(1)} %get-tuple-element.25.refs_0_, f32[256,256]{1,0:T(8,128)S(1)} %get-tuple-element.26.refs_1_, f32[256,256]{1,0:T(8,128)S(1)} %get-tuple-element.27.refs_2_), custom_call_target="tpu_custom_call" | custom-call | flops 10000000000 | bytes 524288 | tf_op jit(solution)/shard_map/pallas_call | solution.py:180
  54.8 0.0 collective-permute-done.10.refs_11_
  54.8 0.0 collective-permute-done.12.refs_13_
  54.8 1.2 %collective-permute-done.13.refs_14_ = f32[128,512]{1,0:T(8,128)S(1)} collective-permute-done((f32[128,512]{1,0:T(8,128)S(1)}, f32[128,512]{1,0:T(8,128)S(1)}, u32[]{:S(2)}, u32[]{:S(2)}) %collective-permute-start.13) | collective-permute-done | bytes 262176 | tf_op jit(solution)/shard_map/ppermute | solution.py:409
  56.0 0.0 collective-permute-done.14.refs_15_
  56.0 0.0 copy-done.3
  56.0 0.0 copy-done.6
  56.0 6.4 %update.1 = (f32[128,512]{1,0:T(8,128)}, f32[32,512]{1,0:T(8,128)}, f32[32,512]{1,0:T(8,128)}, f32[256,128]{1,0:T(8,128)}) custom-call(s32[5]{0:T(128)S(1)} %stack.23.place_ref, f32[128,128]{1,0:T(8,128)S(1)} %get-tuple-element.18.refs_0_, f32[128,256]{1,0:T(8,128)S(1)} %get-tuple-element.22.refs_1_, f32[256,512]{1,0:T(8,128)S(1)} %shard_map.86.refs_2_, ...), custom_call_target="tpu_custom_call" | custom-call | flops 10000000000 | bytes 2097152 | tf_op jit(solution)/shard_map/update/pallas_call | solution.py:376
Async XLA Ops:
  0.7 1.0 %copy-start = (f32[128,512]{1,0:T(8,128)S(1)}, f32[128,512]{1,0:T(8,128)}, u32[]{:S(2)}) copy-start(f32[128,512]{1,0:T(8,128)} %refs_0_.1) | copy-start | bytes 786436
  1.7 0.9 %copy-start.2 = (f32[128,512]{1,0:T(8,128)S(1)}, f32[128,512]{1,0:T(8,128)}, u32[]{:S(2)}) copy-start(f32[128,512]{1,0:T(8,128)} %refs_3_.1) | copy-start | bytes 786436
  2.6 0.8 %copy-start.4 = (f32[32,512]{1,0:T(8,128)S(1)}, f32[32,512]{1,0:T(8,128)}, u32[]{:S(2)}) copy-start(f32[32,512]{1,0:T(8,128)} %b_panel.1) | copy-start | bytes 196612
  3.5 0.8 %copy-start.5 = (f32[32,512]{1,0:T(8,128)S(1)}, f32[32,512]{1,0:T(8,128)}, u32[]{:S(2)}) copy-start(f32[32,512]{1,0:T(8,128)} %a_panel.1) | copy-start | bytes 196612
  5.1 11.2 %collective-permute-start = (f32[128,512]{1,0:T(8,128)S(1)}, f32[128,512]{1,0:T(8,128)S(1)}, u32[]{:S(2)}, u32[]{:S(2)}) collective-permute-start(f32[128,512]{1,0:T(8,128)S(1)} %get-tuple-element.17), channel_id=1, source_target_pairs={{0,24},{1,25},{2,26},{3,27},{4,28},{5,29},{6,30},{7,31},{8,16},{9,... | collective-permute-start | bytes 786440 | tf_op jit(solution)/shard_map/ppermute | solution.py:409
  8.1 9.7 %collective-permute-start.2 = (f32[128,512]{1,0:T(8,128)S(1)}, f32[128,512]{1,0:T(8,128)S(1)}, u32[]{:S(2)}, u32[]{:S(2)}) collective-permute-start(f32[128,512]{1,0:T(8,128)S(1)} %copy-done), channel_id=1, source_target_pairs={{0,8},{1,17},{2,10},{3,19},{4,12},{5,21},{6,14},{7,23},{8,0},{9,25... | collective-permute-start | bytes 786440 | tf_op jit(solution)/shard_map/ppermute | solution.py:409
  8.4 12.3 %collective-permute-start.9 = (f32[128,512]{1,0:T(8,128)S(1)}, f32[128,512]{1,0:T(8,128)S(1)}, u32[]{:S(2)}, u32[]{:S(2)}) collective-permute-start(f32[128,512]{1,0:T(8,128)S(1)} %copy-done.2), channel_id=1, source_target_pairs={{0,8},{1,17},{2,10},{3,19},{4,12},{5,21},{6,14},{7,23},{8,0},{9,25... | collective-permute-start | bytes 786440 | tf_op jit(solution)/shard_map/ppermute | solution.py:409
  9.6 18.3 %copy-start.1 = (f32[128,512]{1,0:T(8,128)S(1)}, f32[128,512]{1,0:T(8,128)}, u32[]{:S(2)}) copy-start(f32[128,512]{1,0:T(8,128)} %refs_0_.1) | copy-start | bytes 786436
  9.6 2.5 %collective-permute-start.4 = (f32[64,512]{1,0:T(8,128)S(1)}, f32[64,512]{1,0:T(8,128)S(1)}, u32[]{:S(2)}, u32[]{:S(2)}) collective-permute-start(f32[64,512]{1,0:T(8,128)S(1)} %get-tuple-element.24.own), channel_id=1, source_target_pairs={{0,1},{1,0},{2,3},{3,2},{4,5},{5,4},{6,7},{7,6},{8,9},{9,8},{10,11... | collective-permute-start | bytes 393224 | tf_op jit(solution)/shard_map/ppermute | solution.py:409
  12.7 8.6 %collective-permute-start.5 = (f32[128,512]{1,0:T(8,128)S(1)}, f32[128,512]{1,0:T(8,128)S(1)}, u32[]{:S(2)}, u32[]{:S(2)}) collective-permute-start(f32[128,512]{1,0:T(8,128)S(1)} %join.1.own.refs_6_), channel_id=1, source_target_pairs={{0,24},{1,7},{2,26},{3,5},{4,28},{5,3},{6,30},{7,1},{8,16},{9,15},... | collective-permute-start | bytes 786440 | tf_op jit(solution)/shard_map/ppermute | solution.py:409
  16.1 10.2 %collective-permute-start.7 = (f32[128,512]{1,0:T(8,128)S(1)}, f32[128,512]{1,0:T(8,128)S(1)}, u32[]{:S(2)}, u32[]{:S(2)}) collective-permute-start(f32[128,512]{1,0:T(8,128)S(1)} %join.1.own.refs_6_), channel_id=1, source_target_pairs={{0,8},{1,17},{2,10},{3,19},{4,12},{5,21},{6,14},{7,23},{8,0},{9,25... | collective-permute-start | bytes 786440 | tf_op jit(solution)/shard_map/ppermute | solution.py:409
  16.3 11.1 %collective-permute-start.11 = (f32[128,512]{1,0:T(8,128)S(1)}, f32[128,512]{1,0:T(8,128)S(1)}, u32[]{:S(2)}, u32[]{:S(2)}) collective-permute-start(f32[128,512]{1,0:T(8,128)S(1)} %join.1.own.refs_6_), channel_id=1, source_target_pairs={{0,2},{1,5},{2,0},{3,7},{4,6},{5,1},{6,4},{7,3},{8,10},{9,13},{10,... | collective-permute-start | bytes 786440 | tf_op jit(solution)/shard_map/ppermute | solution.py:409
  17.8 9.6 %collective-permute-start.1 = (f32[128,512]{1,0:T(8,128)S(1)}, f32[128,512]{1,0:T(8,128)S(1)}, u32[]{:S(2)}, u32[]{:S(2)}) collective-permute-start(f32[128,512]{1,0:T(8,128)S(1)} %collective-permute-done.refs_1_.refs_4_), channel_id=1, source_target_pairs={{0,1},{1,0},{2,3},{3,2},{4,5},{5,4},{6,7},{7,6},{8,9},{9,8},{10,11... | collective-permute-start | bytes 786440 | tf_op jit(solution)/shard_map/ppermute | solution.py:409
  20.6 7.3 %collective-permute-start.3 = (f32[128,512]{1,0:T(8,128)S(1)}, f32[128,512]{1,0:T(8,128)S(1)}, u32[]{:S(2)}, u32[]{:S(2)}) collective-permute-start(f32[128,512]{1,0:T(8,128)S(1)} %collective-permute-done.2.refs_3_), channel_id=1, source_target_pairs={{0,1},{1,0},{2,3},{3,2},{4,5},{5,4},{6,7},{7,6},{8,9},{9,8},{10,11... | collective-permute-start | bytes 786440 | tf_op jit(solution)/shard_map/ppermute | solution.py:409
  21.3 33.5 %collective-permute-start.10 = (f32[128,512]{1,0:T(8,128)S(1)}, f32[128,512]{1,0:T(8,128)S(1)}, u32[]{:S(2)}, u32[]{:S(2)}) collective-permute-start(f32[128,512]{1,0:T(8,128)S(1)} %collective-permute-done.9.refs_10_), channel_id=1, source_target_pairs={{0,1},{1,0},{2,3},{3,2},{4,5},{5,4},{6,7},{7,6},{8,9},{9,8},{10,11... | collective-permute-start | bytes 786440 | tf_op jit(solution)/shard_map/ppermute | solution.py:409
  26.2 13.0 %collective-permute-start.6 = (f32[128,512]{1,0:T(8,128)S(1)}, f32[128,512]{1,0:T(8,128)S(1)}, u32[]{:S(2)}, u32[]{:S(2)}) collective-permute-start(f32[128,512]{1,0:T(8,128)S(1)} %collective-permute-done.5.last.refs_7_), channel_id=1, source_target_pairs={{0,1},{1,0},{2,3},{3,2},{4,5},{5,4},{6,7},{7,6},{8,9},{9,8},{10,11... | collective-permute-start | bytes 786440 | tf_op jit(solution)/shard_map/ppermute | solution.py:409
  27.4 11.8 %collective-permute-start.8 = (f32[128,512]{1,0:T(8,128)S(1)}, f32[128,512]{1,0:T(8,128)S(1)}, u32[]{:S(2)}, u32[]{:S(2)}) collective-permute-start(f32[128,512]{1,0:T(8,128)S(1)} %collective-permute-done.7.refs_0_), channel_id=1, source_target_pairs={{0,1},{1,0},{2,3},{3,2},{4,5},{5,4},{6,7},{7,6},{8,9},{9,8},{10,11... | collective-permute-start | bytes 786440 | tf_op jit(solution)/shard_map/ppermute | solution.py:409
  27.4 27.4 %collective-permute-start.12 = (f32[128,512]{1,0:T(8,128)S(1)}, f32[128,512]{1,0:T(8,128)S(1)}, u32[]{:S(2)}, u32[]{:S(2)}) collective-permute-start(f32[128,512]{1,0:T(8,128)S(1)} %collective-permute-done.11.refs_12_), channel_id=1, source_target_pairs={{0,1},{1,0},{2,3},{3,2},{4,5},{5,4},{6,7},{7,6},{8,9},{9,8},{10,11... | collective-permute-start | bytes 786440 | tf_op jit(solution)/shard_map/ppermute | solution.py:409
  39.9 16.1 %collective-permute-start.13 = (f32[128,512]{1,0:T(8,128)S(1)}, f32[128,512]{1,0:T(8,128)S(1)}, u32[]{:S(2)}, u32[]{:S(2)}) collective-permute-start(f32[128,512]{1,0:T(8,128)S(1)} %get-tuple-element.28), channel_id=1, source_target_pairs={{0,0},{1,2},{2,4},{3,6},{4,1},{5,3},{6,5},{7,7},{8,8},{9,10},{10,1... | collective-permute-start | bytes 786440 | tf_op jit(solution)/shard_map/ppermute | solution.py:409
  42.6 13.4 %collective-permute-start.14 = (f32[128,512]{1,0:T(8,128)S(1)}, f32[128,512]{1,0:T(8,128)S(1)}, u32[]{:S(2)}, u32[]{:S(2)}) collective-permute-start(f32[128,512]{1,0:T(8,128)S(1)} %get-tuple-element.29), channel_id=1, source_target_pairs={{0,4},{1,6},{2,0},{3,2},{4,5},{5,7},{6,1},{7,3},{8,12},{9,14},{10,... | collective-permute-start | bytes 786440 | tf_op jit(solution)/shard_map/ppermute | solution.py:409
  45.4 10.6 %copy-start.3 = (f32[128,512]{1,0:T(8,128)S(1)}, f32[128,512]{1,0:T(8,128)}, u32[]{:S(2)}) copy-start(f32[128,512]{1,0:T(8,128)} %refs_3_.1) | copy-start | bytes 786436
  45.4 10.6 %copy-start.6 = (f32[256,128]{1,0:T(8,128)S(1)}, f32[256,128]{1,0:T(8,128)}, u32[]{:S(2)}) copy-start(f32[256,128]{1,0:T(8,128)} %refs_9_.1) | copy-start | bytes 393220

commit v2 on v1

--- a/solution.py
+++ b/solution.py
@@ -122,7 +122,7 @@
             out_ref[rows, hi:] = jnp.zeros((BLOCK, out_ref.shape[1] - hi), jnp.float32)
 
 
-def gather_square(work, core, me, count, own, ops, swapped, last, last_swapped, holder):
+def gather_square(work, core, me, count, own, ops, swapped, last, last_swapped):
     height = own.shape[0]
 
     def place(source, piece):
@@ -133,11 +133,15 @@
         place(me ^ (2 * j + 1 + core), ops[j])
         place(me ^ (2 * j + 2 - core), swapped[j])
 
-    @pl.when(core == holder)
-    def _():
+    if last_swapped is None:
         place(me ^ (count - 1), last)
-
-    @pl.when(core != holder)
+        return
+
+    @pl.when(core == 0)
+    def _():
+        place(me ^ (count - 1), last)
+
+    @pl.when(core != 0)
     def _():
         place(me ^ (count - 1), last_swapped)
 
@@ -154,7 +158,7 @@
     inverse_out, work, sums = refs[0], refs[-2], refs[-1]
     total, size = inverse_out.shape[1] // BLOCK, work.shape[0]
     if first == 0:
-        gather_square(work, place_ref[1], place_ref[0], count, own, ops, swapped, final, final_swapped, 0)
+        gather_square(work, place_ref[1], place_ref[0], count, own, ops, swapped, final, final_swapped)
         total = size // BLOCK
     else:
         work[...] = work_in[...]
@@ -188,62 +192,25 @@
     )(places, *operands)
 
 
-def pack_kernel(place_ref, b_diag, a_diag, b_panel, a_panel, last_out, panel_out, sems):
-    rows = b_panel.shape[0]
-    upper = pltpu.make_async_copy(b_panel, panel_out.at[pl.ds(0, rows)], sems.at[0])
-    lower = pltpu.make_async_copy(a_panel, panel_out.at[pl.ds(rows, rows)], sems.at[1])
-    upper.start()
-    lower.start()
-
-    @pl.when(place_ref[1] == 0)
-    def _():
-        copy = pltpu.make_async_copy(b_diag, last_out, sems.at[2])
-        copy.start()
-        copy.wait()
-
-    @pl.when(place_ref[1] != 0)
-    def _():
-        copy = pltpu.make_async_copy(a_diag, last_out, sems.at[3])
-        copy.start()
-        copy.wait()
-
-    upper.wait()
-    lower.wait()
-
-
-def pack(places, b_diag, a_diag, b_panel, a_panel):
-    rows, size = b_panel.shape
-    return pl.pallas_call(
-        pack_kernel,
-        out_shape=(
-            jax.ShapeDtypeStruct(b_diag.shape, jnp.float32),
-            jax.ShapeDtypeStruct((2 * rows, size), jnp.float32),
-        ),
-        in_specs=[SMEM] + [pl.BlockSpec(memory_space=pltpu.HBM)] * 4,
-        out_specs=(VMEM,) * 2,
-        scratch_shapes=[pltpu.SemaphoreType.DMA((4,))],
-        compiler_params=memory(4 * a_diag.size + 4 * b_panel.size),
-        name="pack",
-    )(places, b_diag, a_diag, b_panel, a_panel)
-
-
-def join_kernel(place_ref, own, other, out):
-    both = own.shape[0]
+def join_kernel(place_ref, b_own, a_own, b_other, a_other, out):
+    rows = b_own.shape[0]
     core = place_ref[1]
-    out[pl.ds(pl.multiple_of(core * both, 8), both), :] = own[...]
-    out[pl.ds(pl.multiple_of((1 - core) * both, 8), both), :] = other[...]
-
-
-def join(places, own, other):
-    both, size = own.shape
+    for k, piece in enumerate((b_own, a_own)):
+        out[pl.ds(pl.multiple_of((2 * core + k) * rows, 8), rows), :] = piece[...]
+    for k, piece in enumerate((b_other, a_other)):
+        out[pl.ds(pl.multiple_of((2 - 2 * core + k) * rows, 8), rows), :] = piece[...]
+
+
+def join(places, *pieces):
+    rows, size = pieces[0].shape
     return pl.pallas_call(
         join_kernel,
-        out_shape=jax.ShapeDtypeStruct((2 * both, size), jnp.float32),
-        in_specs=[SMEM] + [VMEM] * 2,
+        out_shape=jax.ShapeDtypeStruct((4 * rows, size), jnp.float32),
+        in_specs=[SMEM] + [VMEM] * 4,
         out_specs=VMEM,
-        compiler_params=memory(4 * own.size),
+        compiler_params=memory(8 * pieces[0].size),
         name="join",
-    )(places, own, other)
+    )(places, *pieces)
 
 
 def route_kernel(count, chips, place_ref, _, own, last, last_swapped, *refs):
@@ -302,7 +269,7 @@
 
 def update_kernel(count, chips, parts, place_ref, *refs):
     inverses, refs = refs[:parts], refs[parts:]
-    (diag, square, square_swapped, panel, final, final_swapped, trail_ref), refs = refs[:7], refs[7:]
+    (diag, square, panel, final, final_swapped, trail_ref), refs = refs[:6], refs[6:]
     extra, more, pairs = count // 2 - 1, chips // 2 - 1, chips // 2
     groups = []
     for n in (extra, extra, more, more, pairs):
@@ -313,7 +280,7 @@
     row, core, chip, place = place_ref[0], place_ref[1], place_ref[2], place_ref[4]
     height, size = diag.shape
     rows = panel.shape[0] // 4
-    gather_square(diag_work, core, row, count, diag, diag_ops, diag_swapped, square, square_swapped, 1)
+    gather_square(diag_work, core, row, count, diag, diag_ops, diag_swapped, square, None)
 
     def store(work, spot, piece):
         for c in range(2):
@@ -405,6 +372,8 @@
             for z in range(chips):
                 for c in range(cores):
                     to = target(r, z, c)
+                    if to is None:
+                        continue
                     pairs.append(((r * chips + z) * cores + c, (to[0] * chips + to[1]) * cores + to[2]))
         return lax.ppermute(array, ("row", "chip", "core"), pairs)
 
@@ -421,16 +390,16 @@
     places = jnp.stack([row, core, chip, slot, chip * 2 + core]).astype(jnp.int32)
     extra, more = range(count // 2 - 1), range(chips // 2 - 1)
     b_ops = [to_rows(b_diag, j) for j in extra]
-    mixed, own = pack(places, b_diag, a_diag, b_panel, a_panel)
-    other = swap(own)
-    square = exchange(mixed, lambda r, z, c: (r ^ (count - 1), z, c))
-    panel = join(places, own, other)
+    square = exchange(b_diag, lambda r, z, c: None if c else (r ^ (count - 1), z, c))
+    b_other, a_other = swap(b_panel), swap(a_panel)
+    panel = join(places, b_panel, a_panel, b_other, a_other)
     p_ops = [to_rows(panel, j) for j in extra]
     final = exchange(panel, lambda r, z, c: (r, z ^ (chips - 1), c) if c else (r ^ (count - 1), z, c))
     z_ops = [to_chips(panel, j) for j in more]
-    a_ops = [to_rows(a_diag, j) for j in extra]
     b_swapped = [swap(x) for x in b_ops]
     square_swapped = swap(square)
+    a_ops = [to_rows(a_diag, j) for j in extra]
+    a_last = exchange(a_diag, lambda r, z, c: (r ^ (count - 1), z, c))
     total = size // BLOCK
     cuts = (0, total // 4, total // 2, total)
     top, work, sums, token = factor_part(
@@ -450,7 +419,7 @@
     a_swapped = [swap(x) for x in a_ops]
     (bottom,) = factor_part(places, [token, work, sums], count, cuts[2], cuts[3], total)
     shapes = (a_diag.shape, b_panel.shape, a_panel.shape, a_trail.shape)
-    singles = (a_diag, square, square_swapped, panel, final, final_swapped, a_trail)
+    singles = (a_diag, a_last, panel, final, final_swapped, a_trail)
     groups = (a_ops, a_swapped, z_ops, z_swapped, pieces)
     return update(places, (top, middle, bottom), singles, groups, count, chips, shapes)
 

time: 62.7 us -> 61.2 us (0.976)
  the two profiles are of different devices: /device:TPU:1 before, /device:TPU:0 now
where the time goes in v2:
time: 61.2 us; the launch traced here: 60.8 us
  Pallas kernels  28.2 us (46%)
  starting transfers between devices  25.1 us (41%)
  waiting for transfers between devices  4.96 us (8%)
  local copies, waits for them, and re-layouts  1.77 us (3%)
  between operations  0.77 us (1%)
    ppermute x17, starting transfers between devices, exchange(): return lax.ppermute(array, ('row', 'chip', 'core'), pairs)  25.1 us
    pallas_call x3, Pallas kernels, factor_part(): pl.pallas_call(functools.partial(step_kernel, count, first, last), out_sh...  20.6 us
    pallas_call x1, Pallas kernels, update(): pl.pallas_call(functools.partial(update_kernel, count, chips, len(inverse...  6.36 us
    ppermute x17, waiting for transfers between devices, exchange(): return lax.ppermute(array, ('row', 'chip', 'core'), pairs)  4.96 us
    unnamed x10, local copies, waits for them, and re-layouts  1.69 us
  transfers between devices with their start and end apart: 17, of which 6 were waited for; matrix products, arithmetic and copies ran while one was open for 0% of the time, Pallas kernels for 36%

profile of v2, /device:TPU:0, one launch (start us, length us, event | category | flops | bytes accessed | tf_op | source)
XLA Modules:
  0.0 60.8 jit_solution(6661457659485577339)
XLA Ops:
  0.6 5.8 %collective-permute-start = (f32[128,512]{1,0:T(8,128)}, f32[128,512]{1,0:T(8,128)S(1)}, u32[]{:S(2)}, u32[]{:S(2)}) collective-permute-start(f32[128,512]{1,0:T(8,128)} %refs_0_.1), channel_id=1, source_target_pairs={{0,24},{2,26},{4,28},{6,30},{8,16},{10,18},{12,20},{14,22},{16,8},... | collective-permute-start | bytes 786440 | tf_op jit(solution)/shard_map/ppermute | solution.py:378
  6.5 0.6 collective-permute-start.2
  7.1 1.5 %collective-permute-start.11 = (f32[128,512]{1,0:T(8,128)}, f32[128,512]{1,0:T(8,128)S(1)}, u32[]{:S(2)}, u32[]{:S(2)}) collective-permute-start(f32[128,512]{1,0:T(8,128)} %refs_3_.1), channel_id=1, source_target_pairs={{0,8},{1,17},{2,10},{3,19},{4,12},{5,21},{6,14},{7,23},{8,0},{9,25... | collective-permute-start | bytes 786440 | tf_op jit(solution)/shard_map/ppermute | solution.py:378
  8.6 0.0 collective-permute-start.4
  8.6 0.5 collective-permute-start.5
  9.1 0.1 stack.23.place_ref
  9.2 0.9 %collective-permute-done.4.b_other = f32[32,512]{1,0:T(8,128)S(1)} collective-permute-done((f32[32,512]{1,0:T(8,128)}, f32[32,512]{1,0:T(8,128)S(1)}, u32[]{:S(2)}, u32[]{:S(2)}) %collective-permute-start.4) | collective-permute-done | bytes 65568 | tf_op jit(solution)/shard_map/ppermute | solution.py:378
  10.0 0.2 collective-permute-done.5.a_other
  10.2 0.0 copy-start
  10.2 0.8 %copy-done = f32[32,512]{1,0:T(8,128)S(1)} copy-done((f32[32,512]{1,0:T(8,128)S(1)}, f32[32,512]{1,0:T(8,128)}, u32[]{:S(2)}) %copy-start) | copy-done | bytes 65560
  11.0 0.0 copy-start.1
  11.0 0.8 %copy-done.1 = f32[32,512]{1,0:T(8,128)S(1)} copy-done((f32[32,512]{1,0:T(8,128)S(1)}, f32[32,512]{1,0:T(8,128)}, u32[]{:S(2)}) %copy-start.1) | copy-done | bytes 65560
  11.9 0.0 copy-start.3
  11.9 0.0 copy-start.2
  11.9 0.6 join.1.own.refs_5_
  12.4 0.1 collective-permute-start.6
  12.5 1.9 %collective-permute-start.8 = (f32[128,512]{1,0:T(8,128)S(1)}, f32[128,512]{1,0:T(8,128)S(1)}, u32[]{:S(2)}, u32[]{:S(2)}) collective-permute-start(f32[128,512]{1,0:T(8,128)S(1)} %join.1.own.refs_5_), channel_id=1, source_target_pairs={{0,8},{1,17},{2,10},{3,19},{4,12},{5,21},{6,14},{7,23},{8,0},{9,25... | collective-permute-start | bytes 786440 | tf_op jit(solution)/shard_map/ppermute | solution.py:378
  14.5 0.0 collective-permute-done.refs_1_
  14.5 1.6 %collective-permute-start.13 = (f32[128,512]{1,0:T(8,128)S(1)}, f32[128,512]{1,0:T(8,128)S(1)}, u32[]{:S(2)}, u32[]{:S(2)}) collective-permute-start(f32[128,512]{1,0:T(8,128)S(1)} %join.1.own.refs_5_), channel_id=1, source_target_pairs={{0,2},{1,5},{2,0},{3,7},{4,6},{5,1},{6,4},{7,3},{8,10},{9,13},{10,... | collective-permute-start | bytes 786440 | tf_op jit(solution)/shard_map/ppermute | solution.py:378
  16.1 0.0 collective-permute-done.2.refs_3_
  16.1 0.4 collective-permute-start.1
  16.5 0.7 %collective-permute-done.11.refs_9_ = f32[128,512]{1,0:T(8,128)S(1)} collective-permute-done((f32[128,512]{1,0:T(8,128)}, f32[128,512]{1,0:T(8,128)S(1)}, u32[]{:S(2)}, u32[]{:S(2)}) %collective-permute-start.11) | collective-permute-done | bytes 262176 | tf_op jit(solution)/shard_map/ppermute | solution.py:378
  17.2 0.0 collective-permute-start.3
  17.2 2.7 %collective-permute-done.6.last.refs_6_ = f32[128,512]{1,0:T(8,128)S(1)} collective-permute-done((f32[128,512]{1,0:T(8,128)S(1)}, f32[128,512]{1,0:T(8,128)S(1)}, u32[]{:S(2)}, u32[]{:S(2)}) %collective-permute-start.6) | collective-permute-done | bytes 262176 | tf_op jit(solution)/shard_map/ppermute | solution.py:378
  19.9 0.0 copy-done.3
  19.9 2.6 %collective-permute-start.10 = (f32[128,512]{1,0:T(8,128)S(1)}, f32[128,512]{1,0:T(8,128)S(1)}, u32[]{:S(2)}, u32[]{:S(2)}) collective-permute-start(f32[128,512]{1,0:T(8,128)S(1)} %copy-done.3), channel_id=1, source_target_pairs={{0,24},{1,25},{2,26},{3,27},{4,28},{5,29},{6,30},{7,31},{8,16},{9,... | collective-permute-start | bytes 786440 | tf_op jit(solution)/shard_map/ppermute | solution.py:378
  22.5 0.4 collective-permute-done.8.refs_0_
  22.9 0.0 collective-permute-start.12
  22.9 0.2 collective-permute-done.13.refs_11_
  23.0 4.8 %collective-permute-start.7 = (f32[128,512]{1,0:T(8,128)S(1)}, f32[128,512]{1,0:T(8,128)S(1)}, u32[]{:S(2)}, u32[]{:S(2)}) collective-permute-start(f32[128,512]{1,0:T(8,128)S(1)} %collective-permute-done.6.last.refs_6_), channel_id=1, source_target_pairs={{0,1},{1,0},{2,3},{3,2},{4,5},{5,4},{6,7},{7,6},{8,9},{9,8},{10,11... | collective-permute-start | bytes 786440 | tf_op jit(solution)/shard_map/ppermute | solution.py:378
  27.8 0.0 collective-permute-done.1.refs_2_
  27.8 0.0 collective-permute-start.9
  27.8 0.0 collective-permute-done.3.refs_4_
  27.8 0.5 collective-permute-start.14
  28.3 0.0 copy-done.2
  28.3 5.7 %shard_map.84 = (f32[128,128]{1,0:T(8,128)S(1)}, f32[384,384]{1,0:T(8,128)S(1)}, f32[384,128]{1,0:T(8,128)S(1)}, f32[8,128]{1,0:T(8,128)S(1)}) custom-call(s32[5]{0:T(128)S(1)} %stack.23.place_ref, f32[128,512]{1,0:T(8,128)S(1)} %copy-done.2, f32[128,512]{1,0:T(8,128)S(1)} %collective-permute-done.refs_1_, f32[128,512]{1,0:T(8,128)S(1)} %collective-permute-done.1.refs_2_, ...), custom_call_target="tpu_custom_call" | custom-call | flops 10000000000 | bytes 2097152 | tf_op jit(solution)/shard_map/pallas_call | solution.py:184
  34.0 5.6 %shard_map.85 = (f32[128,256]{1,0:T(8,128)S(1)}, f32[256,256]{1,0:T(8,128)S(1)}, f32[256,256]{1,0:T(8,128)S(1)}, f32[8,128]{1,0:T(8,128)S(1)}) custom-call(s32[5]{0:T(128)S(1)} %stack.23.place_ref, f32[8,128]{1,0:T(8,128)S(1)} %get-tuple-element.16.refs_0_, f32[384,384]{1,0:T(8,128)S(1)} %get-tuple-element.17.refs_1_, f32[384,128]{1,0:T(8,128)S(1)} %get-tuple-element.18.refs_2_), custom_call_target="tpu_custom_call" | custom-call | flops 10000000000 | bytes 1179648 | tf_op jit(solution)/shard_map/pallas_call | solution.py:184
  39.6 0.0 collective-permute-done.7.last_swapped.refs_7_
  39.6 0.0 collective-permute-done.9.refs_1_
  39.6 0.7 %route.1 = (f32[128,512]{1,0:T(8,128)S(1)}, f32[128,512]{1,0:T(8,128)S(1)}, f32[8,128]{1,0:T(8,128)S(1)}) custom-call(s32[5]{0:T(128)S(1)} %stack.23.place_ref, f32[8,128]{1,0:T(8,128)S(1)} %get-tuple-element.20._, f32[128,512]{1,0:T(8,128)S(1)} %join.1.own.refs_5_, f32[128,512]{1,0:T(8,128)S(1)} %collective-permute-done.6.last.refs_6_, ...), custom_call_target="tpu_custom_call" | custom-call | tf_op jit(solution)/shard_map/route/pallas_call | solution.py:242
  40.3 0.7 %collective-permute-start.15 = (f32[128,512]{1,0:T(8,128)S(1)}, f32[128,512]{1,0:T(8,128)S(1)}, u32[]{:S(2)}, u32[]{:S(2)}) collective-permute-start(f32[128,512]{1,0:T(8,128)S(1)} %get-tuple-element.24), channel_id=1, source_target_pairs={{0,0},{1,2},{2,4},{3,6},{4,1},{5,3},{6,5},{7,7},{8,8},{9,10},{10,1... | collective-permute-start | bytes 786440 | tf_op jit(solution)/shard_map/ppermute | solution.py:378
  41.0 4.1 %collective-permute-start.16 = (f32[128,512]{1,0:T(8,128)S(1)}, f32[128,512]{1,0:T(8,128)S(1)}, u32[]{:S(2)}, u32[]{:S(2)}) collective-permute-start(f32[128,512]{1,0:T(8,128)S(1)} %get-tuple-element.25), channel_id=1, source_target_pairs={{0,4},{1,6},{2,0},{3,2},{4,5},{5,7},{6,1},{7,3},{8,12},{9,14},{10,... | collective-permute-start | bytes 786440 | tf_op jit(solution)/shard_map/ppermute | solution.py:378
  45.1 0.0 copy-start.4
  45.1 9.4 %shard_map.86.refs_2_ = f32[256,512]{1,0:T(8,128)S(1)} custom-call(s32[5]{0:T(128)S(1)} %stack.23.place_ref, f32[8,128]{1,0:T(8,128)S(1)} %get-tuple-element.21.refs_0_, f32[256,256]{1,0:T(8,128)S(1)} %get-tuple-element.22.refs_1_, f32[256,256]{1,0:T(8,128)S(1)} %get-tuple-element.23.refs_2_), custom_call_target="tpu_custom_call" | custom-call | flops 10000000000 | bytes 524288 | tf_op jit(solution)/shard_map/pallas_call | solution.py:184
  54.4 0.0 collective-permute-done.10.refs_4_
  54.4 0.0 collective-permute-done.12.refs_10_
  54.4 0.0 collective-permute-done.14.refs_12_
  54.5 0.0 collective-permute-done.15.refs_13_
  54.5 0.0 collective-permute-done.16.refs_14_
  54.5 0.0 copy-done.4
  54.5 6.4 %update.1 = (f32[128,512]{1,0:T(8,128)}, f32[32,512]{1,0:T(8,128)}, f32[32,512]{1,0:T(8,128)}, f32[256,128]{1,0:T(8,128)}) custom-call(s32[5]{0:T(128)S(1)} %stack.23.place_ref, f32[128,128]{1,0:T(8,128)S(1)} %get-tuple-element.15.refs_0_, f32[128,256]{1,0:T(8,128)S(1)} %get-tuple-element.19.refs_1_, f32[256,512]{1,0:T(8,128)S(1)} %shard_map.86.refs_2_, ...), custom_call_target="tpu_custom_call" | custom-call | flops 10000000000 | bytes 2097152 | tf_op jit(solution)/shard_map/update/pallas_call | solution.py:343
Async XLA Ops:
  0.6 13.8 %collective-permute-start = (f32[128,512]{1,0:T(8,128)}, f32[128,512]{1,0:T(8,128)S(1)}, u32[]{:S(2)}, u32[]{:S(2)}) collective-permute-start(f32[128,512]{1,0:T(8,128)} %refs_0_.1), channel_id=1, source_target_pairs={{0,24},{2,26},{4,28},{6,30},{8,16},{10,18},{12,20},{14,22},{16,8},... | collective-permute-start | bytes 786440 | tf_op jit(solution)/shard_map/ppermute | solution.py:378
  6.5 9.6 %collective-permute-start.2 = (f32[128,512]{1,0:T(8,128)}, f32[128,512]{1,0:T(8,128)S(1)}, u32[]{:S(2)}, u32[]{:S(2)}) collective-permute-start(f32[128,512]{1,0:T(8,128)} %refs_0_.1), channel_id=1, source_target_pairs={{0,8},{1,17},{2,10},{3,19},{4,12},{5,21},{6,14},{7,23},{8,0},{9,25... | collective-permute-start | bytes 786440 | tf_op jit(solution)/shard_map/ppermute | solution.py:378
  7.1 10.1 %collective-permute-start.11 = (f32[128,512]{1,0:T(8,128)}, f32[128,512]{1,0:T(8,128)S(1)}, u32[]{:S(2)}, u32[]{:S(2)}) collective-permute-start(f32[128,512]{1,0:T(8,128)} %refs_3_.1), channel_id=1, source_target_pairs={{0,8},{1,17},{2,10},{3,19},{4,12},{5,21},{6,14},{7,23},{8,0},{9,25... | collective-permute-start | bytes 786440 | tf_op jit(solution)/shard_map/ppermute | solution.py:378
  8.6 1.5 %collective-permute-start.4 = (f32[32,512]{1,0:T(8,128)}, f32[32,512]{1,0:T(8,128)S(1)}, u32[]{:S(2)}, u32[]{:S(2)}) collective-permute-start(f32[32,512]{1,0:T(8,128)} %b_own.1), channel_id=1, source_target_pairs={{0,1},{1,0},{2,3},{3,2},{4,5},{5,4},{6,7},{7,6},{8,9},{9,8},{10,11... | collective-permute-start | bytes 196616 | tf_op jit(solution)/shard_map/ppermute | solution.py:378
  8.6 1.6 %collective-permute-start.5 = (f32[32,512]{1,0:T(8,128)}, f32[32,512]{1,0:T(8,128)S(1)}, u32[]{:S(2)}, u32[]{:S(2)}) collective-permute-start(f32[32,512]{1,0:T(8,128)} %a_own.1), channel_id=1, source_target_pairs={{0,1},{1,0},{2,3},{3,2},{4,5},{5,4},{6,7},{7,6},{8,9},{9,8},{10,11... | collective-permute-start | bytes 196616 | tf_op jit(solution)/shard_map/ppermute | solution.py:378
  10.2 0.8 %copy-start = (f32[32,512]{1,0:T(8,128)S(1)}, f32[32,512]{1,0:T(8,128)}, u32[]{:S(2)}) copy-start(f32[32,512]{1,0:T(8,128)} %b_own.1) | copy-start | bytes 196612
  11.0 0.8 %copy-start.1 = (f32[32,512]{1,0:T(8,128)S(1)}, f32[32,512]{1,0:T(8,128)}, u32[]{:S(2)}) copy-start(f32[32,512]{1,0:T(8,128)} %a_own.1) | copy-start | bytes 196612
  11.9 8.0 %copy-start.3 = (f32[128,512]{1,0:T(8,128)S(1)}, f32[128,512]{1,0:T(8,128)}, u32[]{:S(2)}) copy-start(f32[128,512]{1,0:T(8,128)} %refs_3_.1) | copy-start | bytes 786436
  11.9 16.5 %copy-start.2 = (f32[128,512]{1,0:T(8,128)S(1)}, f32[128,512]{1,0:T(8,128)}, u32[]{:S(2)}) copy-start(f32[128,512]{1,0:T(8,128)} %refs_0_.1) | copy-start | bytes 786436
  12.4 7.4 %collective-permute-start.6 = (f32[128,512]{1,0:T(8,128)S(1)}, f32[128,512]{1,0:T(8,128)S(1)}, u32[]{:S(2)}, u32[]{:S(2)}) collective-permute-start(f32[128,512]{1,0:T(8,128)S(1)} %join.1.own.refs_5_), channel_id=1, source_target_pairs={{0,24},{1,7},{2,26},{3,5},{4,28},{5,3},{6,30},{7,1},{8,16},{9,15},... | collective-permute-start | bytes 786440 | tf_op jit(solution)/shard_map/ppermute | solution.py:378
  12.5 10.3 %collective-permute-start.8 = (f32[128,512]{1,0:T(8,128)S(1)}, f32[128,512]{1,0:T(8,128)S(1)}, u32[]{:S(2)}, u32[]{:S(2)}) collective-permute-start(f32[128,512]{1,0:T(8,128)S(1)} %join.1.own.refs_5_), channel_id=1, source_target_pairs={{0,8},{1,17},{2,10},{3,19},{4,12},{5,21},{6,14},{7,23},{8,0},{9,25... | collective-permute-start | bytes 786440 | tf_op jit(solution)/shard_map/ppermute | solution.py:378
  14.5 8.6 %collective-permute-start.13 = (f32[128,512]{1,0:T(8,128)S(1)}, f32[128,512]{1,0:T(8,128)S(1)}, u32[]{:S(2)}, u32[]{:S(2)}) collective-permute-start(f32[128,512]{1,0:T(8,128)S(1)} %join.1.own.refs_5_), channel_id=1, source_target_pairs={{0,2},{1,5},{2,0},{3,7},{4,6},{5,1},{6,4},{7,3},{8,10},{9,13},{10,... | collective-permute-start | bytes 786440 | tf_op jit(solution)/shard_map/ppermute | solution.py:378
  16.1 11.8 %collective-permute-start.1 = (f32[128,512]{1,0:T(8,128)S(1)}, f32[128,512]{1,0:T(8,128)S(1)}, u32[]{:S(2)}, u32[]{:S(2)}) collective-permute-start(f32[128,512]{1,0:T(8,128)S(1)} %collective-permute-done.refs_1_), channel_id=1, source_target_pairs={{0,1},{1,0},{2,3},{3,2},{4,5},{5,4},{6,7},{7,6},{8,9},{9,8},{10,11... | collective-permute-start | bytes 786440 | tf_op jit(solution)/shard_map/ppermute | solution.py:378
  17.2 10.6 %collective-permute-start.3 = (f32[128,512]{1,0:T(8,128)S(1)}, f32[128,512]{1,0:T(8,128)S(1)}, u32[]{:S(2)}, u32[]{:S(2)}) collective-permute-start(f32[128,512]{1,0:T(8,128)S(1)} %collective-permute-done.2.refs_3_), channel_id=1, source_target_pairs={{0,1},{1,0},{2,3},{3,2},{4,5},{5,4},{6,7},{7,6},{8,9},{9,8},{10,11... | collective-permute-start | bytes 786440 | tf_op jit(solution)/shard_map/ppermute | solution.py:378
  19.9 34.5 %collective-permute-start.10 = (f32[128,512]{1,0:T(8,128)S(1)}, f32[128,512]{1,0:T(8,128)S(1)}, u32[]{:S(2)}, u32[]{:S(2)}) collective-permute-start(f32[128,512]{1,0:T(8,128)S(1)} %copy-done.3), channel_id=1, source_target_pairs={{0,24},{1,25},{2,26},{3,27},{4,28},{5,29},{6,30},{7,31},{8,16},{9,... | collective-permute-start | bytes 786440 | tf_op jit(solution)/shard_map/ppermute | solution.py:378
  22.9 31.6 %collective-permute-start.12 = (f32[128,512]{1,0:T(8,128)S(1)}, f32[128,512]{1,0:T(8,128)S(1)}, u32[]{:S(2)}, u32[]{:S(2)}) collective-permute-start(f32[128,512]{1,0:T(8,128)S(1)} %collective-permute-done.11.refs_9_), channel_id=1, source_target_pairs={{0,1},{1,0},{2,3},{3,2},{4,5},{5,4},{6,7},{7,6},{8,9},{9,8},{10,11... | collective-permute-start | bytes 786440 | tf_op jit(solution)/shard_map/ppermute | solution.py:378
  23.0 16.6 %collective-permute-start.7 = (f32[128,512]{1,0:T(8,128)S(1)}, f32[128,512]{1,0:T(8,128)S(1)}, u32[]{:S(2)}, u32[]{:S(2)}) collective-permute-start(f32[128,512]{1,0:T(8,128)S(1)} %collective-permute-done.6.last.refs_6_), channel_id=1, source_target_pairs={{0,1},{1,0},{2,3},{3,2},{4,5},{5,4},{6,7},{7,6},{8,9},{9,8},{10,11... | collective-permute-start | bytes 786440 | tf_op jit(solution)/shard_map/ppermute | solution.py:378
  27.8 11.8 %collective-permute-start.9 = (f32[128,512]{1,0:T(8,128)S(1)}, f32[128,512]{1,0:T(8,128)S(1)}, u32[]{:S(2)}, u32[]{:S(2)}) collective-permute-start(f32[128,512]{1,0:T(8,128)S(1)} %collective-permute-done.8.refs_0_), channel_id=1, source_target_pairs={{0,1},{1,0},{2,3},{3,2},{4,5},{5,4},{6,7},{7,6},{8,9},{9,8},{10,11... | collective-permute-start | bytes 786440 | tf_op jit(solution)/shard_map/ppermute | solution.py:378
  27.8 26.6 %collective-permute-start.14 = (f32[128,512]{1,0:T(8,128)S(1)}, f32[128,512]{1,0:T(8,128)S(1)}, u32[]{:S(2)}, u32[]{:S(2)}) collective-permute-start(f32[128,512]{1,0:T(8,128)S(1)} %collective-permute-done.13.refs_11_), channel_id=1, source_target_pairs={{0,1},{1,0},{2,3},{3,2},{4,5},{5,4},{6,7},{7,6},{8,9},{9,8},{10,11... | collective-permute-start | bytes 786440 | tf_op jit(solution)/shard_map/ppermute | solution.py:378
  40.3 14.1 %collective-permute-start.15 = (f32[128,512]{1,0:T(8,128)S(1)}, f32[128,512]{1,0:T(8,128)S(1)}, u32[]{:S(2)}, u32[]{:S(2)}) collective-permute-start(f32[128,512]{1,0:T(8,128)S(1)} %get-tuple-element.24), channel_id=1, source_target_pairs={{0,0},{1,2},{2,4},{3,6},{4,1},{5,3},{6,5},{7,7},{8,8},{9,10},{10,1... | collective-permute-start | bytes 786440 | tf_op jit(solution)/shard_map/ppermute | solution.py:378
  41.0 13.5 %collective-permute-start.16 = (f32[128,512]{1,0:T(8,128)S(1)}, f32[128,512]{1,0:T(8,128)S(1)}, u32[]{:S(2)}, u32[]{:S(2)}) collective-permute-start(f32[128,512]{1,0:T(8,128)S(1)} %get-tuple-element.25), channel_id=1, source_target_pairs={{0,4},{1,6},{2,0},{3,2},{4,5},{5,7},{6,1},{7,3},{8,12},{9,14},{10,... | collective-permute-start | bytes 786440 | tf_op jit(solution)/shard_map/ppermute | solution.py:378
  45.1 9.4 %copy-start.4 = (f32[256,128]{1,0:T(8,128)S(1)}, f32[256,128]{1,0:T(8,128)}, u32[]{:S(2)}) copy-start(f32[256,128]{1,0:T(8,128)} %refs_8_.1) | copy-start | bytes 393220

commit v3 on v2

--- a/solution.py
+++ b/solution.py
@@ -33,7 +33,7 @@
     )
 
 
-def invert_small(block, offset):
+def invert_small(block, offset, columns):
     lanes = block.shape[1]
     groups = SMALL // 8
     cols = []
@@ -56,13 +56,20 @@
     for j in range(SMALL):
         g = j // 8
         c = cols[j]
-        pivot = spread_row(c[g], j % 8)
+        for h in range(g, groups):
+            columns[j, 8 * h : 8 * h + 8, :] = c[h]
+
+        def entry(m, j=j, c=c):
+            near = j > 0 and m <= j + 1
+            return spread_row(c[m // 8], m % 8) if near else columns[j, pl.ds(m, 8, stride=0), :]
+
+        pivot = entry(j)
         scale = 1.0 / pivot
         pivots[g] = pivot if j % 8 == 0 else jnp.where(sublane == j % 8, pivot, pivots[g])
         row = spread_row(rows[g], j % 8)
         low = [None if c[h] is None else c[h] * scale for h in range(groups)]
         for m in range(j + 1, SMALL):
-            t = spread_row(c[m // 8], m % 8)
+            t = entry(m)
             for h in range(m // 8, groups):
                 if m == j + 1:
                     cols[m][h] = cols[m][h] - (c[h] * t) * scale
@@ -74,14 +81,14 @@
     return jnp.concatenate([rows[h] * lax.rsqrt(pivots[h]) for h in range(groups)], axis=0)
 
 
-def invert_block(block):
+def invert_block(block, columns):
     size = block.shape[0]
     done = []
     total = None
     for b in range(size // SMALL):
         offset = b * SMALL
         below = offset + SMALL
-        small = invert_small(block[offset:below, :], offset)
+        small = invert_small(block[offset:below, :], offset, columns)
         last = below == size
         if not last:
             low = nt(block[below:, :], small)
@@ -95,13 +102,13 @@
     return jnp.concatenate(done, axis=0)
 
 
-def factor_steps(work, sums, out_ref, base, first, last, count):
+def factor_steps(work, sums, columns, out_ref, base, first, last, count):
     start = first * BLOCK
     for k in range(first, last):
         lo, hi = k * BLOCK, (k + 1) * BLOCK
         here = slice(lo - base, hi - base)
         rows = slice(lo - start, hi - start)
-        inverse = invert_block(work[here, here])
+        inverse = invert_block(work[here, here], columns)
         out_ref[rows, lo:hi] = inverse
         if k + 1 < count:
             below = slice(hi - base, count * BLOCK - base)
@@ -155,7 +162,7 @@
     else:
         _, work_in, sums_in = refs[:3]
         refs = refs[3:]
-    inverse_out, work, sums = refs[0], refs[-2], refs[-1]
+    inverse_out, work, sums, columns = refs[0], refs[-3], refs[-2], refs[-1]
     total, size = inverse_out.shape[1] // BLOCK, work.shape[0]
     if first == 0:
         gather_square(work, place_ref[1], place_ref[0], count, own, ops, swapped, final, final_swapped)
@@ -164,7 +171,7 @@
         work[...] = work_in[...]
         sums[:, : first * BLOCK] = sums_in[...]
         total = first + size // BLOCK
-    factor_steps(work, sums, inverse_out, first * BLOCK, first, last, total)
+    factor_steps(work, sums, columns, inverse_out, first * BLOCK, first, last, total)
     if last < total:
         work_out, sums_out, token_out = refs[1:4]
         cut = (last - first) * BLOCK
@@ -186,7 +193,11 @@
         out_shape=tuple(outs),
         in_specs=[SMEM] + [VMEM] * len(operands),
         out_specs=(VMEM,) * len(outs),
-        scratch_shapes=[pltpu.VMEM((size, size), jnp.float32), pltpu.VMEM((size, total * BLOCK), jnp.float32)],
+        scratch_shapes=[
+            pltpu.VMEM((size, size), jnp.float32),
+            pltpu.VMEM((size, total * BLOCK), jnp.float32),
+            pltpu.VMEM((SMALL, SMALL, BLOCK), jnp.float32),
+        ],
         cost_estimate=pl.CostEstimate(flops=10**10, bytes_accessed=8 * size * size, transcendentals=0),
         compiler_params=memory(4 * size * size),
     )(places, *operands)
@@ -276,9 +287,9 @@
         groups.append(refs[:n])
         refs = refs[n:]
     diag_ops, diag_swapped, row_ops, row_swapped, pieces = groups
-    diag_out, low_out, panel_out, trail_out, inverse_work, diag_work, rows_work, cols_work = refs
+    diag_out, low_out, panel_out, trail_out, upper_work, diag_work, rows_work, cols_work = refs
     row, core, chip, place = place_ref[0], place_ref[1], place_ref[2], place_ref[4]
-    height, size = diag.shape
+    height, _ = diag.shape
     rows = panel.shape[0] // 4
     gather_square(diag_work, core, row, count, diag, diag_ops, diag_swapped, square, None)
 
@@ -303,37 +314,41 @@
 
     for t in range(pairs):
         store(cols_work, lax.rem(chip - 2 * t + chips, chips) // 2, pieces[t])
+    cut = upper_work.shape[0]
     at = 0
-    for part in inverses:
+    for part in inverses[:-1]:
         tall, wide = part.shape
-        inverse_work[at : at + tall, :wide] = part[...]
-        if wide < size:
-            inverse_work[at : at + tall, wide:] = jnp.zeros((tall, size - wide), jnp.float32)
+        upper_work[at : at + tall, :wide] = part[...]
+        if wide < cut:
+            upper_work[at : at + tall, wide:] = jnp.zeros((tall, cut - wide), jnp.float32)
         at += tall
-
-    inverse = split(inverse_work[...])
-    left = split(product(inverse, split(diag_work[...]), NN))
-    reduced = product(left, inverse, NT)
-    diag_work[...] = reduced
-    diag_out[...] = diag_work[pl.ds(pl.multiple_of(row * height, 8), height), :]
-    reduced = split(reduced)
+    upper, lower = split(upper_work[...]), split(inverses[-1][...])
+
+    def back(value):
+        parts = split(value)
+        first = product([part[:, :cut] for part in parts], upper, NT)
+        return jnp.concatenate([first, product(parts, lower, NT)], axis=1)
+
+    diag = split(diag_work[...])
+    left = jnp.concatenate([product(upper, [part[:cut] for part in diag], NN), product(lower, diag, NN)], axis=0)
+    diag_work[...] = left
+    left = split(left)
 
     def panel(work):
-        low = product(split(work[0]), inverse, NT)
-        correction = 0.5 * product(split(low), reduced, NN)
-        mixed = product(split(work[1]), inverse, NT) - correction
-        return low, mixed, correction
-
-    low_rows, mixed_rows, correction = panel(rows_work)
-    rows_work[0] = low_rows
-    rows_work[1] = mixed_rows - correction
+        low = back(work[0])
+        change = product(split(low), left, NN)
+        start = work[1]
+        work[0] = low
+        work[1] = start - change
+        return split(low), split(back(start - 0.5 * change))
+
+    low_rows, mixed_rows = panel(rows_work)
+    low_cols, mixed_cols = panel(cols_work)
+    trail_out[...] = trail_ref[...] - (product(mixed_rows, low_cols, NT) + product(low_rows, mixed_cols, NT))
+    diag_out[...] = back(diag_work[pl.ds(pl.multiple_of(row * height, 8), height), :])
     mine = pl.ds(pl.multiple_of(place * rows, 8), rows)
     low_out[...] = rows_work[0, mine, :]
-    panel_out[...] = rows_work[1, mine, :]
-    low_cols, mixed_cols, _ = panel(cols_work)
-    trail_out[...] = trail_ref[...] - (
-        product(split(mixed_rows), split(low_cols), NT) + product(split(low_rows), split(mixed_cols), NT)
-    )
+    panel_out[...] = back(rows_work[1, mine, :])
 
 
 def update(places, inverses, singles, groups, count, chips, shapes):
@@ -346,7 +361,7 @@
         in_specs=[SMEM] + [VMEM] * len(operands),
         out_specs=(VMEM,) * 4,
         scratch_shapes=[
-            pltpu.VMEM((size, size), jnp.float32),
+            pltpu.VMEM((size - inverses[-1].shape[0],) * 2, jnp.float32),
             pltpu.VMEM((size, size), jnp.float32),
             pltpu.VMEM((2, height, size), jnp.float32),
             pltpu.VMEM((2, width, size), jnp.float32),

time: 61.2 us -> 60.6 us (level); the launches traced: 60.8 us -> 59.6 us
  Pallas kernels: 28.2 us -> 26.9 us
    pallas_call x3, Pallas kernels: 20.6 us -> 19.4 us  [factor_part(): pl.pallas_call(functools.partial(step_kernel, count, first, last), out_sh...]
  transfers between devices with their start and end apart: 17 -> 17, of which waited for: 6 -> 6; matrix products, arithmetic and copies ran while one was open for 0% -> 0% of each run, Pallas kernels for 36% -> 35%
where the time goes in v3:
time: 60.6 us; the launch traced here: 59.6 us
  Pallas kernels  26.9 us (44%)
  starting transfers between devices  25.1 us (41%)
  waiting for transfers between devices  4.96 us (8%)
  local copies, waits for them, and re-layouts  1.77 us (3%)
  between operations  0.77 us (1%)
    ppermute x17, starting transfers between devices, exchange(): return lax.ppermute(array, ('row', 'chip', 'core'), pairs)  25.1 us
    pallas_call x3, Pallas kernels, factor_part(): pl.pallas_call(functools.partial(step_kernel, count, first, last), out_sh...  19.4 us
    pallas_call x1, Pallas kernels, update(): pl.pallas_call(functools.partial(update_kernel, count, chips, len(inverse...  6.28 us
    ppermute x17, waiting for transfers between devices, exchange(): return lax.ppermute(array, ('row', 'chip', 'core'), pairs)  4.96 us
    unnamed x10, local copies, waits for them, and re-layouts  1.69 us
  transfers between devices with their start and end apart: 17, of which 6 were waited for; matrix products, arithmetic and copies ran while one was open for 0% of the time, Pallas kernels for 35%

profile of v3, /device:TPU:0, one launch (start us, length us, event | category | flops | bytes accessed | tf_op | source)
XLA Modules:
  0.0 59.6 jit_solution(2102847431503009587)
XLA Ops:
  0.6 5.8 %collective-permute-start = (f32[128,512]{1,0:T(8,128)}, f32[128,512]{1,0:T(8,128)S(1)}, u32[]{:S(2)}, u32[]{:S(2)}) collective-permute-start(f32[128,512]{1,0:T(8,128)} %refs_0_.1), channel_id=1, source_target_pairs={{0,24},{2,26},{4,28},{6,30},{8,16},{10,18},{12,20},{14,22},{16,8},... | collective-permute-start | bytes 786440 | tf_op jit(solution)/shard_map/ppermute | solution.py:393
  6.5 0.6 %collective-permute-start.2 = (f32[128,512]{1,0:T(8,128)}, f32[128,512]{1,0:T(8,128)S(1)}, u32[]{:S(2)}, u32[]{:S(2)}) collective-permute-start(f32[128,512]{1,0:T(8,128)} %refs_0_.1), channel_id=1, source_target_pairs={{0,8},{1,17},{2,10},{3,19},{4,12},{5,21},{6,14},{7,23},{8,0},{9,25... | collective-permute-start | bytes 786440 | tf_op jit(solution)/shard_map/ppermute | solution.py:393
  7.1 1.5 %collective-permute-start.11 = (f32[128,512]{1,0:T(8,128)}, f32[128,512]{1,0:T(8,128)S(1)}, u32[]{:S(2)}, u32[]{:S(2)}) collective-permute-start(f32[128,512]{1,0:T(8,128)} %refs_3_.1), channel_id=1, source_target_pairs={{0,8},{1,17},{2,10},{3,19},{4,12},{5,21},{6,14},{7,23},{8,0},{9,25... | collective-permute-start | bytes 786440 | tf_op jit(solution)/shard_map/ppermute | solution.py:393
  8.6 0.0 collective-permute-start.4
  8.6 0.5 collective-permute-start.5
  9.1 0.1 stack.23.place_ref
  9.2 0.9 %collective-permute-done.4.b_other = f32[32,512]{1,0:T(8,128)S(1)} collective-permute-done((f32[32,512]{1,0:T(8,128)}, f32[32,512]{1,0:T(8,128)S(1)}, u32[]{:S(2)}, u32[]{:S(2)}) %collective-permute-start.4) | collective-permute-done | bytes 65568 | tf_op jit(solution)/shard_map/ppermute | solution.py:393
  10.0 0.2 collective-permute-done.5.a_other
  10.2 0.0 copy-start
  10.2 0.8 %copy-done = f32[32,512]{1,0:T(8,128)S(1)} copy-done((f32[32,512]{1,0:T(8,128)S(1)}, f32[32,512]{1,0:T(8,128)}, u32[]{:S(2)}) %copy-start) | copy-done | bytes 65560
  11.0 0.0 copy-start.1
  11.0 0.8 %copy-done.1 = f32[32,512]{1,0:T(8,128)S(1)} copy-done((f32[32,512]{1,0:T(8,128)S(1)}, f32[32,512]{1,0:T(8,128)}, u32[]{:S(2)}) %copy-start.1) | copy-done | bytes 65560
  11.9 0.0 copy-start.3
  11.9 0.0 copy-start.2
  11.9 0.6 join.1.own.refs_5_
  12.4 0.1 collective-permute-start.6
  12.5 1.9 %collective-permute-start.8 = (f32[128,512]{1,0:T(8,128)S(1)}, f32[128,512]{1,0:T(8,128)S(1)}, u32[]{:S(2)}, u32[]{:S(2)}) collective-permute-start(f32[128,512]{1,0:T(8,128)S(1)} %join.1.own.refs_5_), channel_id=1, source_target_pairs={{0,8},{1,17},{2,10},{3,19},{4,12},{5,21},{6,14},{7,23},{8,0},{9,25... | collective-permute-start | bytes 786440 | tf_op jit(solution)/shard_map/ppermute | solution.py:393
  14.5 0.0 collective-permute-done.refs_1_
  14.5 1.6 %collective-permute-start.13 = (f32[128,512]{1,0:T(8,128)S(1)}, f32[128,512]{1,0:T(8,128)S(1)}, u32[]{:S(2)}, u32[]{:S(2)}) collective-permute-start(f32[128,512]{1,0:T(8,128)S(1)} %join.1.own.refs_5_), channel_id=1, source_target_pairs={{0,2},{1,5},{2,0},{3,7},{4,6},{5,1},{6,4},{7,3},{8,10},{9,13},{10,... | collective-permute-start | bytes 786440 | tf_op jit(solution)/shard_map/ppermute | solution.py:393
  16.1 0.0 collective-permute-done.2.refs_3_
  16.1 0.4 collective-permute-start.1
  16.5 0.7 %collective-permute-done.11.refs_9_ = f32[128,512]{1,0:T(8,128)S(1)} collective-permute-done((f32[128,512]{1,0:T(8,128)}, f32[128,512]{1,0:T(8,128)S(1)}, u32[]{:S(2)}, u32[]{:S(2)}) %collective-permute-start.11) | collective-permute-done | bytes 262176 | tf_op jit(solution)/shard_map/ppermute | solution.py:393
  17.2 0.0 collective-permute-start.3
  17.2 2.7 %collective-permute-done.6.last.refs_6_ = f32[128,512]{1,0:T(8,128)S(1)} collective-permute-done((f32[128,512]{1,0:T(8,128)S(1)}, f32[128,512]{1,0:T(8,128)S(1)}, u32[]{:S(2)}, u32[]{:S(2)}) %collective-permute-start.6) | collective-permute-done | bytes 262176 | tf_op jit(solution)/shard_map/ppermute | solution.py:393
  19.9 0.0 copy-done.3
  19.9 2.6 %collective-permute-start.10 = (f32[128,512]{1,0:T(8,128)S(1)}, f32[128,512]{1,0:T(8,128)S(1)}, u32[]{:S(2)}, u32[]{:S(2)}) collective-permute-start(f32[128,512]{1,0:T(8,128)S(1)} %copy-done.3), channel_id=1, source_target_pairs={{0,24},{1,25},{2,26},{3,27},{4,28},{5,29},{6,30},{7,31},{8,16},{9,... | collective-permute-start | bytes 786440 | tf_op jit(solution)/shard_map/ppermute | solution.py:393
  22.5 0.4 collective-permute-done.8.refs_0_
  22.9 0.0 collective-permute-start.12
  22.9 0.2 collective-permute-done.13.refs_11_
  23.0 4.8 %collective-permute-start.7 = (f32[128,512]{1,0:T(8,128)S(1)}, f32[128,512]{1,0:T(8,128)S(1)}, u32[]{:S(2)}, u32[]{:S(2)}) collective-permute-start(f32[128,512]{1,0:T(8,128)S(1)} %collective-permute-done.6.last.refs_6_), channel_id=1, source_target_pairs={{0,1},{1,0},{2,3},{3,2},{4,5},{5,4},{6,7},{7,6},{8,9},{9,8},{10,11... | collective-permute-start | bytes 786440 | tf_op jit(solution)/shard_map/ppermute | solution.py:393
  27.8 0.0 collective-permute-done.1.refs_2_
  27.8 0.0 collective-permute-start.9
  27.8 0.0 collective-permute-done.3.refs_4_
  27.8 0.5 collective-permute-start.14
  28.3 0.0 copy-done.2
  28.3 5.4 %shard_map.84 = (f32[128,128]{1,0:T(8,128)S(1)}, f32[384,384]{1,0:T(8,128)S(1)}, f32[384,128]{1,0:T(8,128)S(1)}, f32[8,128]{1,0:T(8,128)S(1)}) custom-call(s32[5]{0:T(128)S(1)} %stack.23.place_ref, f32[128,512]{1,0:T(8,128)S(1)} %copy-done.2, f32[128,512]{1,0:T(8,128)S(1)} %collective-permute-done.refs_1_, f32[128,512]{1,0:T(8,128)S(1)} %collective-permute-done.1.refs_2_, ...), custom_call_target="tpu_custom_call" | custom-call | flops 10000000000 | bytes 2097152 | tf_op jit(solution)/shard_map/pallas_call | solution.py:191
  33.8 5.3 %shard_map.85 = (f32[128,256]{1,0:T(8,128)S(1)}, f32[256,256]{1,0:T(8,128)S(1)}, f32[256,256]{1,0:T(8,128)S(1)}, f32[8,128]{1,0:T(8,128)S(1)}) custom-call(s32[5]{0:T(128)S(1)} %stack.23.place_ref, f32[8,128]{1,0:T(8,128)S(1)} %get-tuple-element.16.refs_0_, f32[384,384]{1,0:T(8,128)S(1)} %get-tuple-element.17.refs_1_, f32[384,128]{1,0:T(8,128)S(1)} %get-tuple-element.18.refs_2_), custom_call_target="tpu_custom_call" | custom-call | flops 10000000000 | bytes 1179648 | tf_op jit(solution)/shard_map/pallas_call | solution.py:191
  39.1 0.0 collective-permute-done.7.last_swapped.refs_7_
  39.1 0.0 collective-permute-done.9.refs_1_
  39.1 0.7 %route.1 = (f32[128,512]{1,0:T(8,128)S(1)}, f32[128,512]{1,0:T(8,128)S(1)}, f32[8,128]{1,0:T(8,128)S(1)}) custom-call(s32[5]{0:T(128)S(1)} %stack.23.place_ref, f32[8,128]{1,0:T(8,128)S(1)} %get-tuple-element.20._, f32[128,512]{1,0:T(8,128)S(1)} %join.1.own.refs_5_, f32[128,512]{1,0:T(8,128)S(1)} %collective-permute-done.6.last.refs_6_, ...), custom_call_target="tpu_custom_call" | custom-call | tf_op jit(solution)/shard_map/route/pallas_call | solution.py:253
  39.8 0.7 %collective-permute-start.15 = (f32[128,512]{1,0:T(8,128)S(1)}, f32[128,512]{1,0:T(8,128)S(1)}, u32[]{:S(2)}, u32[]{:S(2)}) collective-permute-start(f32[128,512]{1,0:T(8,128)S(1)} %get-tuple-element.24), channel_id=1, source_target_pairs={{0,0},{1,2},{2,4},{3,6},{4,1},{5,3},{6,5},{7,7},{8,8},{9,10},{10,1... | collective-permute-start | bytes 786440 | tf_op jit(solution)/shard_map/ppermute | solution.py:393
  40.5 4.1 %collective-permute-start.16 = (f32[128,512]{1,0:T(8,128)S(1)}, f32[128,512]{1,0:T(8,128)S(1)}, u32[]{:S(2)}, u32[]{:S(2)}) collective-permute-start(f32[128,512]{1,0:T(8,128)S(1)} %get-tuple-element.25), channel_id=1, source_target_pairs={{0,4},{1,6},{2,0},{3,2},{4,5},{5,7},{6,1},{7,3},{8,12},{9,14},{10,... | collective-permute-start | bytes 786440 | tf_op jit(solution)/shard_map/ppermute | solution.py:393
  44.5 0.0 copy-start.4
  44.5 8.7 %shard_map.86.refs_2_ = f32[256,512]{1,0:T(8,128)S(1)} custom-call(s32[5]{0:T(128)S(1)} %stack.23.place_ref, f32[8,128]{1,0:T(8,128)S(1)} %get-tuple-element.21.refs_0_, f32[256,256]{1,0:T(8,128)S(1)} %get-tuple-element.22.refs_1_, f32[256,256]{1,0:T(8,128)S(1)} %get-tuple-element.23.refs_2_), custom_call_target="tpu_custom_call" | custom-call | flops 10000000000 | bytes 524288 | tf_op jit(solution)/shard_map/pallas_call | solution.py:191
  53.2 0.0 collective-permute-done.10.refs_4_
  53.2 0.0 collective-permute-done.12.refs_10_
  53.2 0.0 collective-permute-done.14.refs_12_
  53.3 0.0 collective-permute-done.15.refs_13_
  53.3 0.0 collective-permute-done.16.refs_14_
  53.3 0.0 copy-done.4
  53.3 6.3 %update.1 = (f32[128,512]{1,0:T(8,128)}, f32[32,512]{1,0:T(8,128)}, f32[32,512]{1,0:T(8,128)}, f32[256,128]{1,0:T(8,128)}) custom-call(s32[5]{0:T(128)S(1)} %stack.23.place_ref, f32[128,128]{1,0:T(8,128)S(1)} %get-tuple-element.15.refs_0_, f32[128,256]{1,0:T(8,128)S(1)} %get-tuple-element.19.refs_1_, f32[256,512]{1,0:T(8,128)S(1)} %shard_map.86.refs_2_, ...), custom_call_target="tpu_custom_call" | custom-call | flops 10000000000 | bytes 2097152 | tf_op jit(solution)/shard_map/update/pallas_call | solution.py:358
Async XLA Ops:
  0.6 13.8 %collective-permute-start = (f32[128,512]{1,0:T(8,128)}, f32[128,512]{1,0:T(8,128)S(1)}, u32[]{:S(2)}, u32[]{:S(2)}) collective-permute-start(f32[128,512]{1,0:T(8,128)} %refs_0_.1), channel_id=1, source_target_pairs={{0,24},{2,26},{4,28},{6,30},{8,16},{10,18},{12,20},{14,22},{16,8},... | collective-permute-start | bytes 786440 | tf_op jit(solution)/shard_map/ppermute | solution.py:393
  6.5 9.6 %collective-permute-start.2 = (f32[128,512]{1,0:T(8,128)}, f32[128,512]{1,0:T(8,128)S(1)}, u32[]{:S(2)}, u32[]{:S(2)}) collective-permute-start(f32[128,512]{1,0:T(8,128)} %refs_0_.1), channel_id=1, source_target_pairs={{0,8},{1,17},{2,10},{3,19},{4,12},{5,21},{6,14},{7,23},{8,0},{9,25... | collective-permute-start | bytes 786440 | tf_op jit(solution)/shard_map/ppermute | solution.py:393
  7.1 10.1 %collective-permute-start.11 = (f32[128,512]{1,0:T(8,128)}, f32[128,512]{1,0:T(8,128)S(1)}, u32[]{:S(2)}, u32[]{:S(2)}) collective-permute-start(f32[128,512]{1,0:T(8,128)} %refs_3_.1), channel_id=1, source_target_pairs={{0,8},{1,17},{2,10},{3,19},{4,12},{5,21},{6,14},{7,23},{8,0},{9,25... | collective-permute-start | bytes 786440 | tf_op jit(solution)/shard_map/ppermute | solution.py:393
  8.6 1.5 %collective-permute-start.4 = (f32[32,512]{1,0:T(8,128)}, f32[32,512]{1,0:T(8,128)S(1)}, u32[]{:S(2)}, u32[]{:S(2)}) collective-permute-start(f32[32,512]{1,0:T(8,128)} %b_own.1), channel_id=1, source_target_pairs={{0,1},{1,0},{2,3},{3,2},{4,5},{5,4},{6,7},{7,6},{8,9},{9,8},{10,11... | collective-permute-start | bytes 196616 | tf_op jit(solution)/shard_map/ppermute | solution.py:393
  8.6 1.6 %collective-permute-start.5 = (f32[32,512]{1,0:T(8,128)}, f32[32,512]{1,0:T(8,128)S(1)}, u32[]{:S(2)}, u32[]{:S(2)}) collective-permute-start(f32[32,512]{1,0:T(8,128)} %a_own.1), channel_id=1, source_target_pairs={{0,1},{1,0},{2,3},{3,2},{4,5},{5,4},{6,7},{7,6},{8,9},{9,8},{10,11... | collective-permute-start | bytes 196616 | tf_op jit(solution)/shard_map/ppermute | solution.py:393
  10.2 0.8 %copy-start = (f32[32,512]{1,0:T(8,128)S(1)}, f32[32,512]{1,0:T(8,128)}, u32[]{:S(2)}) copy-start(f32[32,512]{1,0:T(8,128)} %b_own.1) | copy-start | bytes 196612
  11.0 0.8 %copy-start.1 = (f32[32,512]{1,0:T(8,128)S(1)}, f32[32,512]{1,0:T(8,128)}, u32[]{:S(2)}) copy-start(f32[32,512]{1,0:T(8,128)} %a_own.1) | copy-start | bytes 196612
  11.9 8.0 %copy-start.3 = (f32[128,512]{1,0:T(8,128)S(1)}, f32[128,512]{1,0:T(8,128)}, u32[]{:S(2)}) copy-start(f32[128,512]{1,0:T(8,128)} %refs_3_.1) | copy-start | bytes 786436
  11.9 16.5 %copy-start.2 = (f32[128,512]{1,0:T(8,128)S(1)}, f32[128,512]{1,0:T(8,128)}, u32[]{:S(2)}) copy-start(f32[128,512]{1,0:T(8,128)} %refs_0_.1) | copy-start | bytes 786436
  12.4 7.4 %collective-permute-start.6 = (f32[128,512]{1,0:T(8,128)S(1)}, f32[128,512]{1,0:T(8,128)S(1)}, u32[]{:S(2)}, u32[]{:S(2)}) collective-permute-start(f32[128,512]{1,0:T(8,128)S(1)} %join.1.own.refs_5_), channel_id=1, source_target_pairs={{0,24},{1,7},{2,26},{3,5},{4,28},{5,3},{6,30},{7,1},{8,16},{9,15},... | collective-permute-start | bytes 786440 | tf_op jit(solution)/shard_map/ppermute | solution.py:393
  12.5 10.3 %collective-permute-start.8 = (f32[128,512]{1,0:T(8,128)S(1)}, f32[128,512]{1,0:T(8,128)S(1)}, u32[]{:S(2)}, u32[]{:S(2)}) collective-permute-start(f32[128,512]{1,0:T(8,128)S(1)} %join.1.own.refs_5_), channel_id=1, source_target_pairs={{0,8},{1,17},{2,10},{3,19},{4,12},{5,21},{6,14},{7,23},{8,0},{9,25... | collective-permute-start | bytes 786440 | tf_op jit(solution)/shard_map/ppermute | solution.py:393
  14.5 8.6 %collective-permute-start.13 = (f32[128,512]{1,0:T(8,128)S(1)}, f32[128,512]{1,0:T(8,128)S(1)}, u32[]{:S(2)}, u32[]{:S(2)}) collective-permute-start(f32[128,512]{1,0:T(8,128)S(1)} %join.1.own.refs_5_), channel_id=1, source_target_pairs={{0,2},{1,5},{2,0},{3,7},{4,6},{5,1},{6,4},{7,3},{8,10},{9,13},{10,... | collective-permute-start | bytes 786440 | tf_op jit(solution)/shard_map/ppermute | solution.py:393
  16.1 11.8 %collective-permute-start.1 = (f32[128,512]{1,0:T(8,128)S(1)}, f32[128,512]{1,0:T(8,128)S(1)}, u32[]{:S(2)}, u32[]{:S(2)}) collective-permute-start(f32[128,512]{1,0:T(8,128)S(1)} %collective-permute-done.refs_1_), channel_id=1, source_target_pairs={{0,1},{1,0},{2,3},{3,2},{4,5},{5,4},{6,7},{7,6},{8,9},{9,8},{10,11... | collective-permute-start | bytes 786440 | tf_op jit(solution)/shard_map/ppermute | solution.py:393
  17.2 10.6 %collective-permute-start.3 = (f32[128,512]{1,0:T(8,128)S(1)}, f32[128,512]{1,0:T(8,128)S(1)}, u32[]{:S(2)}, u32[]{:S(2)}) collective-permute-start(f32[128,512]{1,0:T(8,128)S(1)} %collective-permute-done.2.refs_3_), channel_id=1, source_target_pairs={{0,1},{1,0},{2,3},{3,2},{4,5},{5,4},{6,7},{7,6},{8,9},{9,8},{10,11... | collective-permute-start | bytes 786440 | tf_op jit(solution)/shard_map/ppermute | solution.py:393
  19.9 33.4 %collective-permute-start.10 = (f32[128,512]{1,0:T(8,128)S(1)}, f32[128,512]{1,0:T(8,128)S(1)}, u32[]{:S(2)}, u32[]{:S(2)}) collective-permute-start(f32[128,512]{1,0:T(8,128)S(1)} %copy-done.3), channel_id=1, source_target_pairs={{0,24},{1,25},{2,26},{3,27},{4,28},{5,29},{6,30},{7,31},{8,16},{9,... | collective-permute-start | bytes 786440 | tf_op jit(solution)/shard_map/ppermute | solution.py:393
  22.9 30.4 %collective-permute-start.12 = (f32[128,512]{1,0:T(8,128)S(1)}, f32[128,512]{1,0:T(8,128)S(1)}, u32[]{:S(2)}, u32[]{:S(2)}) collective-permute-start(f32[128,512]{1,0:T(8,128)S(1)} %collective-permute-done.11.refs_9_), channel_id=1, source_target_pairs={{0,1},{1,0},{2,3},{3,2},{4,5},{5,4},{6,7},{7,6},{8,9},{9,8},{10,11... | collective-permute-start | bytes 786440 | tf_op jit(solution)/shard_map/ppermute | solution.py:393
  23.0 16.1 %collective-permute-start.7 = (f32[128,512]{1,0:T(8,128)S(1)}, f32[128,512]{1,0:T(8,128)S(1)}, u32[]{:S(2)}, u32[]{:S(2)}) collective-permute-start(f32[128,512]{1,0:T(8,128)S(1)} %collective-permute-done.6.last.refs_6_), channel_id=1, source_target_pairs={{0,1},{1,0},{2,3},{3,2},{4,5},{5,4},{6,7},{7,6},{8,9},{9,8},{10,11... | collective-permute-start | bytes 786440 | tf_op jit(solution)/shard_map/ppermute | solution.py:393
  27.8 11.3 %collective-permute-start.9 = (f32[128,512]{1,0:T(8,128)S(1)}, f32[128,512]{1,0:T(8,128)S(1)}, u32[]{:S(2)}, u32[]{:S(2)}) collective-permute-start(f32[128,512]{1,0:T(8,128)S(1)} %collective-permute-done.8.refs_0_), channel_id=1, source_target_pairs={{0,1},{1,0},{2,3},{3,2},{4,5},{5,4},{6,7},{7,6},{8,9},{9,8},{10,11... | collective-permute-start | bytes 786440 | tf_op jit(solution)/shard_map/ppermute | solution.py:393
  27.8 25.4 %collective-permute-start.14 = (f32[128,512]{1,0:T(8,128)S(1)}, f32[128,512]{1,0:T(8,128)S(1)}, u32[]{:S(2)}, u32[]{:S(2)}) collective-permute-start(f32[128,512]{1,0:T(8,128)S(1)} %collective-permute-done.13.refs_11_), channel_id=1, source_target_pairs={{0,1},{1,0},{2,3},{3,2},{4,5},{5,4},{6,7},{7,6},{8,9},{9,8},{10,11... | collective-permute-start | bytes 786440 | tf_op jit(solution)/shard_map/ppermute | solution.py:393
  39.8 13.5 %collective-permute-start.15 = (f32[128,512]{1,0:T(8,128)S(1)}, f32[128,512]{1,0:T(8,128)S(1)}, u32[]{:S(2)}, u32[]{:S(2)}) collective-permute-start(f32[128,512]{1,0:T(8,128)S(1)} %get-tuple-element.24), channel_id=1, source_target_pairs={{0,0},{1,2},{2,4},{3,6},{4,1},{5,3},{6,5},{7,7},{8,8},{9,10},{10,1... | collective-permute-start | bytes 786440 | tf_op jit(solution)/shard_map/ppermute | solution.py:393
  40.5 12.8 %collective-permute-start.16 = (f32[128,512]{1,0:T(8,128)S(1)}, f32[128,512]{1,0:T(8,128)S(1)}, u32[]{:S(2)}, u32[]{:S(2)}) collective-permute-start(f32[128,512]{1,0:T(8,128)S(1)} %get-tuple-element.25), channel_id=1, source_target_pairs={{0,4},{1,6},{2,0},{3,2},{4,5},{5,7},{6,1},{7,3},{8,12},{9,14},{10,... | collective-permute-start | bytes 786440 | tf_op jit(solution)/shard_map/ppermute | solution.py:393
  44.5 8.7 %copy-start.4 = (f32[256,128]{1,0:T(8,128)S(1)}, f32[256,128]{1,0:T(8,128)}, u32[]{:S(2)}) copy-start(f32[256,128]{1,0:T(8,128)} %refs_8_.1) | copy-start | bytes 393220

commit v4 on v3

--- a/solution.py
+++ b/solution.py
@@ -81,14 +81,18 @@
     return jnp.concatenate([rows[h] * lax.rsqrt(pivots[h]) for h in range(groups)], axis=0)
 
 
-def invert_block(block, columns):
+def invert_block(block, columns, others=()):
     size = block.shape[0]
     done = []
     total = None
     for b in range(size // SMALL):
         offset = b * SMALL
         below = offset + SMALL
-        small = invert_small(block[offset:below, :], offset, columns)
+        mine = block[offset:below, :]
+        if 0 < b <= len(others):
+            nothing = jnp.minimum(jnp.abs(others[b - 1]()), 0.0)
+            mine = mine + jnp.concatenate([nothing] * (SMALL // 8), axis=0)
+        small = invert_small(mine, offset, columns)
         last = below == size
         if not last:
             low = nt(block[below:, :], small)
@@ -102,31 +106,56 @@
     return jnp.concatenate(done, axis=0)
 
 
-def factor_steps(work, sums, columns, out_ref, base, first, last, count):
-    start = first * BLOCK
+def factor_steps(work, sums, columns, out_ref, base, pending, first, last, total):
+    def at(i, j=None):
+        return slice(i * BLOCK - base, (i + 1 if j is None else j) * BLOCK - base)
+
+    def finish(k, inverse):
+        spot = slice((k - 1) * BLOCK, k * BLOCK)
+        lead = -nn(inverse, sums[at(k), : k * BLOCK])
+        out_ref[spot, : k * BLOCK] = lead
+        out_ref[spot, k * BLOCK : (k + 1) * BLOCK] = inverse
+        if k + 1 < total:
+            out_ref[spot, (k + 1) * BLOCK :] = jnp.zeros((BLOCK, (total - k - 1) * BLOCK), jnp.float32)
+        return jnp.concatenate([lead, inverse], axis=1)
+
     for k in range(first, last):
-        lo, hi = k * BLOCK, (k + 1) * BLOCK
-        here = slice(lo - base, hi - base)
-        rows = slice(lo - start, hi - start)
-        inverse = invert_block(work[here, here], columns)
-        out_ref[rows, lo:hi] = inverse
-        if k + 1 < count:
-            below = slice(hi - base, count * BLOCK - base)
-            low = nt(work[below, here], inverse)
-            for i in range(k + 1, count):
-                part = slice(i * BLOCK - base, (i + 1) * BLOCK - base)
-                wide = slice(hi - base, (i + 1) * BLOCK - base)
-                mine = low[i * BLOCK - hi : (i + 1) * BLOCK - hi]
-                work[part, wide] = work[part, wide] - nt(mine, low[: (i + 1) * BLOCK - hi])
+        p = k - 1
+        block = work[at(k), at(k)]
+        others = []
         if k > 0:
-            out_ref[rows, :lo] = -nn(inverse, sums[here, :lo])
-        if k + 1 < count:
-            update = nn(low, out_ref[rows, :hi])
-            if k > 0:
-                sums[below, :lo] = sums[below, :lo] + update[:, :lo]
-            sums[below, lo:hi] = update[:, lo:hi]
-        if hi < out_ref.shape[1]:
-            out_ref[rows, hi:] = jnp.zeros((BLOCK, out_ref.shape[1] - hi), jnp.float32)
+            near = nt(work[at(k), at(p)], pending)
+            block = block - nt(near, near)
+            held = {}
+
+            def lower(p=p, k=k, held=held, near=near, pending=pending):
+                held["strip"] = pending if p == 0 else finish(p, pending)
+                held["lows"] = [near] + [nt(work[at(i), at(p)], pending) for i in range(k + 1, total)]
+                return held["lows"][-1][:8, :] + held["strip"][:8, :BLOCK]
+
+            def trail(k=k, held=held):
+                lows = held["lows"]
+                tile = jnp.zeros((8, BLOCK), jnp.float32)
+                for i in range(k + 1, total):
+                    wide = at(k, i + 1)
+                    value = work[at(i), wide] - nt(lows[i - k], jnp.concatenate(lows[: i - k + 1], axis=0))
+                    work[at(i), wide] = value
+                    tile = tile + value[:8, :BLOCK]
+                return tile
+
+            def total_up(p=p, k=k, held=held):
+                update = nn(jnp.concatenate(held["lows"], axis=0), held["strip"])
+                below = at(k, total)
+                if p > 0:
+                    sums[below, : p * BLOCK] = sums[below, : p * BLOCK] + update[:, : p * BLOCK]
+                sums[below, p * BLOCK : k * BLOCK] = update[:, p * BLOCK :]
+                return update[:8, :BLOCK]
+
+            others = [lower, trail, total_up]
+        pending = invert_block(block, columns, others)
+    if last == total:
+        finish(last - 1, pending)
+    return pending
 
 
 def gather_square(work, core, me, count, own, ops, swapped, last, last_swapped):
@@ -153,43 +182,47 @@
         place(me ^ (count - 1), last_swapped)
 
 
-def step_kernel(count, first, last, place_ref, *refs):
+def step_kernel(count, first, last, total, place_ref, *refs):
+    work, sums, columns = refs[-3:]
     if first == 0:
         own, final, final_swapped = refs[:3]
         extra = count // 2 - 1
         ops, swapped = refs[3 : 3 + extra], refs[3 + extra : 3 + 2 * extra]
-        refs = refs[3 + 2 * extra :]
+        outs = refs[3 + 2 * extra : -3]
+        gather_square(work, place_ref[1], place_ref[0], count, own, ops, swapped, final, final_swapped)
+        pending, base = None, 0
     else:
-        _, work_in, sums_in = refs[:3]
-        refs = refs[3:]
-    inverse_out, work, sums, columns = refs[0], refs[-3], refs[-2], refs[-1]
-    total, size = inverse_out.shape[1] // BLOCK, work.shape[0]
-    if first == 0:
-        gather_square(work, place_ref[1], place_ref[0], count, own, ops, swapped, final, final_swapped)
-        total = size // BLOCK
-    else:
-        work[...] = work_in[...]
-        sums[:, : first * BLOCK] = sums_in[...]
-        total = first + size // BLOCK
-    factor_steps(work, sums, columns, inverse_out, first * BLOCK, first, last, total)
+        _, pending_in, work_in = refs[:3]
+        outs = refs[3:-3]
+        base = (first - 1) * BLOCK
+        work[BLOCK:, :] = work_in[...]
+        if base:
+            sums[:, :base] = outs[0][...]
+            outs = outs[1:]
+        pending = pending_in[...]
+    pending = factor_steps(work, sums, columns, outs[0], base, pending, first, last, total)
     if last < total:
-        work_out, sums_out, token_out = refs[1:4]
-        cut = (last - first) * BLOCK
-        work_out[...] = work[cut:, cut:]
-        sums_out[...] = sums[cut:, : last * BLOCK]
+        pending_out, work_out, token_out = outs[:3]
+        pending_out[...] = pending
+        cut = last * BLOCK - base
+        work_out[...] = work[cut:, cut - BLOCK :]
         token_out[...] = jnp.zeros_like(token_out)
+        if last > 1:
+            outs[3][...] = sums[cut - BLOCK :, : (last - 1) * BLOCK]
 
 
 def factor_part(places, operands, count, first, last, total):
     shape = jax.ShapeDtypeStruct
-    size = (total - first) * BLOCK
+    size = (total - max(first - 1, 0)) * BLOCK
     rest = (total - last) * BLOCK
-    made = last * BLOCK
-    outs = [shape(((last - first) * BLOCK, made), jnp.float32)]
     if rest:
-        outs += [shape((rest, rest), jnp.float32), shape((rest, made), jnp.float32), TOKEN]
+        outs = [shape((BLOCK, BLOCK), jnp.float32), shape((rest, rest + BLOCK), jnp.float32), TOKEN]
+        if last > 1:
+            outs.append(shape((rest + BLOCK, (last - 1) * BLOCK), jnp.float32))
+    else:
+        outs = [shape(((total - 1) * BLOCK, total * BLOCK), jnp.float32)]
     return pl.pallas_call(
-        functools.partial(step_kernel, count, first, last),
+        functools.partial(step_kernel, count, first, last, total),
         out_shape=tuple(outs),
         in_specs=[SMEM] + [VMEM] * len(operands),
         out_specs=(VMEM,) * len(outs),
@@ -287,68 +320,80 @@
         groups.append(refs[:n])
         refs = refs[n:]
     diag_ops, diag_swapped, row_ops, row_swapped, pieces = groups
-    diag_out, low_out, panel_out, trail_out, upper_work, diag_work, rows_work, cols_work = refs
+    diag_out, low_out, panel_out, trail_out, upper_work, diag_work, work = refs
     row, core, chip, place = place_ref[0], place_ref[1], place_ref[2], place_ref[4]
     height, _ = diag.shape
     rows = panel.shape[0] // 4
     gather_square(diag_work, core, row, count, diag, diag_ops, diag_swapped, square, None)
 
-    def store(work, spot, piece):
+    wide = trail_ref.shape[0]
+
+    def store(start, spot, piece):
         for c in range(2):
             for which in range(2):
                 part = slice((2 * c + which) * rows, (2 * c + which + 1) * rows)
-                work[which, pl.ds(pl.multiple_of((2 * spot + c) * rows, 8), rows), :] = piece[part]
-
-    store(rows_work, chip, panel)
+                work[which, pl.ds(pl.multiple_of(start + (2 * spot + c) * rows, 8), rows), :] = piece[part]
+
+    store(0, chip, panel)
     for j in range(more):
-        store(rows_work, chip ^ (2 * j + 1 + core), row_ops[j])
-        store(rows_work, chip ^ (2 * j + 2 - core), row_swapped[j])
+        store(0, chip ^ (2 * j + 1 + core), row_ops[j])
+        store(0, chip ^ (2 * j + 2 - core), row_swapped[j])
 
     @pl.when(core == 1)
     def _():
-        store(rows_work, chip ^ (chips - 1), final)
+        store(0, chip ^ (chips - 1), final)
 
     @pl.when(core != 1)
     def _():
-        store(rows_work, chip ^ (chips - 1), final_swapped)
+        store(0, chip ^ (chips - 1), final_swapped)
 
     for t in range(pairs):
-        store(cols_work, lax.rem(chip - 2 * t + chips, chips) // 2, pieces[t])
+        store(wide, lax.rem(chip - 2 * t + chips, chips) // 2, pieces[t])
     cut = upper_work.shape[0]
-    at = 0
-    for part in inverses[:-1]:
-        tall, wide = part.shape
-        upper_work[at : at + tall, :wide] = part[...]
-        if wide < cut:
-            upper_work[at : at + tall, wide:] = jnp.zeros((tall, cut - wide), jnp.float32)
-        at += tall
-    upper, lower = split(upper_work[...]), split(inverses[-1][...])
+    start, rest = inverses
+    tall = start.shape[0]
+    upper_work[:tall, :tall] = start[...]
+    upper_work[:tall, tall:] = jnp.zeros((tall, cut - tall), jnp.float32)
+    upper_work[tall:, :] = rest[: cut - tall, :cut]
+    upper, lower = split(upper_work[...]), split(rest[cut - tall :, :])
+
+    def halves(value, other, dims):
+        cutoff = value[0].shape[0] // 32 * 16
+        return jnp.concatenate(
+            [product([part[:cutoff] for part in value], other, dims), product([part[cutoff:] for part in value], other, dims)], axis=0
+        )
 
     def back(value):
         parts = split(value)
-        first = product([part[:, :cut] for part in parts], upper, NT)
-        return jnp.concatenate([first, product(parts, lower, NT)], axis=1)
+        first = halves([part[:, :cut] for part in parts], upper, NT)
+        return jnp.concatenate([first, halves(parts, lower, NT)], axis=1)
 
     diag = split(diag_work[...])
-    left = jnp.concatenate([product(upper, [part[:cut] for part in diag], NN), product(lower, diag, NN)], axis=0)
+    left = jnp.concatenate(
+        [halves(upper, [part[:cut] for part in diag], NN), halves(lower, diag, NN)], axis=0
+    )
     diag_work[...] = left
-    left = split(left)
-
-    def panel(work):
-        low = back(work[0])
-        change = product(split(low), left, NN)
-        start = work[1]
-        work[0] = low
-        work[1] = start - change
-        return split(low), split(back(start - 0.5 * change))
-
-    low_rows, mixed_rows = panel(rows_work)
-    low_cols, mixed_cols = panel(cols_work)
-    trail_out[...] = trail_ref[...] - (product(mixed_rows, low_cols, NT) + product(low_rows, mixed_cols, NT))
-    diag_out[...] = back(diag_work[pl.ds(pl.multiple_of(row * height, 8), height), :])
+    low = back(work[0])
+    work[0] = low
+    low = split(low)
+    change = halves(low, split(left), NN)
+    start = work[1]
+    work[1] = start - change
     mine = pl.ds(pl.multiple_of(place * rows, 8), rows)
-    low_out[...] = rows_work[0, mine, :]
-    panel_out[...] = back(rows_work[1, mine, :])
+    last = back(
+        jnp.concatenate(
+            [start - 0.5 * change, work[1, mine, :], diag_work[pl.ds(pl.multiple_of(row * height, 8), height), :]], axis=0
+        )
+    )
+    tall = start.shape[0]
+    mixed = split(last[:tall])
+    trail_out[...] = trail_ref[...] - (
+        halves([part[:wide] for part in mixed], [part[wide:] for part in low], NT)
+        + halves([part[:wide] for part in low], [part[wide:] for part in mixed], NT)
+    )
+    low_out[...] = work[0, mine, :]
+    panel_out[...] = last[tall : tall + rows]
+    diag_out[...] = last[tall + rows :]
 
 
 def update(places, inverses, singles, groups, count, chips, shapes):
@@ -361,10 +406,9 @@
         in_specs=[SMEM] + [VMEM] * len(operands),
         out_specs=(VMEM,) * 4,
         scratch_shapes=[
-            pltpu.VMEM((size - inverses[-1].shape[0],) * 2, jnp.float32),
+            pltpu.VMEM((size // 2, size // 2), jnp.float32),
             pltpu.VMEM((size, size), jnp.float32),
-            pltpu.VMEM((2, height, size), jnp.float32),
-            pltpu.VMEM((2, width, size), jnp.float32),
+            pltpu.VMEM((2, height + width, size), jnp.float32),
         ],
         cost_estimate=pl.CostEstimate(flops=10**10, bytes_accessed=8 * size * size, transcendentals=0),
         compiler_params=memory(3 * size * size + 4 * height * size + 4 * width * size + 2 * height * width),
@@ -416,13 +460,14 @@
     a_ops = [to_rows(a_diag, j) for j in extra]
     a_last = exchange(a_diag, lambda r, z, c: (r ^ (count - 1), z, c))
     total = size // BLOCK
-    cuts = (0, total // 4, total // 2, total)
-    top, work, sums, token = factor_part(
+    cuts = (0, 1, 2, total)
+    assert total > 2
+    top, work, token = factor_part(
         places, [b_diag, square, square_swapped, *b_ops, *b_swapped], count, cuts[0], cuts[1], total
     )
     p_swapped = [swap(x) for x in p_ops]
     final_swapped = swap(final)
-    middle, work, sums, token = factor_part(places, [token, work, sums], count, cuts[1], cuts[2], total)
+    middle, work, token, sums = factor_part(places, [token, top, work], count, cuts[1], cuts[2], total)
     sends, token = route(places, token, panel, final, final_swapped, p_ops, p_swapped, count, chips)
     pieces = [
         exchange(
@@ -432,11 +477,11 @@
     ]
     z_swapped = [swap(x) for x in z_ops]
     a_swapped = [swap(x) for x in a_ops]
-    (bottom,) = factor_part(places, [token, work, sums], count, cuts[2], cuts[3], total)
+    (bottom,) = factor_part(places, [token, middle, work, sums], count, cuts[2], cuts[3], total)
     shapes = (a_diag.shape, b_panel.shape, a_panel.shape, a_trail.shape)
     singles = (a_diag, a_last, panel, final, final_swapped, a_trail)
     groups = (a_ops, a_swapped, z_ops, z_swapped, pieces)
-    return update(places, (top, middle, bottom), singles, groups, count, chips, shapes)
+    return update(places, (top, bottom), singles, groups, count, chips, shapes)
 
 
 def solution(mesh):

time: 60.6 us -> 59.6 us (0.983)
  the two profiles are of different devices: /device:TPU:0 before, /device:TPU:1 now
where the time goes in v4:
time: 59.6 us; the launch traced here: 59.4 us
  Pallas kernels  25.8 us (43%)
  starting transfers between devices  21.5 us (36%)
  waiting for transfers between devices  9.6 us (16%)
  local copies, waits for them, and re-layouts  1.77 us (3%)
  between operations  0.72 us (1%)
    ppermute x17, starting transfers between devices, exchange(): return lax.ppermute(array, ('row', 'chip', 'core'), pairs)  21.5 us
    pallas_call x3, Pallas kernels, factor_part(): pl.pallas_call(functools.partial(step_kernel, count, first, last, total),...  19.7 us
    ppermute x17, waiting for transfers between devices, exchange(): return lax.ppermute(array, ('row', 'chip', 'core'), pairs)  9.6 us
    pallas_call x1, Pallas kernels, update(): pl.pallas_call(functools.partial(update_kernel, count, chips, len(inverse...  4.83 us
    unnamed x10, local copies, waits for them, and re-layouts  1.69 us
  transfers between devices with their start and end apart: 17, of which 6 were waited for; matrix products, arithmetic and copies ran while one was open for 0% of the time, Pallas kernels for 35%

profile of v4, /device:TPU:1, one launch (start us, length us, event | category | flops | bytes accessed | tf_op | source)
XLA Modules:
  0.0 59.4 jit_solution(17615994789894699756)
XLA Ops:
  0.6 0.7 %collective-permute-start = (f32[128,512]{1,0:T(8,128)}, f32[128,512]{1,0:T(8,128)S(1)}, u32[]{:S(2)}, u32[]{:S(2)}) collective-permute-start(f32[128,512]{1,0:T(8,128)} %refs_0_.1), channel_id=1, source_target_pairs={{0,24},{2,26},{4,28},{6,30},{8,16},{10,18},{12,20},{14,22},{16,8},... | collective-permute-start | bytes 786440 | tf_op jit(solution)/shard_map/ppermute | solution.py:437
  1.3 2.1 %collective-permute-start.2 = (f32[128,512]{1,0:T(8,128)}, f32[128,512]{1,0:T(8,128)S(1)}, u32[]{:S(2)}, u32[]{:S(2)}) collective-permute-start(f32[128,512]{1,0:T(8,128)} %refs_0_.1), channel_id=1, source_target_pairs={{0,8},{1,17},{2,10},{3,19},{4,12},{5,21},{6,14},{7,23},{8,0},{9,25... | collective-permute-start | bytes 786440 | tf_op jit(solution)/shard_map/ppermute | solution.py:437
  3.4 0.1 collective-permute-start.11
  3.5 5.1 %collective-permute-start.4 = (f32[32,512]{1,0:T(8,128)}, f32[32,512]{1,0:T(8,128)S(1)}, u32[]{:S(2)}, u32[]{:S(2)}) collective-permute-start(f32[32,512]{1,0:T(8,128)} %b_own.1), channel_id=1, source_target_pairs={{0,1},{1,0},{2,3},{3,2},{4,5},{5,4},{6,7},{7,6},{8,9},{9,8},{10,11... | collective-permute-start | bytes 196616 | tf_op jit(solution)/shard_map/ppermute | solution.py:437
  8.6 0.0 collective-permute-start.5
  8.6 0.1 stack.23.place_ref
  8.7 1.0 %collective-permute-done.4.b_other = f32[32,512]{1,0:T(8,128)S(1)} collective-permute-done((f32[32,512]{1,0:T(8,128)}, f32[32,512]{1,0:T(8,128)S(1)}, u32[]{:S(2)}, u32[]{:S(2)}) %collective-permute-start.4) | collective-permute-done | bytes 65568 | tf_op jit(solution)/shard_map/ppermute | solution.py:437
  9.7 0.4 collective-permute-done.5.a_other
  10.0 0.0 copy-start
  10.0 0.8 %copy-done = f32[32,512]{1,0:T(8,128)S(1)} copy-done((f32[32,512]{1,0:T(8,128)S(1)}, f32[32,512]{1,0:T(8,128)}, u32[]{:S(2)}) %copy-start) | copy-done | bytes 65560
  10.9 0.0 copy-start.1
  10.9 0.8 %copy-done.1 = f32[32,512]{1,0:T(8,128)S(1)} copy-done((f32[32,512]{1,0:T(8,128)S(1)}, f32[32,512]{1,0:T(8,128)}, u32[]{:S(2)}) %copy-start.1) | copy-done | bytes 65560
  11.7 0.0 copy-start.3
  11.7 0.0 copy-start.2
  11.7 0.6 join.1.own.refs_4_
  12.3 2.4 %collective-permute-start.13 = (f32[128,512]{1,0:T(8,128)S(1)}, f32[128,512]{1,0:T(8,128)S(1)}, u32[]{:S(2)}, u32[]{:S(2)}) collective-permute-start(f32[128,512]{1,0:T(8,128)S(1)} %join.1.own.refs_4_), channel_id=1, source_target_pairs={{0,2},{1,5},{2,0},{3,7},{4,6},{5,1},{6,4},{7,3},{8,10},{9,13},{10,... | collective-permute-start | bytes 786440 | tf_op jit(solution)/shard_map/ppermute | solution.py:437
  14.7 0.2 collective-permute-start.8
  14.9 0.0 collective-permute-done.refs_1_
  14.9 1.1 %collective-permute-start.6 = (f32[128,512]{1,0:T(8,128)S(1)}, f32[128,512]{1,0:T(8,128)S(1)}, u32[]{:S(2)}, u32[]{:S(2)}) collective-permute-start(f32[128,512]{1,0:T(8,128)S(1)} %join.1.own.refs_4_), channel_id=1, source_target_pairs={{0,24},{1,7},{2,26},{3,5},{4,28},{5,3},{6,30},{7,1},{8,16},{9,15},... | collective-permute-start | bytes 786440 | tf_op jit(solution)/shard_map/ppermute | solution.py:437
  16.0 0.0 collective-permute-done.2.refs_3_
  16.0 0.1 collective-permute-start.1
  16.1 0.0 collective-permute-done.11.refs_8_
  16.1 1.1 %collective-permute-start.3 = (f32[128,512]{1,0:T(8,128)S(1)}, f32[128,512]{1,0:T(8,128)S(1)}, u32[]{:S(2)}, u32[]{:S(2)}) collective-permute-start(f32[128,512]{1,0:T(8,128)S(1)} %collective-permute-done.2.refs_3_), channel_id=1, source_target_pairs={{0,1},{1,0},{2,3},{3,2},{4,5},{5,4},{6,7},{7,6},{8,9},{9,8},{10,11... | collective-permute-start | bytes 786440 | tf_op jit(solution)/shard_map/ppermute | solution.py:437
  17.2 4.2 %collective-permute-done.13.refs_10_ = f32[128,512]{1,0:T(8,128)S(1)} collective-permute-done((f32[128,512]{1,0:T(8,128)S(1)}, f32[128,512]{1,0:T(8,128)S(1)}, u32[]{:S(2)}, u32[]{:S(2)}) %collective-permute-start.13) | collective-permute-done | bytes 262176 | tf_op jit(solution)/shard_map/ppermute | solution.py:437
  21.4 0.0 copy-done.3
  21.4 0.0 collective-permute-start.10
  21.4 1.5 %collective-permute-done.8.refs_0_ = f32[128,512]{1,0:T(8,128)S(1)} collective-permute-done((f32[128,512]{1,0:T(8,128)S(1)}, f32[128,512]{1,0:T(8,128)S(1)}, u32[]{:S(2)}, u32[]{:S(2)}) %collective-permute-start.8) | collective-permute-done | bytes 262176 | tf_op jit(solution)/shard_map/ppermute | solution.py:437
  22.9 0.0 collective-permute-start.12
  22.9 2.2 %collective-permute-done.6.last.refs_5_ = f32[128,512]{1,0:T(8,128)S(1)} collective-permute-done((f32[128,512]{1,0:T(8,128)S(1)}, f32[128,512]{1,0:T(8,128)S(1)}, u32[]{:S(2)}, u32[]{:S(2)}) %collective-permute-start.6) | collective-permute-done | bytes 262176 | tf_op jit(solution)/shard_map/ppermute | solution.py:437
  25.1 0.0 collective-permute-start.14
  25.1 0.0 collective-permute-done.1.refs_2_
  25.1 0.5 collective-permute-start.9
  25.6 0.0 collective-permute-done.3.refs_4_
  25.6 0.1 collective-permute-start.7
  25.7 0.0 copy-done.2
  25.7 4.3 %shard_map.84 = (f32[128,128]{1,0:T(8,128)S(1)}, f32[384,512]{1,0:T(8,128)S(1)}, f32[8,128]{1,0:T(8,128)S(1)}) custom-call(s32[5]{0:T(128)S(1)} %stack.23.place_ref, f32[128,512]{1,0:T(8,128)S(1)} %copy-done.2, f32[128,512]{1,0:T(8,128)S(1)} %collective-permute-done.refs_1_, f32[128,512]{1,0:T(8,128)S(1)} %collective-permute-done.1.refs_2_, ...), custom_call_target="tpu_custom_call" | custom-call | flops 10000000000 | bytes 2097152 | tf_op jit(solution)/shard_map/pallas_call | solution.py:224
  30.0 5.4 %shard_map.85 = (f32[128,128]{1,0:T(8,128)S(1)}, f32[256,384]{1,0:T(8,128)S(1)}, f32[8,128]{1,0:T(8,128)S(1)}, f32[384,128]{1,0:T(8,128)S(1)}) custom-call(s32[5]{0:T(128)S(1)} %stack.23.place_ref, f32[8,128]{1,0:T(8,128)S(1)} %get-tuple-element.15.refs_0_, f32[128,128]{1,0:T(8,128)S(1)} %get-tuple-element.14.refs_1_.refs_0_, ...), custom_call_target="tpu_custom_call" | custom-call | flops 10000000000 | bytes 2097152 | tf_op jit(solution)/shard_map/pallas_call | solution.py:224
  35.3 0.0 collective-permute-done.9.refs_1_
  35.3 0.0 collective-permute-done.7.last_swapped.refs_6_
  35.3 0.7 %route.1 = (f32[128,512]{1,0:T(8,128)S(1)}, f32[128,512]{1,0:T(8,128)S(1)}, f32[8,128]{1,0:T(8,128)S(1)}) custom-call(s32[5]{0:T(128)S(1)} %stack.23.place_ref, f32[8,128]{1,0:T(8,128)S(1)} %get-tuple-element.17._, f32[128,512]{1,0:T(8,128)S(1)} %join.1.own.refs_4_, f32[128,512]{1,0:T(8,128)S(1)} %collective-permute-done.6.last.refs_5_, ...), custom_call_target="tpu_custom_call" | custom-call | tf_op jit(solution)/shard_map/route/pallas_call | solution.py:286
  36.0 4.8 %collective-permute-start.15 = (f32[128,512]{1,0:T(8,128)S(1)}, f32[128,512]{1,0:T(8,128)S(1)}, u32[]{:S(2)}, u32[]{:S(2)}) collective-permute-start(f32[128,512]{1,0:T(8,128)S(1)} %get-tuple-element.22), channel_id=1, source_target_pairs={{0,0},{1,2},{2,4},{3,6},{4,1},{5,3},{6,5},{7,7},{8,8},{9,10},{10,1... | collective-permute-start | bytes 786440 | tf_op jit(solution)/shard_map/ppermute | solution.py:437
  40.8 3.3 %collective-permute-start.16 = (f32[128,512]{1,0:T(8,128)S(1)}, f32[128,512]{1,0:T(8,128)S(1)}, u32[]{:S(2)}, u32[]{:S(2)}) collective-permute-start(f32[128,512]{1,0:T(8,128)S(1)} %get-tuple-element.23), channel_id=1, source_target_pairs={{0,4},{1,6},{2,0},{3,2},{4,5},{5,7},{6,1},{7,3},{8,12},{9,14},{10,... | collective-permute-start | bytes 786440 | tf_op jit(solution)/shard_map/ppermute | solution.py:437
  44.1 0.0 copy-start.4
  44.1 10.1 %shard_map.86.refs_1_ = f32[384,512]{1,0:T(8,128)S(1)} custom-call(s32[5]{0:T(128)S(1)} %stack.23.place_ref, f32[8,128]{1,0:T(8,128)S(1)} %get-tuple-element.18.refs_0_, f32[128,128]{1,0:T(8,128)S(1)} %get-tuple-element.19.refs_1_, f32[256,384]{1,0:T(8,128)S(1)} %get-tuple-element.20.refs_2_, f32[384,128]{1,0:T(8,128)S(1)} %get-tuple-element.21.refs_3_), custom_call_target="tpu_custom_call" | custom-call | flops 10000000000 | bytes 1179648 | tf_op jit(solution)/shard_map/pallas_call | solution.py:224
  54.2 0.0 collective-permute-done.10.refs_3_
  54.2 0.0 collective-permute-done.12.refs_9_
  54.2 0.0 collective-permute-done.14.refs_11_
  54.3 0.3 collective-permute-done.15.refs_12_
  54.5 0.0 collective-permute-done.16.refs_13_
  54.6 0.0 copy-done.4
  54.6 4.8 %update.1 = (f32[128,512]{1,0:T(8,128)}, f32[32,512]{1,0:T(8,128)}, f32[32,512]{1,0:T(8,128)}, f32[256,128]{1,0:T(8,128)}) custom-call(s32[5]{0:T(128)S(1)} %stack.23.place_ref, f32[128,128]{1,0:T(8,128)S(1)} %get-tuple-element.14.refs_1_.refs_0_, f32[384,512]{1,0:T(8,128)S(1)} %shard_map.86.refs_1_, f32[128,512]{1,0:T(8,128)S(1)} %copy-done.3, ...), custom_call_target="tpu_custom_call" | custom-call | flops 10000000000 | bytes 2097152 | tf_op jit(solution)/shard_map/update/pallas_call | solution.py:403
Async XLA Ops:
  0.6 14.3 %collective-permute-start = (f32[128,512]{1,0:T(8,128)}, f32[128,512]{1,0:T(8,128)S(1)}, u32[]{:S(2)}, u32[]{:S(2)}) collective-permute-start(f32[128,512]{1,0:T(8,128)} %refs_0_.1), channel_id=1, source_target_pairs={{0,24},{2,26},{4,28},{6,30},{8,16},{10,18},{12,20},{14,22},{16,8},... | collective-permute-start | bytes 786440 | tf_op jit(solution)/shard_map/ppermute | solution.py:437
  1.3 14.7 %collective-permute-start.2 = (f32[128,512]{1,0:T(8,128)}, f32[128,512]{1,0:T(8,128)S(1)}, u32[]{:S(2)}, u32[]{:S(2)}) collective-permute-start(f32[128,512]{1,0:T(8,128)} %refs_0_.1), channel_id=1, source_target_pairs={{0,8},{1,17},{2,10},{3,19},{4,12},{5,21},{6,14},{7,23},{8,0},{9,25... | collective-permute-start | bytes 786440 | tf_op jit(solution)/shard_map/ppermute | solution.py:437
  3.4 12.6 %collective-permute-start.11 = (f32[128,512]{1,0:T(8,128)}, f32[128,512]{1,0:T(8,128)S(1)}, u32[]{:S(2)}, u32[]{:S(2)}) collective-permute-start(f32[128,512]{1,0:T(8,128)} %refs_2_.1), channel_id=1, source_target_pairs={{0,8},{1,17},{2,10},{3,19},{4,12},{5,21},{6,14},{7,23},{8,0},{9,25... | collective-permute-start | bytes 786440 | tf_op jit(solution)/shard_map/ppermute | solution.py:437
  3.5 6.2 %collective-permute-start.4 = (f32[32,512]{1,0:T(8,128)}, f32[32,512]{1,0:T(8,128)S(1)}, u32[]{:S(2)}, u32[]{:S(2)}) collective-permute-start(f32[32,512]{1,0:T(8,128)} %b_own.1), channel_id=1, source_target_pairs={{0,1},{1,0},{2,3},{3,2},{4,5},{5,4},{6,7},{7,6},{8,9},{9,8},{10,11... | collective-permute-start | bytes 196616 | tf_op jit(solution)/shard_map/ppermute | solution.py:437
  8.6 1.5 %collective-permute-start.5 = (f32[32,512]{1,0:T(8,128)}, f32[32,512]{1,0:T(8,128)S(1)}, u32[]{:S(2)}, u32[]{:S(2)}) collective-permute-start(f32[32,512]{1,0:T(8,128)} %a_own.1), channel_id=1, source_target_pairs={{0,1},{1,0},{2,3},{3,2},{4,5},{5,4},{6,7},{7,6},{8,9},{9,8},{10,11... | collective-permute-start | bytes 196616 | tf_op jit(solution)/shard_map/ppermute | solution.py:437
  10.0 0.8 %copy-start = (f32[32,512]{1,0:T(8,128)S(1)}, f32[32,512]{1,0:T(8,128)}, u32[]{:S(2)}) copy-start(f32[32,512]{1,0:T(8,128)} %b_own.1) | copy-start | bytes 196612
  10.9 0.8 %copy-start.1 = (f32[32,512]{1,0:T(8,128)S(1)}, f32[32,512]{1,0:T(8,128)}, u32[]{:S(2)}) copy-start(f32[32,512]{1,0:T(8,128)} %a_own.1) | copy-start | bytes 196612
  11.7 9.7 %copy-start.3 = (f32[128,512]{1,0:T(8,128)S(1)}, f32[128,512]{1,0:T(8,128)}, u32[]{:S(2)}) copy-start(f32[128,512]{1,0:T(8,128)} %refs_2_.1) | copy-start | bytes 786436
  11.7 14.0 %copy-start.2 = (f32[128,512]{1,0:T(8,128)S(1)}, f32[128,512]{1,0:T(8,128)}, u32[]{:S(2)}) copy-start(f32[128,512]{1,0:T(8,128)} %refs_0_.1) | copy-start | bytes 786436
  12.3 9.1 %collective-permute-start.13 = (f32[128,512]{1,0:T(8,128)S(1)}, f32[128,512]{1,0:T(8,128)S(1)}, u32[]{:S(2)}, u32[]{:S(2)}) collective-permute-start(f32[128,512]{1,0:T(8,128)S(1)} %join.1.own.refs_4_), channel_id=1, source_target_pairs={{0,2},{1,5},{2,0},{3,7},{4,6},{5,1},{6,4},{7,3},{8,10},{9,13},{10,... | collective-permute-start | bytes 786440 | tf_op jit(solution)/shard_map/ppermute | solution.py:437
  14.7 8.2 %collective-permute-start.8 = (f32[128,512]{1,0:T(8,128)S(1)}, f32[128,512]{1,0:T(8,128)S(1)}, u32[]{:S(2)}, u32[]{:S(2)}) collective-permute-start(f32[128,512]{1,0:T(8,128)S(1)} %join.1.own.refs_4_), channel_id=1, source_target_pairs={{0,8},{1,17},{2,10},{3,19},{4,12},{5,21},{6,14},{7,23},{8,0},{9,25... | collective-permute-start | bytes 786440 | tf_op jit(solution)/shard_map/ppermute | solution.py:437
  14.9 10.2 %collective-permute-start.6 = (f32[128,512]{1,0:T(8,128)S(1)}, f32[128,512]{1,0:T(8,128)S(1)}, u32[]{:S(2)}, u32[]{:S(2)}) collective-permute-start(f32[128,512]{1,0:T(8,128)S(1)} %join.1.own.refs_4_), channel_id=1, source_target_pairs={{0,24},{1,7},{2,26},{3,5},{4,28},{5,3},{6,30},{7,1},{8,16},{9,15},... | collective-permute-start | bytes 786440 | tf_op jit(solution)/shard_map/ppermute | solution.py:437
  16.0 9.1 %collective-permute-start.1 = (f32[128,512]{1,0:T(8,128)S(1)}, f32[128,512]{1,0:T(8,128)S(1)}, u32[]{:S(2)}, u32[]{:S(2)}) collective-permute-start(f32[128,512]{1,0:T(8,128)S(1)} %collective-permute-done.refs_1_), channel_id=1, source_target_pairs={{0,1},{1,0},{2,3},{3,2},{4,5},{5,4},{6,7},{7,6},{8,9},{9,8},{10,11... | collective-permute-start | bytes 786440 | tf_op jit(solution)/shard_map/ppermute | solution.py:437
  16.1 9.6 %collective-permute-start.3 = (f32[128,512]{1,0:T(8,128)S(1)}, f32[128,512]{1,0:T(8,128)S(1)}, u32[]{:S(2)}, u32[]{:S(2)}) collective-permute-start(f32[128,512]{1,0:T(8,128)S(1)} %collective-permute-done.2.refs_3_), channel_id=1, source_target_pairs={{0,1},{1,0},{2,3},{3,2},{4,5},{5,4},{6,7},{7,6},{8,9},{9,8},{10,11... | collective-permute-start | bytes 786440 | tf_op jit(solution)/shard_map/ppermute | solution.py:437
  21.4 32.8 %collective-permute-start.10 = (f32[128,512]{1,0:T(8,128)S(1)}, f32[128,512]{1,0:T(8,128)S(1)}, u32[]{:S(2)}, u32[]{:S(2)}) collective-permute-start(f32[128,512]{1,0:T(8,128)S(1)} %copy-done.3), channel_id=1, source_target_pairs={{0,24},{1,25},{2,26},{3,27},{4,28},{5,29},{6,30},{7,31},{8,16},{9,... | collective-permute-start | bytes 786440 | tf_op jit(solution)/shard_map/ppermute | solution.py:437
  22.9 31.4 %collective-permute-start.12 = (f32[128,512]{1,0:T(8,128)S(1)}, f32[128,512]{1,0:T(8,128)S(1)}, u32[]{:S(2)}, u32[]{:S(2)}) collective-permute-start(f32[128,512]{1,0:T(8,128)S(1)} %collective-permute-done.11.refs_8_), channel_id=1, source_target_pairs={{0,1},{1,0},{2,3},{3,2},{4,5},{5,4},{6,7},{7,6},{8,9},{9,8},{10,11... | collective-permute-start | bytes 786440 | tf_op jit(solution)/shard_map/ppermute | solution.py:437
  25.1 29.1 %collective-permute-start.14 = (f32[128,512]{1,0:T(8,128)S(1)}, f32[128,512]{1,0:T(8,128)S(1)}, u32[]{:S(2)}, u32[]{:S(2)}) collective-permute-start(f32[128,512]{1,0:T(8,128)S(1)} %collective-permute-done.13.refs_10_), channel_id=1, source_target_pairs={{0,1},{1,0},{2,3},{3,2},{4,5},{5,4},{6,7},{7,6},{8,9},{9,8},{10,11... | collective-permute-start | bytes 786440 | tf_op jit(solution)/shard_map/ppermute | solution.py:437
  25.1 10.2 %collective-permute-start.9 = (f32[128,512]{1,0:T(8,128)S(1)}, f32[128,512]{1,0:T(8,128)S(1)}, u32[]{:S(2)}, u32[]{:S(2)}) collective-permute-start(f32[128,512]{1,0:T(8,128)S(1)} %collective-permute-done.8.refs_0_), channel_id=1, source_target_pairs={{0,1},{1,0},{2,3},{3,2},{4,5},{5,4},{6,7},{7,6},{8,9},{9,8},{10,11... | collective-permute-start | bytes 786440 | tf_op jit(solution)/shard_map/ppermute | solution.py:437
  25.6 9.7 %collective-permute-start.7 = (f32[128,512]{1,0:T(8,128)S(1)}, f32[128,512]{1,0:T(8,128)S(1)}, u32[]{:S(2)}, u32[]{:S(2)}) collective-permute-start(f32[128,512]{1,0:T(8,128)S(1)} %collective-permute-done.6.last.refs_5_), channel_id=1, source_target_pairs={{0,1},{1,0},{2,3},{3,2},{4,5},{5,4},{6,7},{7,6},{8,9},{9,8},{10,11... | collective-permute-start | bytes 786440 | tf_op jit(solution)/shard_map/ppermute | solution.py:437
  36.0 18.5 %collective-permute-start.15 = (f32[128,512]{1,0:T(8,128)S(1)}, f32[128,512]{1,0:T(8,128)S(1)}, u32[]{:S(2)}, u32[]{:S(2)}) collective-permute-start(f32[128,512]{1,0:T(8,128)S(1)} %get-tuple-element.22), channel_id=1, source_target_pairs={{0,0},{1,2},{2,4},{3,6},{4,1},{5,3},{6,5},{7,7},{8,8},{9,10},{10,1... | collective-permute-start | bytes 786440 | tf_op jit(solution)/shard_map/ppermute | solution.py:437
  40.8 13.8 %collective-permute-start.16 = (f32[128,512]{1,0:T(8,128)S(1)}, f32[128,512]{1,0:T(8,128)S(1)}, u32[]{:S(2)}, u32[]{:S(2)}) collective-permute-start(f32[128,512]{1,0:T(8,128)S(1)} %get-tuple-element.23), channel_id=1, source_target_pairs={{0,4},{1,6},{2,0},{3,2},{4,5},{5,7},{6,1},{7,3},{8,12},{9,14},{10,... | collective-permute-start | bytes 786440 | tf_op jit(solution)/shard_map/ppermute | solution.py:437
  44.1 10.5 %copy-start.4 = (f32[256,128]{1,0:T(8,128)S(1)}, f32[256,128]{1,0:T(8,128)}, u32[]{:S(2)}) copy-start(f32[256,128]{1,0:T(8,128)} %refs_7_.1) | copy-start | bytes 393220

commit v5 on v4

--- a/solution.py
+++ b/solution.py
@@ -236,25 +236,23 @@
     )(places, *operands)
 
 
-def join_kernel(place_ref, b_own, a_own, b_other, a_other, out):
-    rows = b_own.shape[0]
+def join_kernel(place_ref, own, other, out):
+    both = own.shape[0]
     core = place_ref[1]
-    for k, piece in enumerate((b_own, a_own)):
-        out[pl.ds(pl.multiple_of((2 * core + k) * rows, 8), rows), :] = piece[...]
-    for k, piece in enumerate((b_other, a_other)):
-        out[pl.ds(pl.multiple_of((2 - 2 * core + k) * rows, 8), rows), :] = piece[...]
-
-
-def join(places, *pieces):
-    rows, size = pieces[0].shape
+    out[pl.ds(pl.multiple_of(core * both, 8), both), :] = own[...]
+    out[pl.ds(pl.multiple_of((1 - core) * both, 8), both), :] = other[...]
+
+
+def join(places, own, other):
+    both, size = own.shape
     return pl.pallas_call(
         join_kernel,
-        out_shape=jax.ShapeDtypeStruct((4 * rows, size), jnp.float32),
-        in_specs=[SMEM] + [VMEM] * 4,
+        out_shape=jax.ShapeDtypeStruct((2 * both, size), jnp.float32),
+        in_specs=[SMEM] + [VMEM] * 2,
         out_specs=VMEM,
-        compiler_params=memory(8 * pieces[0].size),
+        compiler_params=memory(4 * own.size),
         name="join",
-    )(places, *pieces)
+    )(places, own, other)
 
 
 def route_kernel(count, chips, place_ref, _, own, last, last_swapped, *refs):
@@ -450,8 +448,9 @@
     extra, more = range(count // 2 - 1), range(chips // 2 - 1)
     b_ops = [to_rows(b_diag, j) for j in extra]
     square = exchange(b_diag, lambda r, z, c: None if c else (r ^ (count - 1), z, c))
-    b_other, a_other = swap(b_panel), swap(a_panel)
-    panel = join(places, b_panel, a_panel, b_other, a_other)
+    own = jnp.concatenate([b_panel, a_panel], axis=0)
+    other = swap(own)
+    panel = join(places, own, other)
     p_ops = [to_rows(panel, j) for j in extra]
     final = exchange(panel, lambda r, z, c: (r, z ^ (chips - 1), c) if c else (r ^ (count - 1), z, c))
     z_ops = [to_chips(panel, j) for j in more]

time: 59.6 us -> 58.5 us (0.982)
  waiting for transfers between devices: 9.6 us -> 7.58 us
  starting transfers between devices: 21.5 us -> 23.2 us
  local copies, waits for them, and re-layouts: 1.77 us -> 0.95 us
    ppermute x17 -> x16, waiting for transfers between devices: 9.6 us -> 7.58 us  [exchange(): return lax.ppermute(array, ('row', 'chip', 'core'), pairs)]
    ppermute x17 -> x16, starting transfers between devices: 21.5 us -> 23.2 us  [exchange(): return lax.ppermute(array, ('row', 'chip', 'core'), pairs)]
    unnamed x10 -> x9, local copies, waits for them, and re-layouts: 1.69 us -> 0.86 us
  transfers between devices with their start and end apart: 17 -> 16, of which waited for: 6 -> 4; matrix products, arithmetic and copies ran while one was open for 0% -> 2% of each run, Pallas kernels for 35% -> 36%
where the time goes in v5:
time: 58.5 us; the launch traced here: 58.3 us
  Pallas kernels  25.8 us (44%)
  starting transfers between devices  23.2 us (40%)
  waiting for transfers between devices  7.58 us (13%)
  local copies, waits for them, and re-layouts  0.95 us (2%)
  between operations  0.74 us (1%)
    ppermute x16, starting transfers between devices, exchange(): return lax.ppermute(array, ('row', 'chip', 'core'), pairs)  23.2 us
    pallas_call x3, Pallas kernels, factor_part(): pl.pallas_call(functools.partial(step_kernel, count, first, last, total),...  19.7 us
    ppermute x16, waiting for transfers between devices, exchange(): return lax.ppermute(array, ('row', 'chip', 'core'), pairs)  7.58 us
    pallas_call x1, Pallas kernels, update(): pl.pallas_call(functools.partial(update_kernel, count, chips, len(inverse...  4.83 us
  transfers between devices with their start and end apart: 16, of which 4 were waited for; matrix products, arithmetic and copies ran while one was open for 2% of the time, Pallas kernels for 36%

profile of v5, /device:TPU:1, one launch (start us, length us, event | category | flops | bytes accessed | tf_op | source)
XLA Modules:
  0.0 58.3 jit_solution(14011851623255379263)
XLA Ops:
  0.6 0.0 copy-start.3
  0.6 0.8 %collective-permute-start = (f32[128,512]{1,0:T(8,128)}, f32[128,512]{1,0:T(8,128)S(1)}, u32[]{:S(2)}, u32[]{:S(2)}) collective-permute-start(f32[128,512]{1,0:T(8,128)} %refs_0_.1), channel_id=1, source_target_pairs={{0,24},{2,26},{4,28},{6,30},{8,16},{10,18},{12,20},{14,22},{16,8},... | collective-permute-start | bytes 786440 | tf_op jit(solution)/shard_map/ppermute | solution.py:435
  1.5 2.1 %collective-permute-start.2 = (f32[128,512]{1,0:T(8,128)}, f32[128,512]{1,0:T(8,128)S(1)}, u32[]{:S(2)}, u32[]{:S(2)}) collective-permute-start(f32[128,512]{1,0:T(8,128)} %refs_0_.1), channel_id=1, source_target_pairs={{0,8},{1,17},{2,10},{3,19},{4,12},{5,21},{6,14},{7,23},{8,0},{9,25... | collective-permute-start | bytes 786440 | tf_op jit(solution)/shard_map/ppermute | solution.py:435
  3.6 0.1 collective-permute-start.10
  3.7 0.8 %constant_dynamic-update-slice_fusion.1 = f32[64,512]{1,0:T(8,128)S(1)} fusion(f32[32,512]{1,0:T(8,128)} %param.7), kind=kLoop, calls=%fused_computation.1 | loop fusion | bytes 131072
  4.5 0.0 copy-done.3
  4.5 5.1 %collective-permute-start.4 = (f32[64,512]{1,0:T(8,128)S(1)}, f32[64,512]{1,0:T(8,128)S(1)}, u32[]{:S(2)}, u32[]{:S(2)}) collective-permute-start(f32[64,512]{1,0:T(8,128)S(1)} %constant_dynamic-update-slice_fusion.own), channel_id=1, source_target_pairs={{0,1},{1,0},{2,3},{3,2},{4,5},{5,4},{6,7},{7,6},{8,9},{9,8},{10,11... | collective-permute-start | bytes 393224 | tf_op jit(solution)/shard_map/ppermute | solution.py:435
  9.6 0.1 stack.23.place_ref
  9.7 0.0 copy-start.1
  9.7 0.0 copy-start
  9.7 0.9 %collective-permute-done.4.other = f32[64,512]{1,0:T(8,128)S(1)} collective-permute-done((f32[64,512]{1,0:T(8,128)S(1)}, f32[64,512]{1,0:T(8,128)S(1)}, u32[]{:S(2)}, u32[]{:S(2)}) %collective-permute-start.4) | collective-permute-done | bytes 131104 | tf_op jit(solution)/shard_map/ppermute | solution.py:435
  10.6 0.6 join.1.own.refs_4_
  11.2 2.4 %collective-permute-start.12 = (f32[128,512]{1,0:T(8,128)S(1)}, f32[128,512]{1,0:T(8,128)S(1)}, u32[]{:S(2)}, u32[]{:S(2)}) collective-permute-start(f32[128,512]{1,0:T(8,128)S(1)} %join.1.own.refs_4_), channel_id=1, source_target_pairs={{0,2},{1,5},{2,0},{3,7},{4,6},{5,1},{6,4},{7,3},{8,10},{9,13},{10,... | collective-permute-start | bytes 786440 | tf_op jit(solution)/shard_map/ppermute | solution.py:435
  13.6 0.2 collective-permute-start.7
  13.8 0.0 collective-permute-done.refs_1_
  13.8 1.1 %collective-permute-start.5 = (f32[128,512]{1,0:T(8,128)S(1)}, f32[128,512]{1,0:T(8,128)S(1)}, u32[]{:S(2)}, u32[]{:S(2)}) collective-permute-start(f32[128,512]{1,0:T(8,128)S(1)} %join.1.own.refs_4_), channel_id=1, source_target_pairs={{0,24},{1,7},{2,26},{3,5},{4,28},{5,3},{6,30},{7,1},{8,16},{9,15},... | collective-permute-start | bytes 786440 | tf_op jit(solution)/shard_map/ppermute | solution.py:435
  14.9 0.0 collective-permute-done.2.refs_3_
  14.9 0.3 collective-permute-start.1
  15.2 0.0 collective-permute-done.10.refs_8_
  15.2 2.2 %collective-permute-start.3 = (f32[128,512]{1,0:T(8,128)S(1)}, f32[128,512]{1,0:T(8,128)S(1)}, u32[]{:S(2)}, u32[]{:S(2)}) collective-permute-start(f32[128,512]{1,0:T(8,128)S(1)} %collective-permute-done.2.refs_3_), channel_id=1, source_target_pairs={{0,1},{1,0},{2,3},{3,2},{4,5},{5,4},{6,7},{7,6},{8,9},{9,8},{10,11... | collective-permute-start | bytes 786440 | tf_op jit(solution)/shard_map/ppermute | solution.py:435
  17.4 3.1 %collective-permute-done.12.refs_10_ = f32[128,512]{1,0:T(8,128)S(1)} collective-permute-done((f32[128,512]{1,0:T(8,128)S(1)}, f32[128,512]{1,0:T(8,128)S(1)}, u32[]{:S(2)}, u32[]{:S(2)}) %collective-permute-start.12) | collective-permute-done | bytes 262176 | tf_op jit(solution)/shard_map/ppermute | solution.py:435
  20.5 0.0 copy-done.1
  20.5 0.0 collective-permute-start.9
  20.5 0.0 collective-permute-done.7.refs_0_
  20.5 0.3 collective-permute-start.11
  20.8 3.2 %collective-permute-done.5.last.refs_5_ = f32[128,512]{1,0:T(8,128)S(1)} collective-permute-done((f32[128,512]{1,0:T(8,128)S(1)}, f32[128,512]{1,0:T(8,128)S(1)}, u32[]{:S(2)}, u32[]{:S(2)}) %collective-permute-start.5) | collective-permute-done | bytes 262176 | tf_op jit(solution)/shard_map/ppermute | solution.py:435
  24.0 0.0 collective-permute-start.13
  24.0 0.0 collective-permute-done.1.refs_2_
  24.0 0.5 collective-permute-start.8
  24.6 0.0 collective-permute-done.3.refs_4_
  24.6 0.1 collective-permute-start.6
  24.6 0.0 copy-done
  24.6 4.3 %shard_map.84 = (f32[128,128]{1,0:T(8,128)S(1)}, f32[384,512]{1,0:T(8,128)S(1)}, f32[8,128]{1,0:T(8,128)S(1)}) custom-call(s32[5]{0:T(128)S(1)} %stack.23.place_ref, f32[128,512]{1,0:T(8,128)S(1)} %copy-done, f32[128,512]{1,0:T(8,128)S(1)} %collective-permute-done.refs_1_, f32[128,512]{1,0:T(8,128)S(1)} %collective-permute-done.1.refs_2_, ...), custom_call_target="tpu_custom_call" | custom-call | flops 10000000000 | bytes 2097152 | tf_op jit(solution)/shard_map/pallas_call | solution.py:224
  28.9 5.3 %shard_map.85 = (f32[128,128]{1,0:T(8,128)S(1)}, f32[256,384]{1,0:T(8,128)S(1)}, f32[8,128]{1,0:T(8,128)S(1)}, f32[384,128]{1,0:T(8,128)S(1)}) custom-call(s32[5]{0:T(128)S(1)} %stack.23.place_ref, f32[8,128]{1,0:T(8,128)S(1)} %get-tuple-element.15.refs_0_, f32[128,128]{1,0:T(8,128)S(1)} %get-tuple-element.14.refs_1_.refs_0_, ...), custom_call_target="tpu_custom_call" | custom-call | flops 10000000000 | bytes 2097152 | tf_op jit(solution)/shard_map/pallas_call | solution.py:224
  34.2 0.0 collective-permute-done.8.refs_1_
  34.2 0.0 collective-permute-done.6.last_swapped.refs_6_
  34.2 0.7 %route.1 = (f32[128,512]{1,0:T(8,128)S(1)}, f32[128,512]{1,0:T(8,128)S(1)}, f32[8,128]{1,0:T(8,128)S(1)}) custom-call(s32[5]{0:T(128)S(1)} %stack.23.place_ref, f32[8,128]{1,0:T(8,128)S(1)} %get-tuple-element.17._, f32[128,512]{1,0:T(8,128)S(1)} %join.1.own.refs_4_, f32[128,512]{1,0:T(8,128)S(1)} %collective-permute-done.5.last.refs_5_, ...), custom_call_target="tpu_custom_call" | custom-call | tf_op jit(solution)/shard_map/route/pallas_call | solution.py:284
  34.9 4.8 %collective-permute-start.14 = (f32[128,512]{1,0:T(8,128)S(1)}, f32[128,512]{1,0:T(8,128)S(1)}, u32[]{:S(2)}, u32[]{:S(2)}) collective-permute-start(f32[128,512]{1,0:T(8,128)S(1)} %get-tuple-element.22), channel_id=1, source_target_pairs={{0,0},{1,2},{2,4},{3,6},{4,1},{5,3},{6,5},{7,7},{8,8},{9,10},{10,1... | collective-permute-start | bytes 786440 | tf_op jit(solution)/shard_map/ppermute | solution.py:435
  39.7 3.3 %collective-permute-start.15 = (f32[128,512]{1,0:T(8,128)S(1)}, f32[128,512]{1,0:T(8,128)S(1)}, u32[]{:S(2)}, u32[]{:S(2)}) collective-permute-start(f32[128,512]{1,0:T(8,128)S(1)} %get-tuple-element.23), channel_id=1, source_target_pairs={{0,4},{1,6},{2,0},{3,2},{4,5},{5,7},{6,1},{7,3},{8,12},{9,14},{10,... | collective-permute-start | bytes 786440 | tf_op jit(solution)/shard_map/ppermute | solution.py:435
  43.0 0.0 copy-start.2
  43.0 10.1 %shard_map.86.refs_1_ = f32[384,512]{1,0:T(8,128)S(1)} custom-call(s32[5]{0:T(128)S(1)} %stack.23.place_ref, f32[8,128]{1,0:T(8,128)S(1)} %get-tuple-element.18.refs_0_, f32[128,128]{1,0:T(8,128)S(1)} %get-tuple-element.19.refs_1_, f32[256,384]{1,0:T(8,128)S(1)} %get-tuple-element.20.refs_2_, f32[384,128]{1,0:T(8,128)S(1)} %get-tuple-element.21.refs_3_), custom_call_target="tpu_custom_call" | custom-call | flops 10000000000 | bytes 1179648 | tf_op jit(solution)/shard_map/pallas_call | solution.py:224
  53.1 0.0 collective-permute-done.9.refs_3_
  53.1 0.0 collective-permute-done.11.refs_9_
  53.1 0.0 collective-permute-done.13.refs_11_
  53.2 0.3 collective-permute-done.14.refs_12_
  53.4 0.0 collective-permute-done.15.refs_13_
  53.4 0.0 copy-done.2
  53.5 4.8 %update.1 = (f32[128,512]{1,0:T(8,128)}, f32[32,512]{1,0:T(8,128)}, f32[32,512]{1,0:T(8,128)}, f32[256,128]{1,0:T(8,128)}) custom-call(s32[5]{0:T(128)S(1)} %stack.23.place_ref, f32[128,128]{1,0:T(8,128)S(1)} %get-tuple-element.14.refs_1_.refs_0_, f32[384,512]{1,0:T(8,128)S(1)} %shard_map.86.refs_1_, f32[128,512]{1,0:T(8,128)S(1)} %copy-done.1, ...), custom_call_target="tpu_custom_call" | custom-call | flops 10000000000 | bytes 2097152 | tf_op jit(solution)/shard_map/update/pallas_call | solution.py:401
  (1 shorter events, 0.0 us)
Async XLA Ops:
  0.6 3.9 %copy-start.3 = (f32[32,512]{1,0:T(8,128)S(1)}, f32[32,512]{1,0:T(8,128)}, u32[]{:S(2)}) copy-start(f32[32,512]{1,0:T(8,128)} %param.8) | copy-start | bytes 196612
  0.6 13.2 %collective-permute-start = (f32[128,512]{1,0:T(8,128)}, f32[128,512]{1,0:T(8,128)S(1)}, u32[]{:S(2)}, u32[]{:S(2)}) collective-permute-start(f32[128,512]{1,0:T(8,128)} %refs_0_.1), channel_id=1, source_target_pairs={{0,24},{2,26},{4,28},{6,30},{8,16},{10,18},{12,20},{14,22},{16,8},... | collective-permute-start | bytes 786440 | tf_op jit(solution)/shard_map/ppermute | solution.py:435
  1.5 13.4 %collective-permute-start.2 = (f32[128,512]{1,0:T(8,128)}, f32[128,512]{1,0:T(8,128)S(1)}, u32[]{:S(2)}, u32[]{:S(2)}) collective-permute-start(f32[128,512]{1,0:T(8,128)} %refs_0_.1), channel_id=1, source_target_pairs={{0,8},{1,17},{2,10},{3,19},{4,12},{5,21},{6,14},{7,23},{8,0},{9,25... | collective-permute-start | bytes 786440 | tf_op jit(solution)/shard_map/ppermute | solution.py:435
  3.6 11.6 %collective-permute-start.10 = (f32[128,512]{1,0:T(8,128)}, f32[128,512]{1,0:T(8,128)S(1)}, u32[]{:S(2)}, u32[]{:S(2)}) collective-permute-start(f32[128,512]{1,0:T(8,128)} %refs_2_.1), channel_id=1, source_target_pairs={{0,8},{1,17},{2,10},{3,19},{4,12},{5,21},{6,14},{7,23},{8,0},{9,25... | collective-permute-start | bytes 786440 | tf_op jit(solution)/shard_map/ppermute | solution.py:435
  4.5 6.1 %collective-permute-start.4 = (f32[64,512]{1,0:T(8,128)S(1)}, f32[64,512]{1,0:T(8,128)S(1)}, u32[]{:S(2)}, u32[]{:S(2)}) collective-permute-start(f32[64,512]{1,0:T(8,128)S(1)} %constant_dynamic-update-slice_fusion.own), channel_id=1, source_target_pairs={{0,1},{1,0},{2,3},{3,2},{4,5},{5,4},{6,7},{7,6},{8,9},{9,8},{10,11... | collective-permute-start | bytes 393224 | tf_op jit(solution)/shard_map/ppermute | solution.py:435
  9.7 10.8 %copy-start.1 = (f32[128,512]{1,0:T(8,128)S(1)}, f32[128,512]{1,0:T(8,128)}, u32[]{:S(2)}) copy-start(f32[128,512]{1,0:T(8,128)} %refs_2_.1) | copy-start | bytes 786436
  9.7 14.9 %copy-start = (f32[128,512]{1,0:T(8,128)S(1)}, f32[128,512]{1,0:T(8,128)}, u32[]{:S(2)}) copy-start(f32[128,512]{1,0:T(8,128)} %refs_0_.1) | copy-start | bytes 786436
  11.2 9.3 %collective-permute-start.12 = (f32[128,512]{1,0:T(8,128)S(1)}, f32[128,512]{1,0:T(8,128)S(1)}, u32[]{:S(2)}, u32[]{:S(2)}) collective-permute-start(f32[128,512]{1,0:T(8,128)S(1)} %join.1.own.refs_4_), channel_id=1, source_target_pairs={{0,2},{1,5},{2,0},{3,7},{4,6},{5,1},{6,4},{7,3},{8,10},{9,13},{10,... | collective-permute-start | bytes 786440 | tf_op jit(solution)/shard_map/ppermute | solution.py:435
  13.6 6.9 %collective-permute-start.7 = (f32[128,512]{1,0:T(8,128)S(1)}, f32[128,512]{1,0:T(8,128)S(1)}, u32[]{:S(2)}, u32[]{:S(2)}) collective-permute-start(f32[128,512]{1,0:T(8,128)S(1)} %join.1.own.refs_4_), channel_id=1, source_target_pairs={{0,8},{1,17},{2,10},{3,19},{4,12},{5,21},{6,14},{7,23},{8,0},{9,25... | collective-permute-start | bytes 786440 | tf_op jit(solution)/shard_map/ppermute | solution.py:435
  13.8 10.2 %collective-permute-start.5 = (f32[128,512]{1,0:T(8,128)S(1)}, f32[128,512]{1,0:T(8,128)S(1)}, u32[]{:S(2)}, u32[]{:S(2)}) collective-permute-start(f32[128,512]{1,0:T(8,128)S(1)} %join.1.own.refs_4_), channel_id=1, source_target_pairs={{0,24},{1,7},{2,26},{3,5},{4,28},{5,3},{6,30},{7,1},{8,16},{9,15},... | collective-permute-start | bytes 786440 | tf_op jit(solution)/shard_map/ppermute | solution.py:435
  14.9 9.1 %collective-permute-start.1 = (f32[128,512]{1,0:T(8,128)S(1)}, f32[128,512]{1,0:T(8,128)S(1)}, u32[]{:S(2)}, u32[]{:S(2)}) collective-permute-start(f32[128,512]{1,0:T(8,128)S(1)} %collective-permute-done.refs_1_), channel_id=1, source_target_pairs={{0,1},{1,0},{2,3},{3,2},{4,5},{5,4},{6,7},{7,6},{8,9},{9,8},{10,11... | collective-permute-start | bytes 786440 | tf_op jit(solution)/shard_map/ppermute | solution.py:435
  15.2 9.4 %collective-permute-start.3 = (f32[128,512]{1,0:T(8,128)S(1)}, f32[128,512]{1,0:T(8,128)S(1)}, u32[]{:S(2)}, u32[]{:S(2)}) collective-permute-start(f32[128,512]{1,0:T(8,128)S(1)} %collective-permute-done.2.refs_3_), channel_id=1, source_target_pairs={{0,1},{1,0},{2,3},{3,2},{4,5},{5,4},{6,7},{7,6},{8,9},{9,8},{10,11... | collective-permute-start | bytes 786440 | tf_op jit(solution)/shard_map/ppermute | solution.py:435
  20.5 32.6 %collective-permute-start.9 = (f32[128,512]{1,0:T(8,128)S(1)}, f32[128,512]{1,0:T(8,128)S(1)}, u32[]{:S(2)}, u32[]{:S(2)}) collective-permute-start(f32[128,512]{1,0:T(8,128)S(1)} %copy-done.1), channel_id=1, source_target_pairs={{0,24},{1,25},{2,26},{3,27},{4,28},{5,29},{6,30},{7,31},{8,16},{9,... | collective-permute-start | bytes 786440 | tf_op jit(solution)/shard_map/ppermute | solution.py:435
  20.5 32.6 %collective-permute-start.11 = (f32[128,512]{1,0:T(8,128)S(1)}, f32[128,512]{1,0:T(8,128)S(1)}, u32[]{:S(2)}, u32[]{:S(2)}) collective-permute-start(f32[128,512]{1,0:T(8,128)S(1)} %collective-permute-done.10.refs_8_), channel_id=1, source_target_pairs={{0,1},{1,0},{2,3},{3,2},{4,5},{5,4},{6,7},{7,6},{8,9},{9,8},{10,11... | collective-permute-start | bytes 786440 | tf_op jit(solution)/shard_map/ppermute | solution.py:435
  24.0 29.1 %collective-permute-start.13 = (f32[128,512]{1,0:T(8,128)S(1)}, f32[128,512]{1,0:T(8,128)S(1)}, u32[]{:S(2)}, u32[]{:S(2)}) collective-permute-start(f32[128,512]{1,0:T(8,128)S(1)} %collective-permute-done.12.refs_10_), channel_id=1, source_target_pairs={{0,1},{1,0},{2,3},{3,2},{4,5},{5,4},{6,7},{7,6},{8,9},{9,8},{10,11... | collective-permute-start | bytes 786440 | tf_op jit(solution)/shard_map/ppermute | solution.py:435
  24.0 10.2 %collective-permute-start.8 = (f32[128,512]{1,0:T(8,128)S(1)}, f32[128,512]{1,0:T(8,128)S(1)}, u32[]{:S(2)}, u32[]{:S(2)}) collective-permute-start(f32[128,512]{1,0:T(8,128)S(1)} %collective-permute-done.7.refs_0_), channel_id=1, source_target_pairs={{0,1},{1,0},{2,3},{3,2},{4,5},{5,4},{6,7},{7,6},{8,9},{9,8},{10,11... | collective-permute-start | bytes 786440 | tf_op jit(solution)/shard_map/ppermute | solution.py:435
  24.6 9.7 %collective-permute-start.6 = (f32[128,512]{1,0:T(8,128)S(1)}, f32[128,512]{1,0:T(8,128)S(1)}, u32[]{:S(2)}, u32[]{:S(2)}) collective-permute-start(f32[128,512]{1,0:T(8,128)S(1)} %collective-permute-done.5.last.refs_5_), channel_id=1, source_target_pairs={{0,1},{1,0},{2,3},{3,2},{4,5},{5,4},{6,7},{7,6},{8,9},{9,8},{10,11... | collective-permute-start | bytes 786440 | tf_op jit(solution)/shard_map/ppermute | solution.py:435
  34.9 18.5 %collective-permute-start.14 = (f32[128,512]{1,0:T(8,128)S(1)}, f32[128,512]{1,0:T(8,128)S(1)}, u32[]{:S(2)}, u32[]{:S(2)}) collective-permute-start(f32[128,512]{1,0:T(8,128)S(1)} %get-tuple-element.22), channel_id=1, source_target_pairs={{0,0},{1,2},{2,4},{3,6},{4,1},{5,3},{6,5},{7,7},{8,8},{9,10},{10,1... | collective-permute-start | bytes 786440 | tf_op jit(solution)/shard_map/ppermute | solution.py:435
  39.7 13.8 %collective-permute-start.15 = (f32[128,512]{1,0:T(8,128)S(1)}, f32[128,512]{1,0:T(8,128)S(1)}, u32[]{:S(2)}, u32[]{:S(2)}) collective-permute-start(f32[128,512]{1,0:T(8,128)S(1)} %get-tuple-element.23), channel_id=1, source_target_pairs={{0,4},{1,6},{2,0},{3,2},{4,5},{5,7},{6,1},{7,3},{8,12},{9,14},{10,... | collective-permute-start | bytes 786440 | tf_op jit(solution)/shard_map/ppermute | solution.py:435
  43.0 10.5 %copy-start.2 = (f32[256,128]{1,0:T(8,128)S(1)}, f32[256,128]{1,0:T(8,128)}, u32[]{:S(2)}) copy-start(f32[256,128]{1,0:T(8,128)} %refs_7_.1) | copy-start | bytes 393220

commit v6 on v5

--- a/solution.py
+++ b/solution.py
@@ -81,7 +81,8 @@
     return jnp.concatenate([rows[h] * lax.rsqrt(pivots[h]) for h in range(groups)], axis=0)
 
 
-def invert_block(block, columns, others=()):
+def invert_block(block, columns, others=(), following=None):
+    square = None
     size = block.shape[0]
     done = []
     total = None
@@ -92,8 +93,17 @@
         if 0 < b <= len(others):
             nothing = jnp.minimum(jnp.abs(others[b - 1]()), 0.0)
             mine = mine + jnp.concatenate([nothing] * (SMALL // 8), axis=0)
+        last = below == size
+        ahead = None
+        if last and following is not None:
+            ahead, square = following()
+            near = nt(ahead, jnp.concatenate(done, axis=0))
+            square = square - nt(near, near)
+            ahead = ahead - nt(ahead, total)
         small = invert_small(mine, offset, columns)
-        last = below == size
+        if ahead is not None:
+            near = nt(ahead, small)
+            square = square - nt(near, near)
         if not last:
             low = nt(block[below:, :], small)
             full = jnp.concatenate([jnp.zeros((below, SMALL), jnp.float32), low], axis=0)
@@ -103,7 +113,7 @@
         if not last:
             update = nn(full, strip)
             total = update if total is None else total + update
-    return jnp.concatenate(done, axis=0)
+    return jnp.concatenate(done, axis=0), square
 
 
 def factor_steps(work, sums, columns, out_ref, base, pending, first, last, total):
@@ -125,7 +135,8 @@
         others = []
         if k > 0:
             near = nt(work[at(k), at(p)], pending)
-            block = block - nt(near, near)
+            if k == first:
+                block = block - nt(near, near)
             held = {}
 
             def lower(p=p, k=k, held=held, near=near, pending=pending):
@@ -152,7 +163,15 @@
                 return update[:8, :BLOCK]
 
             others = [lower, trail, total_up]
-        pending = invert_block(block, columns, others)
+        following = None
+        if k + 1 < last:
+
+            def following(k=k):
+                return work[at(k + 1), at(k)], work[at(k + 1), at(k + 1)]
+
+        pending, square = invert_block(block, columns, others, following)
+        if k + 1 < last:
+            work[at(k + 1), at(k + 1)] = square
     if last == total:
         finish(last - 1, pending)
     return pending

time: 58.5 us -> 58.5 us (level)
  transfers between devices with their start and end apart: 16 -> 16, of which waited for: 4 -> 4; matrix products, arithmetic and copies ran while one was open for 2% -> 2% of each run, Pallas kernels for 36% -> 35%
where the time goes in v6:
time: 58.5 us; the launch traced here: 58.3 us
  Pallas kernels  25.5 us (44%)
  starting transfers between devices  23.2 us (40%)
  waiting for transfers between devices  7.88 us (13%)
  local copies, waits for them, and re-layouts  0.95 us (2%)
  between operations  0.74 us (1%)
    ppermute x16, starting transfers between devices, exchange(): return lax.ppermute(array, ('row', 'chip', 'core'), pairs)  23.2 us
    pallas_call x3, Pallas kernels, factor_part(): pl.pallas_call(functools.partial(step_kernel, count, first, last, total),...  19.4 us
    ppermute x16, waiting for transfers between devices, exchange(): return lax.ppermute(array, ('row', 'chip', 'core'), pairs)  7.88 us
    pallas_call x1, Pallas kernels, update(): pl.pallas_call(functools.partial(update_kernel, count, chips, len(inverse...  4.83 us
  transfers between devices with their start and end apart: 16, of which 4 were waited for; matrix products, arithmetic and copies ran while one was open for 2% of the time, Pallas kernels for 35%

profile of v6, /device:TPU:1, one launch (start us, length us, event | category | flops | bytes accessed | tf_op | source)
XLA Modules:
  0.0 58.3 jit_solution(9515544922049952918)
XLA Ops:
  0.6 0.0 copy-start.3
  0.6 0.8 %collective-permute-start = (f32[128,512]{1,0:T(8,128)}, f32[128,512]{1,0:T(8,128)S(1)}, u32[]{:S(2)}, u32[]{:S(2)}) collective-permute-start(f32[128,512]{1,0:T(8,128)} %refs_0_.1), channel_id=1, source_target_pairs={{0,24},{2,26},{4,28},{6,30},{8,16},{10,18},{12,20},{14,22},{16,8},... | collective-permute-start | bytes 786440 | tf_op jit(solution)/shard_map/ppermute | solution.py:454
  1.5 2.1 %collective-permute-start.2 = (f32[128,512]{1,0:T(8,128)}, f32[128,512]{1,0:T(8,128)S(1)}, u32[]{:S(2)}, u32[]{:S(2)}) collective-permute-start(f32[128,512]{1,0:T(8,128)} %refs_0_.1), channel_id=1, source_target_pairs={{0,8},{1,17},{2,10},{3,19},{4,12},{5,21},{6,14},{7,23},{8,0},{9,25... | collective-permute-start | bytes 786440 | tf_op jit(solution)/shard_map/ppermute | solution.py:454
  3.6 0.1 collective-permute-start.10
  3.7 0.8 %constant_dynamic-update-slice_fusion.1 = f32[64,512]{1,0:T(8,128)S(1)} fusion(f32[32,512]{1,0:T(8,128)} %param.7), kind=kLoop, calls=%fused_computation.1 | loop fusion | bytes 131072
  4.5 0.0 copy-done.3
  4.5 5.1 %collective-permute-start.4 = (f32[64,512]{1,0:T(8,128)S(1)}, f32[64,512]{1,0:T(8,128)S(1)}, u32[]{:S(2)}, u32[]{:S(2)}) collective-permute-start(f32[64,512]{1,0:T(8,128)S(1)} %constant_dynamic-update-slice_fusion.own), channel_id=1, source_target_pairs={{0,1},{1,0},{2,3},{3,2},{4,5},{5,4},{6,7},{7,6},{8,9},{9,8},{10,11... | collective-permute-start | bytes 393224 | tf_op jit(solution)/shard_map/ppermute | solution.py:454
  9.6 0.1 stack.23.place_ref
  9.7 0.0 copy-start.1
  9.7 0.0 copy-start
  9.7 0.9 %collective-permute-done.4.other = f32[64,512]{1,0:T(8,128)S(1)} collective-permute-done((f32[64,512]{1,0:T(8,128)S(1)}, f32[64,512]{1,0:T(8,128)S(1)}, u32[]{:S(2)}, u32[]{:S(2)}) %collective-permute-start.4) | collective-permute-done | bytes 131104 | tf_op jit(solution)/shard_map/ppermute | solution.py:454
  10.6 0.6 join.1.own.refs_4_
  11.2 2.4 %collective-permute-start.12 = (f32[128,512]{1,0:T(8,128)S(1)}, f32[128,512]{1,0:T(8,128)S(1)}, u32[]{:S(2)}, u32[]{:S(2)}) collective-permute-start(f32[128,512]{1,0:T(8,128)S(1)} %join.1.own.refs_4_), channel_id=1, source_target_pairs={{0,2},{1,5},{2,0},{3,7},{4,6},{5,1},{6,4},{7,3},{8,10},{9,13},{10,... | collective-permute-start | bytes 786440 | tf_op jit(solution)/shard_map/ppermute | solution.py:454
  13.6 0.2 collective-permute-start.7
  13.8 0.0 collective-permute-done.refs_1_
  13.8 1.1 %collective-permute-start.5 = (f32[128,512]{1,0:T(8,128)S(1)}, f32[128,512]{1,0:T(8,128)S(1)}, u32[]{:S(2)}, u32[]{:S(2)}) collective-permute-start(f32[128,512]{1,0:T(8,128)S(1)} %join.1.own.refs_4_), channel_id=1, source_target_pairs={{0,24},{1,7},{2,26},{3,5},{4,28},{5,3},{6,30},{7,1},{8,16},{9,15},... | collective-permute-start | bytes 786440 | tf_op jit(solution)/shard_map/ppermute | solution.py:454
  14.9 0.0 collective-permute-done.2.refs_3_
  14.9 0.3 collective-permute-start.1
  15.2 0.0 collective-permute-done.10.refs_8_
  15.2 2.2 %collective-permute-start.3 = (f32[128,512]{1,0:T(8,128)S(1)}, f32[128,512]{1,0:T(8,128)S(1)}, u32[]{:S(2)}, u32[]{:S(2)}) collective-permute-start(f32[128,512]{1,0:T(8,128)S(1)} %collective-permute-done.2.refs_3_), channel_id=1, source_target_pairs={{0,1},{1,0},{2,3},{3,2},{4,5},{5,4},{6,7},{7,6},{8,9},{9,8},{10,11... | collective-permute-start | bytes 786440 | tf_op jit(solution)/shard_map/ppermute | solution.py:454
  17.4 3.1 %collective-permute-done.12.refs_10_ = f32[128,512]{1,0:T(8,128)S(1)} collective-permute-done((f32[128,512]{1,0:T(8,128)S(1)}, f32[128,512]{1,0:T(8,128)S(1)}, u32[]{:S(2)}, u32[]{:S(2)}) %collective-permute-start.12) | collective-permute-done | bytes 262176 | tf_op jit(solution)/shard_map/ppermute | solution.py:454
  20.5 0.0 copy-done.1
  20.5 0.0 collective-permute-start.9
  20.5 0.0 collective-permute-done.7.refs_0_
  20.5 0.3 collective-permute-start.11
  20.8 3.2 %collective-permute-done.5.last.refs_5_ = f32[128,512]{1,0:T(8,128)S(1)} collective-permute-done((f32[128,512]{1,0:T(8,128)S(1)}, f32[128,512]{1,0:T(8,128)S(1)}, u32[]{:S(2)}, u32[]{:S(2)}) %collective-permute-start.5) | collective-permute-done | bytes 262176 | tf_op jit(solution)/shard_map/ppermute | solution.py:454
  24.0 0.0 collective-permute-start.13
  24.0 0.0 collective-permute-done.1.refs_2_
  24.0 0.5 collective-permute-start.8
  24.6 0.0 collective-permute-done.3.refs_4_
  24.6 0.1 collective-permute-start.6
  24.6 0.0 copy-done
  24.6 4.3 %shard_map.84 = (f32[128,128]{1,0:T(8,128)S(1)}, f32[384,512]{1,0:T(8,128)S(1)}, f32[8,128]{1,0:T(8,128)S(1)}) custom-call(s32[5]{0:T(128)S(1)} %stack.23.place_ref, f32[128,512]{1,0:T(8,128)S(1)} %copy-done, f32[128,512]{1,0:T(8,128)S(1)} %collective-permute-done.refs_1_, f32[128,512]{1,0:T(8,128)S(1)} %collective-permute-done.1.refs_2_, ...), custom_call_target="tpu_custom_call" | custom-call | flops 10000000000 | bytes 2097152 | tf_op jit(solution)/shard_map/pallas_call | solution.py:243
  28.9 5.3 %shard_map.85 = (f32[128,128]{1,0:T(8,128)S(1)}, f32[256,384]{1,0:T(8,128)S(1)}, f32[8,128]{1,0:T(8,128)S(1)}, f32[384,128]{1,0:T(8,128)S(1)}) custom-call(s32[5]{0:T(128)S(1)} %stack.23.place_ref, f32[8,128]{1,0:T(8,128)S(1)} %get-tuple-element.15.refs_0_, f32[128,128]{1,0:T(8,128)S(1)} %get-tuple-element.14.refs_1_.refs_0_, ...), custom_call_target="tpu_custom_call" | custom-call | flops 10000000000 | bytes 2097152 | tf_op jit(solution)/shard_map/pallas_call | solution.py:243
  34.2 0.0 collective-permute-done.8.refs_1_
  34.2 0.0 collective-permute-done.6.last_swapped.refs_6_
  34.2 0.7 %route.1 = (f32[128,512]{1,0:T(8,128)S(1)}, f32[128,512]{1,0:T(8,128)S(1)}, f32[8,128]{1,0:T(8,128)S(1)}) custom-call(s32[5]{0:T(128)S(1)} %stack.23.place_ref, f32[8,128]{1,0:T(8,128)S(1)} %get-tuple-element.17._, f32[128,512]{1,0:T(8,128)S(1)} %join.1.own.refs_4_, f32[128,512]{1,0:T(8,128)S(1)} %collective-permute-done.5.last.refs_5_, ...), custom_call_target="tpu_custom_call" | custom-call | tf_op jit(solution)/shard_map/route/pallas_call | solution.py:303
  34.9 4.8 %collective-permute-start.14 = (f32[128,512]{1,0:T(8,128)S(1)}, f32[128,512]{1,0:T(8,128)S(1)}, u32[]{:S(2)}, u32[]{:S(2)}) collective-permute-start(f32[128,512]{1,0:T(8,128)S(1)} %get-tuple-element.22), channel_id=1, source_target_pairs={{0,0},{1,2},{2,4},{3,6},{4,1},{5,3},{6,5},{7,7},{8,8},{9,10},{10,1... | collective-permute-start | bytes 786440 | tf_op jit(solution)/shard_map/ppermute | solution.py:454
  39.7 3.3 %collective-permute-start.15 = (f32[128,512]{1,0:T(8,128)S(1)}, f32[128,512]{1,0:T(8,128)S(1)}, u32[]{:S(2)}, u32[]{:S(2)}) collective-permute-start(f32[128,512]{1,0:T(8,128)S(1)} %get-tuple-element.23), channel_id=1, source_target_pairs={{0,4},{1,6},{2,0},{3,2},{4,5},{5,7},{6,1},{7,3},{8,12},{9,14},{10,... | collective-permute-start | bytes 786440 | tf_op jit(solution)/shard_map/ppermute | solution.py:454
  43.0 0.0 copy-start.2
  43.0 9.8 %shard_map.86.refs_1_ = f32[384,512]{1,0:T(8,128)S(1)} custom-call(s32[5]{0:T(128)S(1)} %stack.23.place_ref, f32[8,128]{1,0:T(8,128)S(1)} %get-tuple-element.18.refs_0_, f32[128,128]{1,0:T(8,128)S(1)} %get-tuple-element.19.refs_1_, f32[256,384]{1,0:T(8,128)S(1)} %get-tuple-element.20.refs_2_, f32[384,128]{1,0:T(8,128)S(1)} %get-tuple-element.21.refs_3_), custom_call_target="tpu_custom_call" | custom-call | flops 10000000000 | bytes 1179648 | tf_op jit(solution)/shard_map/pallas_call | solution.py:243
  52.8 0.0 collective-permute-done.9.refs_3_
  52.8 0.0 collective-permute-done.11.refs_9_
  52.8 0.0 collective-permute-done.13.refs_11_
  52.9 0.6 %collective-permute-done.14.refs_12_ = f32[128,512]{1,0:T(8,128)S(1)} collective-permute-done((f32[128,512]{1,0:T(8,128)S(1)}, f32[128,512]{1,0:T(8,128)S(1)}, u32[]{:S(2)}, u32[]{:S(2)}) %collective-permute-start.14) | collective-permute-done | bytes 262176 | tf_op jit(solution)/shard_map/ppermute | solution.py:454
  53.4 0.0 collective-permute-done.15.refs_13_
  53.4 0.0 copy-done.2
  53.5 4.8 %update.1 = (f32[128,512]{1,0:T(8,128)}, f32[32,512]{1,0:T(8,128)}, f32[32,512]{1,0:T(8,128)}, f32[256,128]{1,0:T(8,128)}) custom-call(s32[5]{0:T(128)S(1)} %stack.23.place_ref, f32[128,128]{1,0:T(8,128)S(1)} %get-tuple-element.14.refs_1_.refs_0_, f32[384,512]{1,0:T(8,128)S(1)} %shard_map.86.refs_1_, f32[128,512]{1,0:T(8,128)S(1)} %copy-done.1, ...), custom_call_target="tpu_custom_call" | custom-call | flops 10000000000 | bytes 2097152 | tf_op jit(solution)/shard_map/update/pallas_call | solution.py:420
  (1 shorter events, 0.0 us)
Async XLA Ops:
  0.6 3.9 %copy-start.3 = (f32[32,512]{1,0:T(8,128)S(1)}, f32[32,512]{1,0:T(8,128)}, u32[]{:S(2)}) copy-start(f32[32,512]{1,0:T(8,128)} %param.8) | copy-start | bytes 196612
  0.6 13.2 %collective-permute-start = (f32[128,512]{1,0:T(8,128)}, f32[128,512]{1,0:T(8,128)S(1)}, u32[]{:S(2)}, u32[]{:S(2)}) collective-permute-start(f32[128,512]{1,0:T(8,128)} %refs_0_.1), channel_id=1, source_target_pairs={{0,24},{2,26},{4,28},{6,30},{8,16},{10,18},{12,20},{14,22},{16,8},... | collective-permute-start | bytes 786440 | tf_op jit(solution)/shard_map/ppermute | solution.py:454
  1.5 13.4 %collective-permute-start.2 = (f32[128,512]{1,0:T(8,128)}, f32[128,512]{1,0:T(8,128)S(1)}, u32[]{:S(2)}, u32[]{:S(2)}) collective-permute-start(f32[128,512]{1,0:T(8,128)} %refs_0_.1), channel_id=1, source_target_pairs={{0,8},{1,17},{2,10},{3,19},{4,12},{5,21},{6,14},{7,23},{8,0},{9,25... | collective-permute-start | bytes 786440 | tf_op jit(solution)/shard_map/ppermute | solution.py:454
  3.6 11.6 %collective-permute-start.10 = (f32[128,512]{1,0:T(8,128)}, f32[128,512]{1,0:T(8,128)S(1)}, u32[]{:S(2)}, u32[]{:S(2)}) collective-permute-start(f32[128,512]{1,0:T(8,128)} %refs_2_.1), channel_id=1, source_target_pairs={{0,8},{1,17},{2,10},{3,19},{4,12},{5,21},{6,14},{7,23},{8,0},{9,25... | collective-permute-start | bytes 786440 | tf_op jit(solution)/shard_map/ppermute | solution.py:454
  4.5 6.1 %collective-permute-start.4 = (f32[64,512]{1,0:T(8,128)S(1)}, f32[64,512]{1,0:T(8,128)S(1)}, u32[]{:S(2)}, u32[]{:S(2)}) collective-permute-start(f32[64,512]{1,0:T(8,128)S(1)} %constant_dynamic-update-slice_fusion.own), channel_id=1, source_target_pairs={{0,1},{1,0},{2,3},{3,2},{4,5},{5,4},{6,7},{7,6},{8,9},{9,8},{10,11... | collective-permute-start | bytes 393224 | tf_op jit(solution)/shard_map/ppermute | solution.py:454
  9.7 10.8 %copy-start.1 = (f32[128,512]{1,0:T(8,128)S(1)}, f32[128,512]{1,0:T(8,128)}, u32[]{:S(2)}) copy-start(f32[128,512]{1,0:T(8,128)} %refs_2_.1) | copy-start | bytes 786436
  9.7 14.9 %copy-start = (f32[128,512]{1,0:T(8,128)S(1)}, f32[128,512]{1,0:T(8,128)}, u32[]{:S(2)}) copy-start(f32[128,512]{1,0:T(8,128)} %refs_0_.1) | copy-start | bytes 786436
  11.2 9.3 %collective-permute-start.12 = (f32[128,512]{1,0:T(8,128)S(1)}, f32[128,512]{1,0:T(8,128)S(1)}, u32[]{:S(2)}, u32[]{:S(2)}) collective-permute-start(f32[128,512]{1,0:T(8,128)S(1)} %join.1.own.refs_4_), channel_id=1, source_target_pairs={{0,2},{1,5},{2,0},{3,7},{4,6},{5,1},{6,4},{7,3},{8,10},{9,13},{10,... | collective-permute-start | bytes 786440 | tf_op jit(solution)/shard_map/ppermute | solution.py:454
  13.6 6.9 %collective-permute-start.7 = (f32[128,512]{1,0:T(8,128)S(1)}, f32[128,512]{1,0:T(8,128)S(1)}, u32[]{:S(2)}, u32[]{:S(2)}) collective-permute-start(f32[128,512]{1,0:T(8,128)S(1)} %join.1.own.refs_4_), channel_id=1, source_target_pairs={{0,8},{1,17},{2,10},{3,19},{4,12},{5,21},{6,14},{7,23},{8,0},{9,25... | collective-permute-start | bytes 786440 | tf_op jit(solution)/shard_map/ppermute | solution.py:454
  13.8 10.2 %collective-permute-start.5 = (f32[128,512]{1,0:T(8,128)S(1)}, f32[128,512]{1,0:T(8,128)S(1)}, u32[]{:S(2)}, u32[]{:S(2)}) collective-permute-start(f32[128,512]{1,0:T(8,128)S(1)} %join.1.own.refs_4_), channel_id=1, source_target_pairs={{0,24},{1,7},{2,26},{3,5},{4,28},{5,3},{6,30},{7,1},{8,16},{9,15},... | collective-permute-start | bytes 786440 | tf_op jit(solution)/shard_map/ppermute | solution.py:454
  14.9 9.1 %collective-permute-start.1 = (f32[128,512]{1,0:T(8,128)S(1)}, f32[128,512]{1,0:T(8,128)S(1)}, u32[]{:S(2)}, u32[]{:S(2)}) collective-permute-start(f32[128,512]{1,0:T(8,128)S(1)} %collective-permute-done.refs_1_), channel_id=1, source_target_pairs={{0,1},{1,0},{2,3},{3,2},{4,5},{5,4},{6,7},{7,6},{8,9},{9,8},{10,11... | collective-permute-start | bytes 786440 | tf_op jit(solution)/shard_map/ppermute | solution.py:454
  15.2 9.4 %collective-permute-start.3 = (f32[128,512]{1,0:T(8,128)S(1)}, f32[128,512]{1,0:T(8,128)S(1)}, u32[]{:S(2)}, u32[]{:S(2)}) collective-permute-start(f32[128,512]{1,0:T(8,128)S(1)} %collective-permute-done.2.refs_3_), channel_id=1, source_target_pairs={{0,1},{1,0},{2,3},{3,2},{4,5},{5,4},{6,7},{7,6},{8,9},{9,8},{10,11... | collective-permute-start | bytes 786440 | tf_op jit(solution)/shard_map/ppermute | solution.py:454
  20.5 32.3 %collective-permute-start.9 = (f32[128,512]{1,0:T(8,128)S(1)}, f32[128,512]{1,0:T(8,128)S(1)}, u32[]{:S(2)}, u32[]{:S(2)}) collective-permute-start(f32[128,512]{1,0:T(8,128)S(1)} %copy-done.1), channel_id=1, source_target_pairs={{0,24},{1,25},{2,26},{3,27},{4,28},{5,29},{6,30},{7,31},{8,16},{9,... | collective-permute-start | bytes 786440 | tf_op jit(solution)/shard_map/ppermute | solution.py:454
  20.5 32.3 %collective-permute-start.11 = (f32[128,512]{1,0:T(8,128)S(1)}, f32[128,512]{1,0:T(8,128)S(1)}, u32[]{:S(2)}, u32[]{:S(2)}) collective-permute-start(f32[128,512]{1,0:T(8,128)S(1)} %collective-permute-done.10.refs_8_), channel_id=1, source_target_pairs={{0,1},{1,0},{2,3},{3,2},{4,5},{5,4},{6,7},{7,6},{8,9},{9,8},{10,11... | collective-permute-start | bytes 786440 | tf_op jit(solution)/shard_map/ppermute | solution.py:454
  24.0 28.8 %collective-permute-start.13 = (f32[128,512]{1,0:T(8,128)S(1)}, f32[128,512]{1,0:T(8,128)S(1)}, u32[]{:S(2)}, u32[]{:S(2)}) collective-permute-start(f32[128,512]{1,0:T(8,128)S(1)} %collective-permute-done.12.refs_10_), channel_id=1, source_target_pairs={{0,1},{1,0},{2,3},{3,2},{4,5},{5,4},{6,7},{7,6},{8,9},{9,8},{10,11... | collective-permute-start | bytes 786440 | tf_op jit(solution)/shard_map/ppermute | solution.py:454
  24.0 10.2 %collective-permute-start.8 = (f32[128,512]{1,0:T(8,128)S(1)}, f32[128,512]{1,0:T(8,128)S(1)}, u32[]{:S(2)}, u32[]{:S(2)}) collective-permute-start(f32[128,512]{1,0:T(8,128)S(1)} %collective-permute-done.7.refs_0_), channel_id=1, source_target_pairs={{0,1},{1,0},{2,3},{3,2},{4,5},{5,4},{6,7},{7,6},{8,9},{9,8},{10,11... | collective-permute-start | bytes 786440 | tf_op jit(solution)/shard_map/ppermute | solution.py:454
  24.6 9.7 %collective-permute-start.6 = (f32[128,512]{1,0:T(8,128)S(1)}, f32[128,512]{1,0:T(8,128)S(1)}, u32[]{:S(2)}, u32[]{:S(2)}) collective-permute-start(f32[128,512]{1,0:T(8,128)S(1)} %collective-permute-done.5.last.refs_5_), channel_id=1, source_target_pairs={{0,1},{1,0},{2,3},{3,2},{4,5},{5,4},{6,7},{7,6},{8,9},{9,8},{10,11... | collective-permute-start | bytes 786440 | tf_op jit(solution)/shard_map/ppermute | solution.py:454
  34.9 18.5 %collective-permute-start.14 = (f32[128,512]{1,0:T(8,128)S(1)}, f32[128,512]{1,0:T(8,128)S(1)}, u32[]{:S(2)}, u32[]{:S(2)}) collective-permute-start(f32[128,512]{1,0:T(8,128)S(1)} %get-tuple-element.22), channel_id=1, source_target_pairs={{0,0},{1,2},{2,4},{3,6},{4,1},{5,3},{6,5},{7,7},{8,8},{9,10},{10,1... | collective-permute-start | bytes 786440 | tf_op jit(solution)/shard_map/ppermute | solution.py:454
  39.7 13.8 %collective-permute-start.15 = (f32[128,512]{1,0:T(8,128)S(1)}, f32[128,512]{1,0:T(8,128)S(1)}, u32[]{:S(2)}, u32[]{:S(2)}) collective-permute-start(f32[128,512]{1,0:T(8,128)S(1)} %get-tuple-element.23), channel_id=1, source_target_pairs={{0,4},{1,6},{2,0},{3,2},{4,5},{5,7},{6,1},{7,3},{8,12},{9,14},{10,... | collective-permute-start | bytes 786440 | tf_op jit(solution)/shard_map/ppermute | solution.py:454
  43.0 10.5 %copy-start.2 = (f32[256,128]{1,0:T(8,128)S(1)}, f32[256,128]{1,0:T(8,128)}, u32[]{:S(2)}) copy-start(f32[256,128]{1,0:T(8,128)} %refs_7_.1) | copy-start | bytes 393220
